TPU v7x, 8 devices: a whole 2x2x1 slice. The times are simulated.
8 devices in a mesh: cp: 8 (over z, y, x, core).
Axes of the slice: x: 2, y: 2, z: 1, core: 2. Of those that a mesh axis runs over, the one named last changes fastest.
Arguments:
- queries: bfloat16 [1024, 128, 192], P('cp')
- latent: bfloat16 [1024, 512], P('cp')
- key_rope: bfloat16 [1024, 64], P('cp')
- w_uk: bfloat16 [512, 128, 128], replicated
- w_uv: bfloat16 [512, 128, 128], replicated
- d_out: bfloat16 [1024, 128, 128], P('cp')
Outputs:
- output 1: bfloat16 [1024, 128, 128], P('cp')
- output 2: bfloat16 [1024, 128, 192], P('cp')
- output 3: bfloat16 [1024, 512], P('cp')
- output 4: bfloat16 [1024, 64], P('cp')
- output 5: float32 [512, 128, 128], replicated
- output 6: float32 [512, 128, 128], replicated
All inputs are finite; a program needn't handle non-finite values.
Results may differ from a plain program's by a relative error of at most 0.014118.
Values are sent between devices in bfloat16 or wider.
A program may use at most 1 GiB of HBM per device.

v0:
```python
import functools
import math
import jax
import jax.numpy as jnp
from jax import lax
from jax.experimental import pallas as pl
from jax.experimental.pallas import tpu as pltpu
from jax.sharding import PartitionSpec as P


TB = 128
ND = 8
S = TB * ND
QB = 256
NQ = S // QB
HC = 8
NP = HC // 2
L = 512
D = 128
R = 64
ROWS = 32
NEG = -1e30
BF = jnp.bfloat16
F32 = jnp.float32


def dot(a, b, ca, cb):
    return lax.dot_general(a, b, (((ca,), (cb,)), ((), ())), preferred_element_type=F32)


def pack_kernel(core_ref, qo_ref, do_ref, qp_ref, dp_ref, own_ref, oth_ref, qs, rs, ds):
    for q_ref, g_ref, out in ((qo_ref, do_ref, own_ref), (qp_ref, dp_ref, oth_ref)):
        qs[...] = q_ref[:, :, :D].astype(F32).reshape(TB * HC, D)
        rs[:, :R] = q_ref[:, :, D:].astype(F32).reshape(TB * HC, R)
        ds[...] = g_ref[...].astype(F32).reshape(TB * HC, D)
        for p in range(NP):
            ropes = []
            for k in range(2):
                h = 2 * p + k
                rows = pl.ds(h, TB, stride=HC)
                out[p, k] = qs[rows, :].astype(BF)
                out[p, 2 + k] = ds[rows, :].astype(BF)
                ropes.append(rs[rows, :][:, :R])
            out[p, 4] = jnp.concatenate(ropes, axis=1).astype(BF)


def pack_chunk(j, core, queries, d_out):
    def own(i, c):
        return (0, c[0] * (64 // HC) + j, 0)

    def oth(i, c):
        return (0, (1 - c[0]) * (64 // HC) + j, 0)

    shape = jax.ShapeDtypeStruct((NP, 5, TB, D), BF)
    spec = pl.BlockSpec((NP, 5, TB, D), lambda i, c: (0, 0, 0, 0))
    return pl.pallas_call(
        pack_kernel,
        grid_spec=pltpu.PrefetchScalarGridSpec(
            num_scalar_prefetch=1, grid=(1,),
            in_specs=[pl.BlockSpec((TB, HC, D + R), own), pl.BlockSpec((TB, HC, D), own),
                      pl.BlockSpec((TB, HC, D + R), oth), pl.BlockSpec((TB, HC, D), oth)],
            out_specs=[spec, spec],
            scratch_shapes=[pltpu.VMEM((TB * HC, D), F32)] * 3),
        out_shape=[shape, shape],
        name="pack",
        cost_estimate=pl.CostEstimate(flops=10 ** 9, bytes_accessed=3 * 10 ** 6, transcendentals=0),
    )(core, queries, d_out, queries, d_out)


def prep_kernel(me_ref, *refs):
    ins, (c_ref, ct_ref, r_ref) = refs[:ND], refs[ND:]
    for d in range(ND):
        slot = pl.multiple_of(jnp.bitwise_xor(me_ref[0], d) * TB, TB)
        c = ins[d][:, :L]
        c_ref[pl.ds(slot, TB), :] = c
        ct_ref[:, pl.ds(slot, TB)] = c.astype(F32).T.astype(BF)
        r_ref[pl.ds(slot, TB), :] = ins[d][:, L:]


def prep(me, blocks):
    return pl.pallas_call(
        prep_kernel,
        grid_spec=pltpu.PrefetchScalarGridSpec(
            num_scalar_prefetch=1, grid=(1,),
            in_specs=[pl.BlockSpec((TB, L + D), lambda i, m: (0, 0))] * ND,
            out_specs=[pl.BlockSpec((S, L), lambda i, m: (0, 0)),
                       pl.BlockSpec((L, S), lambda i, m: (0, 0)),
                       pl.BlockSpec((S, D), lambda i, m: (0, 0))]),
        out_shape=[jax.ShapeDtypeStruct((S, L), BF), jax.ShapeDtypeStruct((L, S), BF),
                   jax.ShapeDtypeStruct((S, D), BF)],
        name="prep",
    )(me, *blocks)


def main_kernel(aliased, score_scale, me_ref, *refs):
    n_big = 4 if aliased else 0
    a_refs = refs[:ND]
    c_ref, ct_ref, r_ref, wk_ref, wv_ref, dc_in, dr_in = refs[ND:ND + 7]
    outs = refs[ND + 7 + n_big:]
    (dwk_big, dwv_big, o_big, dq_big, dwk_out, dwv_out, o_par, dq_par, dc_out, dr_out,
     wsc, wk, wv, kr, vs, qa, do, pt, dst, st, dp, dkr, dkb, dvb, osc, dqn, dqr, oacc, dqacc) = outs
    me = me_ref[0]
    core = jnp.bitwise_and(me, 1)
    chip = me // 2
    p = pl.program_id(0)
    own_rows = pl.ds(pl.multiple_of(chip * QB, QB), QB)
    k2 = score_scale * math.log2(math.e)

    @pl.when(p == 0)
    def _():
        for src, dst_w in ((wk_ref, wk), (wv_ref, wv)):
            wsc[...] = src[...].astype(F32).reshape(L * HC, D)
            for h in range(HC):
                dst_w[h // 2, :, (h % 2) * D:(h % 2 + 1) * D] = wsc[pl.ds(h, L, stride=HC), :].astype(BF)
        r = r_ref[...]
        zero = jnp.zeros((S, R), BF)
        kr[0, :, D:] = jnp.concatenate([r[:, :R], zero], axis=1)
        kr[1, :, D:] = jnp.concatenate([zero, r[:, :R]], axis=1)
        for t in range(1, NQ):
            pt[t * QB:(t + 1) * QB, :t * QB] = jnp.zeros((QB, t * QB), BF)
            dst[t * QB:(t + 1) * QB, :t * QB] = jnp.zeros((QB, t * QB), BF)
        dc_out[...] = dc_in[...]
        dr_out[...] = dr_in[...]

    for d in range(ND):
        slot = pl.ds(pl.multiple_of(jnp.bitwise_xor(me, d) * TB, TB), TB)
        for k in range(2):
            qa[k, slot, :D] = a_refs[d][0, k]
            qa[k, slot, D:] = a_refs[d][0, 4]
            do[k, slot, :] = a_refs[d][0, 2 + k]

    for t in range(NQ):
        rows = slice(t * QB, (t + 1) * QB)
        keys = dot(c_ref[rows, :], wk[p], 1, 0).astype(BF)
        vals = dot(c_ref[rows, :], wv[p], 1, 0).astype(BF)
        for k in range(2):
            kr[k, rows, :D] = keys[:, k * D:(k + 1) * D]
            vs[k, rows, :] = vals[:, k * D:(k + 1) * D]

    upper = lax.broadcasted_iota(jnp.int32, (QB, QB), 0) <= lax.broadcasted_iota(jnp.int32, (QB, QB), 1)

    @pl.loop(0, 2)
    def _(k):
        def scores(i):
            q_i = qa[k, i * QB:(i + 1) * QB, :]
            d_i = do[k, i * QB:(i + 1) * QB, :]
            base = QB * (i * (i + 1) // 2)
            for t in range(i + 1):
                rows = slice(t * QB, (t + 1) * QB)
                out = slice(base + t * QB, base + (t + 1) * QB)
                sc = dot(kr[k, rows, :], q_i, 1, 1)
                st[out, :] = jnp.where(upper, sc, NEG) if t == i else sc
                dp[out, :] = dot(vs[k, rows, :], d_i, 1, 1)

        def soften(i):
            n = (i + 1) * QB
            base = QB * (i * (i + 1) // 2)
            mxs = [st[base + 8 * a:base + 8 * a + 8, :] for a in range(4)]
            for r0 in range(32, n, 32):
                for a in range(4):
                    mxs[a] = jnp.maximum(mxs[a], st[base + r0 + 8 * a:base + r0 + 8 * a + 8, :])
            mx = jnp.maximum(jnp.maximum(mxs[0], mxs[1]), jnp.maximum(mxs[2], mxs[3]))
            mx = jnp.max(mx, axis=0, keepdims=True)
            ls = jnp.zeros((8, QB), F32)
            ts = jnp.zeros((8, QB), F32)
            for r0 in range(base, base + n, ROWS):
                e = jnp.exp2((st[r0:r0 + ROWS, :] - mx) * k2)
                st[r0:r0 + ROWS, :] = e
                ls += jnp.sum(e.reshape(ROWS // 8, 8, QB), axis=0)
                ts += jnp.sum((e * dp[r0:r0 + ROWS, :]).reshape(ROWS // 8, 8, QB), axis=0)
            inv = 1.0 / jnp.sum(ls, axis=0, keepdims=True)
            delta = jnp.sum(ts, axis=0, keepdims=True) * inv
            for r0 in range(0, n, ROWS):
                prob = st[base + r0:base + r0 + ROWS, :] * inv
                pt[r0:r0 + ROWS, i * QB:n] = prob.astype(BF)
                dst[r0:r0 + ROWS, i * QB:n] = (prob * (dp[base + r0:base + r0 + ROWS, :] - delta)).astype(BF)

        def grads(t):
            rows = slice(t * QB, (t + 1) * QB)
            grad = dot(dst[rows, t * QB:], qa[k, t * QB:, :], 1, 0)
            dkr[rows, :] = grad[:, D:]
            dkb[k, rows, :] = grad[:, :D].astype(BF)
            dvb[k, rows, :] = dot(pt[rows, t * QB:], do[k, t * QB:, :], 1, 0).astype(BF)

        scores(NQ - 1)
        for i in range(NQ - 1, -1, -1):
            if i:
                scores(i - 1)
            soften(i)
            grads(i)
        dr_out[k] += dkr[own_rows, :] * score_scale

        cols = pl.ds(pl.multiple_of(chip * QB, QB), QB)
        oacc[...] = dot(pt[:, cols], vs[k], 0, 0)
        dqacc[...] = dot(dst[:, cols], kr[k], 0, 0) * score_scale
        head = 2 * p + k
        for side in range(2):
            half = jnp.bitwise_xor(core, side)
            tok = pl.ds(pl.multiple_of(half * TB, TB), TB)
            rows = pl.ds(head, TB, stride=HC)
            osc[side, rows, :] = oacc[tok, :]
            dqn[side, rows, :] = dqacc[tok, :D]
            rope = dqacc[tok, D:]
            dqr[side, rows, :] = jnp.where(k == 0, rope, pltpu.roll(rope, R, 1))

    for w, grad_b, big, out, mul in ((wk, dkb, dwk_big, dwk_out, score_scale), (wv, dvb, dwv_big, dwv_out, None)):
        own = jnp.concatenate([grad_b[0, own_rows, :], grad_b[1, own_rows, :]], axis=1)
        d_lat = dot(own, w[p], 1, 1)
        dc_out[...] += d_lat if mul is None else d_lat * mul
        both = jnp.concatenate([grad_b[0], grad_b[1]], axis=1)
        for t in range(2):
            rows = slice(t * QB, (t + 1) * QB)
            dw = dot(ct_ref[rows, :], both, 1, 0)
            dw = dw if mul is None else dw * mul
            for k in range(2):
                view = pl.ds(t * QB * HC + 2 * p + k, QB, stride=HC)
                big.reshape(L * HC, D)[view, :] = dw[:, k * D:(k + 1) * D]
                out.reshape(L * HC, D)[view, :] = dw[:, k * D:(k + 1) * D]

    @pl.when(p == NP - 1)
    def _():
        o_big[...] = osc[0].reshape(TB, HC, D).astype(BF)
        o_par[...] = osc[1].reshape(TB, HC, D).astype(BF)
        for side, dq in ((0, dq_big), (1, dq_par)):
            dq[:, :, :D] = dqn[side].reshape(TB, HC, D).astype(BF)
            dq[:, :, D:] = dqr[side].reshape(TB, HC, D)[:, :, :R].astype(BF)


def big_shapes():
    return [jax.ShapeDtypeStruct((L, 128, D), F32), jax.ShapeDtypeStruct((L, 128, D), F32),
            jax.ShapeDtypeStruct((TB, 128, D), BF), jax.ShapeDtypeStruct((TB, 128, D + R), BF)]


def main_chunk(j, score_scale, me, blocks, c_abs, c_t, r_abs, w_uk, w_uv, dc, dr, big):
    def head_block(i, m):
        return (0, (m[0] % 2) * (64 // HC) + j, 0)

    def full2(i, m):
        return (0, 0)

    def full3(i, m):
        return (0, 0, 0)

    aliased = big is not None
    once = pl.Buffered(1)
    in_specs = ([pl.BlockSpec((1, 5, TB, D), lambda i, m: (i, 0, 0, 0))] * ND
                + [pl.BlockSpec((S, L), full2, pipeline_mode=once),
                   pl.BlockSpec((L, S), full2, pipeline_mode=once),
                   pl.BlockSpec((S, D), full2, pipeline_mode=once),
                   pl.BlockSpec((L, HC, D), head_block, pipeline_mode=once),
                   pl.BlockSpec((L, HC, D), head_block, pipeline_mode=once),
                   pl.BlockSpec((QB, L), full2, pipeline_mode=once),
                   pl.BlockSpec((2, QB, D), full3, pipeline_mode=once)])
    args = list(blocks) + [c_abs, c_t, r_abs, w_uk, w_uv, dc, dr]
    aliases = {}
    if aliased:
        in_specs += [pl.BlockSpec(memory_space=pl.ANY)] * 4
        aliases = {1 + len(args) + b: b for b in range(4)}
        args += list(big)
    outs = pl.pallas_call(
        functools.partial(main_kernel, aliased, score_scale),
        grid_spec=pltpu.PrefetchScalarGridSpec(
            num_scalar_prefetch=1, grid=(NP,),
            in_specs=in_specs,
            out_specs=[pl.BlockSpec((L, HC, D), head_block, pipeline_mode=once),
                       pl.BlockSpec((L, HC, D), head_block, pipeline_mode=once),
                       pl.BlockSpec((TB, HC, D), head_block, pipeline_mode=once),
                       pl.BlockSpec((TB, HC, D + R), head_block, pipeline_mode=once),
                       pl.BlockSpec((L, HC, D), full3, pipeline_mode=once),
                       pl.BlockSpec((L, HC, D), full3, pipeline_mode=once),
                       pl.BlockSpec((TB, HC, D), full3, pipeline_mode=once),
                       pl.BlockSpec((TB, HC, D + R), full3, pipeline_mode=once),
                       pl.BlockSpec((QB, L), full2, pipeline_mode=once),
                       pl.BlockSpec((2, QB, D), full3, pipeline_mode=once)],
            scratch_shapes=[
                pltpu.VMEM((L * HC, D), F32),
                pltpu.VMEM((NP, L, 2 * D), BF), pltpu.VMEM((NP, L, 2 * D), BF),
                pltpu.VMEM((2, S, 2 * D), BF), pltpu.VMEM((2, S, D), BF),
                pltpu.VMEM((2, S, 2 * D), BF), pltpu.VMEM((2, S, D), BF),
                pltpu.VMEM((S, S), BF), pltpu.VMEM((S, S), BF),
                pltpu.VMEM((QB * NQ * (NQ + 1) // 2, QB), F32), pltpu.VMEM((QB * NQ * (NQ + 1) // 2, QB), F32),
                pltpu.VMEM((S, D), F32),
                pltpu.VMEM((2, S, D), BF), pltpu.VMEM((2, S, D), BF),
                pltpu.VMEM((2, TB * HC, D), F32), pltpu.VMEM((2, TB * HC, D), F32),
                pltpu.VMEM((2, TB * HC, D), F32),
                pltpu.VMEM((QB, D), F32), pltpu.VMEM((QB, 2 * D), F32)]),
        out_shape=big_shapes() + [
            jax.ShapeDtypeStruct((L, HC, D), F32), jax.ShapeDtypeStruct((L, HC, D), F32),
            jax.ShapeDtypeStruct((TB, HC, D), BF), jax.ShapeDtypeStruct((TB, HC, D + R), BF),
            jax.ShapeDtypeStruct((QB, L), F32), jax.ShapeDtypeStruct((2, QB, D), F32)],
        input_output_aliases=aliases,
        compiler_params=pltpu.CompilerParams(vmem_limit_bytes=60 * 2 ** 20),
        name="mla_chunk",
        cost_estimate=pl.CostEstimate(flops=25 * 10 ** 9, bytes_accessed=20 * 10 ** 6, transcendentals=0),
    )(me, *args)
    return outs[:4], outs[4:8], outs[8], outs[9]


def place_kernel(core_ref, *refs):
    ins, outs = refs[:4], refs[8:]
    for a, b in zip(ins, outs):
        b[...] = a[...]


def place(j, core, received, big):
    def at(i, c):
        return (i, (1 - c[0]) * (64 // HC) + j, 0)

    def src(i, c):
        return (i, 0, 0)

    steps = 4
    shapes = [(L // steps, HC, D), (L // steps, HC, D), (TB // steps, HC, D), (TB // steps, HC, D + R)]
    return pl.pallas_call(
        place_kernel,
        grid_spec=pltpu.PrefetchScalarGridSpec(
            num_scalar_prefetch=1, grid=(steps,),
            in_specs=[pl.BlockSpec(s, src) for s in shapes] + [pl.BlockSpec(memory_space=pl.ANY)] * 4,
            out_specs=[pl.BlockSpec(s, at) for s in shapes]),
        out_shape=big_shapes(),
        input_output_aliases={5 + b: b for b in range(4)},
        name="place",
        cost_estimate=pl.CostEstimate(flops=2 * 10 ** 9, bytes_accessed=10 ** 7, transcendentals=0),
    )(core, *received, *big)


def solution(mesh):
    def hop(x, k):
        perm = [(i, i ^ k) for i in range(ND)]
        return lax.ppermute(x, "cp", perm)

    def step(queries, latent, key_rope, w_uk, w_uv, d_out):
        score_scale = 1.0 / math.sqrt(queries.shape[-1])
        dev = lax.axis_index("cp").astype(jnp.int32)
        me = dev[None]
        core = me % 2
        n_chunks = queries.shape[1] // 2 // HC

        lat = jnp.concatenate([latent, key_rope, jnp.zeros((TB, D - R), BF)], axis=1)
        lats = [lat] + [hop(lat, k) for k in range(1, ND)]
        queries, lat1 = lax.optimization_barrier((queries, lats[1]))
        lats[1] = lat1
        c_abs, c_t, r_abs = prep(me, lats)

        recv = []
        for j in range(n_chunks):
            own, oth = pack_chunk(j, core, queries, d_out)
            a1, a2, a5, a3, a4 = [hop(x, k)
                                  for x, k in ((oth, 1), (own, 2), (oth, 5), (oth, 3), (own, 4))]
            a6, a7 = hop(a2, 4), hop(a5, 2)
            recv.append([own, a1, a2, a3, a4, a5, a6, a7])

        dc = jnp.zeros((QB, L), F32)
        dr = jnp.zeros((2, QB, D), F32)
        big = None
        pending = None
        for j in range(n_chunks):
            big, send, dc, dr = main_chunk(j, score_scale, me, recv[j], c_abs, c_t, r_abs,
                                           w_uk, w_uv, dc, dr, big)
            if pending is not None:
                big = place(j - 1, core, pending, big)
            pending = [hop(x, 1) for x in send]
        dc = dc.reshape(2, TB, L)
        dr = dr[0, :, :R] + dr[1, :, R:]
        dr = dr.reshape(2, TB, R)
        c_idx = core[0]

        def swap_sum(x):
            mine = lax.dynamic_index_in_dim(x, c_idx, 0, keepdims=False)
            theirs = lax.dynamic_index_in_dim(x, 1 - c_idx, 0, keepdims=False)
            return (mine + hop(theirs, 1)).astype(BF)

        d_latent = swap_sum(dc)
        d_key_rope = swap_sum(dr)
        d_w_uk, d_w_uv, attn_out, d_query = place(n_chunks - 1, core, pending, big)
        return attn_out, d_query, d_latent, d_key_rope, d_w_uk, d_w_uv

    seq = P("cp")
    return jax.shard_map(step, mesh=mesh,
                         in_specs=(seq, seq, seq, P(), P(), seq),
                         out_specs=(seq, seq, seq, seq, P(), P()),
                         check_vma=False)
```

profile of v0, /device:TPU:0, one launch (start us, length us, event | category | flops | bytes accessed | tf_op | source)
XLA Modules:
  0.0 704.7 jit_solution(16553998508922902482)
XLA Ops:
  4.4 10.1 %copy.73.qo_ref.qp_ref = bf16[128,128,192]{2,1,0:T(8,128)(2,1)} copy(bf16[128,128,192]{1,2,0:T(8,128)(2,1)} %param.6) | data formatting | bytes 12582912 | tf_op jit(solution)/shard_map/optimization_barrier | solution.py:341
  14.5 2.9 pack.15
  29.7 11.3 %collective-permute-done.12.refs_6_ = bf16[128,640]{1,0:T(8,128)(2,1)S(1)} collective-permute-done((bf16[128,640]{1,0:T(8,128)(2,1)S(1)}, bf16[128,640]{1,0:T(8,128)(2,1)S(1)}, u32[]{:S(2)}, u32[]{:S(2)}) %collective-permute-start.12) | collective-permute-done | bytes 163872 | tf_op jit(solution)/shard_map/ppermute | solution.py:330
  52.0 6.4 collective-permute-done.60.refs_5_
  58.7 3.1 pack.13
  61.7 3.3 collective-permute-done.58.refs_3_
  66.7 4.5 collective-permute-done.59.refs_4_
  73.0 6.4 collective-permute-done.50.refs_2_
  80.9 5.6 collective-permute-done.53.refs_5_
  87.6 2.9 pack.12
  94.8 4.5 collective-permute-done.52.refs_4_
  101.1 6.4 collective-permute-done.43.refs_2_
  109.0 5.6 collective-permute-done.46.refs_5_
  116.3 4.9 collective-permute-done.44.refs_3_
  122.7 4.5 collective-permute-done.45.refs_4_
  129.0 6.6 collective-permute-done.36.refs_2_
  137.2 3.2 prep.1
  140.3 3.0 pack.11
  145.0 4.2 collective-permute-done.37.refs_3_
  150.0 5.5 collective-permute-done.61.refs_6_
  157.2 6.5 collective-permute-done.62.refs_7_
  166.9 42.5 %mla_chunk.8 = (f32[512,128,128]{2,1,0:T(8,128)}, f32[512,128,128]{2,1,0:T(8,128)}, bf16[128,128,128]{2,1,0:T(8,128)(2,1)}, bf16[128,128,192]{2,1,0:T(8,128)(2,1...) custom-call(s32[1]{0:T(128)} %bitcast.me_ref, ...), custom_call_target="tpu_custom_call" | custom-call | flops 24999999488 | bytes 20000000 | tf_op jit(solution)/shard_map/mla_chunk/pallas_call | solution.py:260
  211.8 42.8 %mla_chunk.9 = (f32[512,128,128]{2,1,0:T(8,128)}, f32[512,128,128]{2,1,0:T(8,128)}, bf16[128,128,128]{2,1,0:T(8,128)(2,1)}, bf16[128,128,192]{2,1,0:T(8,128)(2,1...) custom-call(s32[1]{0:T(128)} %bitcast.me_ref, ...), custom_call_target="tpu_custom_call", output_to_operand_aliasing={{0}: (16, {}), {1}: (17, {}), {2}: (18, {}), {3}: (19, {})} | custom-call | flops 24999999488 | bytes 20000000 | tf_op jit(solution)/shard_map/mla_chunk/pallas_call | solution.py:260
  257.7 15.3 %collective-permute-done.47.refs_6_ = bf16[4,5,128,128]{3,2,1,0:T(8,128)(2,1)} collective-permute-done((bf16[4,5,128,128]{3,2,1,0:T(8,128)(2,1)}, bf16[4,5,128,128]{3,2,1,0:T(8,128)(2,1)}, u32[]{:S(2)}, u32[]{:S(2)}) %collective-permute-start.47) | collective-permute-done | bytes 655392 | tf_op jit(solution)/shard_map/ppermute | solution.py:330
  278.7 2.9 pack.10
  282.1 3.0 pack.9
  285.1 5.1 place.8
  290.3 3.8 collective-permute-done.48.refs_7_
  299.1 42.7 %mla_chunk.10 = (f32[512,128,128]{2,1,0:T(8,128)}, f32[512,128,128]{2,1,0:T(8,128)}, bf16[128,128,128]{2,1,0:T(8,128)(2,1)}, bf16[128,128,192]{2,1,0:T(8,128)(2,...) custom-call(s32[1]{0:T(128)} %bitcast.me_ref, ...), custom_call_target="tpu_custom_call", output_to_operand_aliasing={{0}: (16, {}), {1}: (17, {}), {2}: (18, {}), {3}: (19, {})} | custom-call | flops 24999999488 | bytes 20000000 | tf_op jit(solution)/shard_map/mla_chunk/pallas_call | solution.py:260
  341.8 5.2 place.9
  351.1 42.8 %mla_chunk.11 = (f32[512,128,128]{2,1,0:T(8,128)}, f32[512,128,128]{2,1,0:T(8,128)}, bf16[128,128,128]{2,1,0:T(8,128)(2,1)}, bf16[128,128,192]{2,1,0:T(8,128)(2,...) custom-call(s32[1]{0:T(128)} %bitcast.me_ref, ...), custom_call_target="tpu_custom_call", output_to_operand_aliasing={{0}: (16, {}), {1}: (17, {}), {2}: (18, {}), {3}: (19, {})} | custom-call | flops 24999999488 | bytes 20000000 | tf_op jit(solution)/shard_map/mla_chunk/pallas_call | solution.py:260
  396.2 15.7 %collective-permute-done.33.refs_6_ = bf16[4,5,128,128]{3,2,1,0:T(8,128)(2,1)S(1)} collective-permute-done((bf16[4,5,128,128]{3,2,1,0:T(8,128)(2,1)S(1)}, bf16[4,5,128,128]{3,2,1,0:T(8,128)(2,1)S(1)}, u32[]{:S(2)}, u32[]{:S(2)}) %collective-permute-start.33) | collective-permute-done | bytes 655392 | tf_op jit(solution)/shard_map/ppermute | solution.py:330
  419.2 3.0 pack.8
  422.2 5.2 place.10
  427.4 6.6 collective-permute-done.34.refs_7_
  437.9 43.0 %mla_chunk.12 = (f32[512,128,128]{2,1,0:T(8,128)}, f32[512,128,128]{2,1,0:T(8,128)}, bf16[128,128,128]{2,1,0:T(8,128)(2,1)}, bf16[128,128,192]{2,1,0:T(8,128)(2,...) custom-call(s32[1]{0:T(128)} %bitcast.me_ref, ...), custom_call_target="tpu_custom_call", output_to_operand_aliasing={{0}: (16, {}), {1}: (17, {}), {2}: (18, {}), {3}: (19, {})} | custom-call | flops 24999999488 | bytes 20000000 | tf_op jit(solution)/shard_map/mla_chunk/pallas_call | solution.py:260
  480.9 5.1 place.11
  490.3 42.7 %mla_chunk.13 = (f32[512,128,128]{2,1,0:T(8,128)}, f32[512,128,128]{2,1,0:T(8,128)}, bf16[128,128,128]{2,1,0:T(8,128)(2,1)}, bf16[128,128,192]{2,1,0:T(8,128)(2,...) custom-call(s32[1]{0:T(128)} %bitcast.me_ref, ...), custom_call_target="tpu_custom_call", output_to_operand_aliasing={{0}: (16, {}), {1}: (17, {}), {2}: (18, {}), {3}: (19, {})} | custom-call | flops 24999999488 | bytes 20000000 | tf_op jit(solution)/shard_map/mla_chunk/pallas_call | solution.py:260
  535.6 16.1 %collective-permute-done.19.refs_6_ = bf16[4,5,128,128]{3,2,1,0:T(8,128)(2,1)} collective-permute-done((bf16[4,5,128,128]{3,2,1,0:T(8,128)(2,1)}, bf16[4,5,128,128]{3,2,1,0:T(8,128)(2,1)}, u32[]{:S(2)}, u32[]{:S(2)}) %collective-permute-start.19) | collective-permute-done | bytes 655392 | tf_op jit(solution)/shard_map/ppermute | solution.py:330
  556.4 5.1 place.12
  561.5 11.0 %collective-permute-done.20.refs_7_ = bf16[4,5,128,128]{3,2,1,0:T(8,128)(2,1)} collective-permute-done((bf16[4,5,128,128]{3,2,1,0:T(8,128)(2,1)}, bf16[4,5,128,128]{3,2,1,0:T(8,128)(2,1)}, u32[]{:S(2)}, u32[]{:S(2)}) %collective-permute-start.20) | collective-permute-done | bytes 655392 | tf_op jit(solution)/shard_map/ppermute | solution.py:330
  576.7 42.6 %mla_chunk.14 = (f32[512,128,128]{2,1,0:T(8,128)}, f32[512,128,128]{2,1,0:T(8,128)}, bf16[128,128,128]{2,1,0:T(8,128)(2,1)}, bf16[128,128,192]{2,1,0:T(8,128)(2,...) custom-call(s32[1]{0:T(128)} %bitcast.me_ref, ...), custom_call_target="tpu_custom_call", output_to_operand_aliasing={{0}: (16, {}), {1}: (17, {}), {2}: (18, {}), {3}: (19, {})} | custom-call | flops 24999999488 | bytes 20000000 | tf_op jit(solution)/shard_map/mla_chunk/pallas_call | solution.py:260
  619.3 5.1 place.13
  625.3 42.7 %mla_chunk.15 = (f32[512,128,128]{2,1,0:T(8,128)}, f32[512,128,128]{2,1,0:T(8,128)}, bf16[128,128,128]{2,1,0:T(8,128)(2,1)}, bf16[128,128,192]{2,1,0:T(8,128)(2,...) custom-call(s32[1]{0:T(128)} %bitcast.me_ref, ...), custom_call_target="tpu_custom_call", output_to_operand_aliasing={{0}: (16, {}), {1}: (17, {}), {2}: (18, {}), {3}: (19, {})} | custom-call | flops 24999999488 | bytes 20000000 | tf_op jit(solution)/shard_map/mla_chunk/pallas_call | solution.py:260
  670.7 4.8 collective-permute-done.96
  683.4 5.1 place.14
  689.3 5.1 place.15
  694.4 10.1 %copy.91 = bf16[128,128,192]{1,2,0:T(8,128)(2,1)} copy(bf16[128,128,192]{2,1,0:T(8,128)(2,1)} %get-tuple-element.273) | data formatting | bytes 12582912
  (296 shorter events, 116.6 us)
Async XLA Ops:
  17.4 33.1 %collective-permute-start.57 = (bf16[4,5,128,128]{3,2,1,0:T(8,128)(2,1)}, bf16[4,5,128,128]{3,2,1,0:T(8,128)(2,1)S(1)}, u32[]{:S(2)}, u32[]{:S(2)}) collective-permute-start(bf16[4,5,128,128]{3,2,1,0:T(8,128)(2,1)} %get-tuple-element.158.refs_0_), channel_id=1, source_target_pairs={{0,2},{1,3},{2,0},{3,1},{4,6},{5,7},{6,4},{7,5}} | collective-permute-start | bytes 1966088 | tf_op jit(solution)/shard_map/ppermute | solution.py:330
  50.5 28.9 %collective-permute-start.50 = (bf16[4,5,128,128]{3,2,1,0:T(8,128)(2,1)}, bf16[4,5,128,128]{3,2,1,0:T(8,128)(2,1)S(1)}, u32[]{:S(2)}, u32[]{:S(2)}) collective-permute-start(bf16[4,5,128,128]{3,2,1,0:T(8,128)(2,1)} %get-tuple-element.156.refs_0_), channel_id=1, source_target_pairs={{0,2},{1,3},{2,0},{3,1},{4,6},{5,7},{6,4},{7,5}} | collective-permute-start | bytes 1966088 | tf_op jit(solution)/shard_map/ppermute | solution.py:330
  58.7 29.0 %collective-permute-start.49 = (bf16[4,5,128,128]{3,2,1,0:T(8,128)(2,1)}, bf16[4,5,128,128]{3,2,1,0:T(8,128)(2,1)}, u32[]{:S(2)}, u32[]{:S(2)}) collective-permute-start(bf16[4,5,128,128]{3,2,1,0:T(8,128)(2,1)} %get-tuple-element.157), channel_id=1, source_target_pairs={{0,1},{1,0},{2,3},{3,2},{4,5},{5,4},{6,7},{7,6}} | collective-permute-start | bytes 1966088 | tf_op jit(solution)/shard_map/ppermute | solution.py:330
  114.6 28.8 %collective-permute-start.39 = (bf16[4,5,128,128]{3,2,1,0:T(8,128)(2,1)}, bf16[4,5,128,128]{3,2,1,0:T(8,128)(2,1)S(1)}, u32[]{:S(2)}, u32[]{:S(2)}) collective-permute-start(bf16[4,5,128,128]{3,2,1,0:T(8,128)(2,1)} %get-tuple-element.153), channel_id=1, source_target_pairs={{0,5},{1,4},{2,7},{3,6},{4,1},{5,0},{6,3},{7,2}} | collective-permute-start | bytes 1966088 | tf_op jit(solution)/shard_map/ppermute | solution.py:330
  115.4 28.5 %collective-permute-start.35 = (bf16[4,5,128,128]{3,2,1,0:T(8,128)(2,1)}, bf16[4,5,128,128]{3,2,1,0:T(8,128)(2,1)S(1)}, u32[]{:S(2)}, u32[]{:S(2)}) collective-permute-start(bf16[4,5,128,128]{3,2,1,0:T(8,128)(2,1)} %get-tuple-element.153), channel_id=1, source_target_pairs={{0,1},{1,0},{2,3},{3,2},{4,5},{5,4},{6,7},{7,6}} | collective-permute-start | bytes 1966088 | tf_op jit(solution)/shard_map/ppermute | solution.py:330
  143.4 66.1 %collective-permute-start.38 = (bf16[4,5,128,128]{3,2,1,0:T(8,128)(2,1)S(1)}, bf16[4,5,128,128]{3,2,1,0:T(8,128)(2,1)}, u32[]{:S(2)}, u32[]{:S(2)}) collective-permute-start(bf16[4,5,128,128]{3,2,1,0:T(8,128)(2,1)S(1)} %copy-done.10), channel_id=1, source_target_pairs={{0,4},{1,5},{2,6},{3,7},{4,0},{5,1},{6,2},{7,3}} | collective-permute-start | bytes 1966088 | tf_op jit(solution)/shard_map/ppermute | solution.py:330
  144.3 65.2 %collective-permute-start.29 = (bf16[4,5,128,128]{3,2,1,0:T(8,128)(2,1)}, bf16[4,5,128,128]{3,2,1,0:T(8,128)(2,1)S(1)}, u32[]{:S(2)}, u32[]{:S(2)}) collective-permute-start(bf16[4,5,128,128]{3,2,1,0:T(8,128)(2,1)} %get-tuple-element.150.refs_0_), channel_id=1, source_target_pairs={{0,2},{1,3},{2,0},{3,1},{4,6},{5,7},{6,4},{7,5}} | collective-permute-start | bytes 1966088 | tf_op jit(solution)/shard_map/ppermute | solution.py:330
  149.3 61.3 %collective-permute-start.32 = (bf16[4,5,128,128]{3,2,1,0:T(8,128)(2,1)}, bf16[4,5,128,128]{3,2,1,0:T(8,128)(2,1)S(1)}, u32[]{:S(2)}, u32[]{:S(2)}) collective-permute-start(bf16[4,5,128,128]{3,2,1,0:T(8,128)(2,1)} %get-tuple-element.151), channel_id=1, source_target_pairs={{0,5},{1,4},{2,7},{3,6},{4,1},{5,0},{6,3},{7,2}} | collective-permute-start | bytes 1966088 | tf_op jit(solution)/shard_map/ppermute | solution.py:330
  155.5 55.8 %collective-permute-start.54 = (bf16[4,5,128,128]{3,2,1,0:T(8,128)(2,1)}, bf16[4,5,128,128]{3,2,1,0:T(8,128)(2,1)}, u32[]{:S(2)}, u32[]{:S(2)}) collective-permute-start(bf16[4,5,128,128]{3,2,1,0:T(8,128)(2,1)} %copy-done.27), channel_id=1, source_target_pairs={{0,4},{1,5},{2,6},{3,7},{4,0},{5,1},{6,2},{7,3}} | collective-permute-start | bytes 1966088 | tf_op jit(solution)/shard_map/ppermute | solution.py:330
  163.8 47.5 %collective-permute-start.55 = (bf16[4,5,128,128]{3,2,1,0:T(8,128)(2,1)}, bf16[4,5,128,128]{3,2,1,0:T(8,128)(2,1)}, u32[]{:S(2)}, u32[]{:S(2)}) collective-permute-start(bf16[4,5,128,128]{3,2,1,0:T(8,128)(2,1)} %copy-done.28), channel_id=1, source_target_pairs={{0,2},{1,3},{2,0},{3,1},{4,6},{5,7},{6,4},{7,5}} | collective-permute-start | bytes 1966088 | tf_op jit(solution)/shard_map/ppermute | solution.py:330
  209.5 45.2 %collective-permute-start.28 = (bf16[4,5,128,128]{3,2,1,0:T(8,128)(2,1)}, bf16[4,5,128,128]{3,2,1,0:T(8,128)(2,1)S(1)}, u32[]{:S(2)}, u32[]{:S(2)}) collective-permute-start(bf16[4,5,128,128]{3,2,1,0:T(8,128)(2,1)} %get-tuple-element.151), channel_id=1, source_target_pairs={{0,1},{1,0},{2,3},{3,2},{4,5},{5,4},{6,7},{7,6}} | collective-permute-start | bytes 1966088 | tf_op jit(solution)/shard_map/ppermute | solution.py:330
  209.5 46.0 %collective-permute-start.30 = (bf16[4,5,128,128]{3,2,1,0:T(8,128)(2,1)}, bf16[4,5,128,128]{3,2,1,0:T(8,128)(2,1)S(1)}, u32[]{:S(2)}, u32[]{:S(2)}) collective-permute-start(bf16[4,5,128,128]{3,2,1,0:T(8,128)(2,1)} %get-tuple-element.151), channel_id=1, source_target_pairs={{0,3},{1,2},{2,1},{3,0},{4,7},{5,6},{6,5},{7,4}} | collective-permute-start | bytes 1966088 | tf_op jit(solution)/shard_map/ppermute | solution.py:330
  210.6 45.5 %collective-permute-start.31 = (bf16[4,5,128,128]{3,2,1,0:T(8,128)(2,1)S(1)}, bf16[4,5,128,128]{3,2,1,0:T(8,128)(2,1)}, u32[]{:S(2)}, u32[]{:S(2)}) collective-permute-start(bf16[4,5,128,128]{3,2,1,0:T(8,128)(2,1)S(1)} %copy-done.5), channel_id=1, source_target_pairs={{0,4},{1,5},{2,6},{3,7},{4,0},{5,1},{6,2},{7,3}} | collective-permute-start | bytes 1966088 | tf_op jit(solution)/shard_map/ppermute | solution.py:330
  211.3 67.4 %collective-permute-start.63 = (f32[512,8,128]{2,1,0:T(8,128)}, f32[512,8,128]{2,1,0:T(8,128)}, u32[]{:S(2)}, u32[]{:S(2)}) collective-permute-start(f32[512,8,128]{2,1,0:T(8,128)} %get-tuple-element.168), channel_id=1, source_target_pairs={{0,1},{1,0},{2,3},{3,2},{4,5},{5,4},{6,7},{7,6}} | collective-permute-start | bytes 6291464 | tf_op jit(solution)/shard_map/ppermute | solution.py:330
  211.3 70.3 %collective-permute-start.64 = (f32[512,8,128]{2,1,0:T(8,128)}, f32[512,8,128]{2,1,0:T(8,128)}, u32[]{:S(2)}, u32[]{:S(2)}) collective-permute-start(f32[512,8,128]{2,1,0:T(8,128)} %get-tuple-element.169), channel_id=1, source_target_pairs={{0,1},{1,0},{2,3},{3,2},{4,5},{5,4},{6,7},{7,6}} | collective-permute-start | bytes 6291464 | tf_op jit(solution)/shard_map/ppermute | solution.py:330
  255.5 42.4 %collective-permute-start.67 = (f32[512,8,128]{2,1,0:T(8,128)}, f32[512,8,128]{2,1,0:T(8,128)S(1)}, u32[]{:S(2)}, u32[]{:S(2)}) collective-permute-start(f32[512,8,128]{2,1,0:T(8,128)} %get-tuple-element.182), channel_id=1, source_target_pairs={{0,1},{1,0},{2,3},{3,2},{4,5},{5,4},{6,7},{7,6}} | collective-permute-start | bytes 6291464 | tf_op jit(solution)/shard_map/ppermute | solution.py:330
  255.5 43.1 %collective-permute-start.68 = (f32[512,8,128]{2,1,0:T(8,128)}, f32[512,8,128]{2,1,0:T(8,128)}, u32[]{:S(2)}, u32[]{:S(2)}) collective-permute-start(f32[512,8,128]{2,1,0:T(8,128)} %get-tuple-element.183), channel_id=1, source_target_pairs={{0,1},{1,0},{2,3},{3,2},{4,5},{5,4},{6,7},{7,6}} | collective-permute-start | bytes 6291464 | tf_op jit(solution)/shard_map/ppermute | solution.py:330
  294.9 53.0 %collective-permute-start.25 = (bf16[4,5,128,128]{3,2,1,0:T(8,128)(2,1)}, bf16[4,5,128,128]{3,2,1,0:T(8,128)(2,1)S(1)}, u32[]{:S(2)}, u32[]{:S(2)}) collective-permute-start(bf16[4,5,128,128]{3,2,1,0:T(8,128)(2,1)} %get-tuple-element.149), channel_id=1, source_target_pairs={{0,5},{1,4},{2,7},{3,6},{4,1},{5,0},{6,3},{7,2}} | collective-permute-start | bytes 1966088 | tf_op jit(solution)/shard_map/ppermute | solution.py:330
  295.5 53.9 %collective-permute-start.21 = (bf16[4,5,128,128]{3,2,1,0:T(8,128)(2,1)}, bf16[4,5,128,128]{3,2,1,0:T(8,128)(2,1)}, u32[]{:S(2)}, u32[]{:S(2)}) collective-permute-start(bf16[4,5,128,128]{3,2,1,0:T(8,128)(2,1)} %get-tuple-element.149), channel_id=1, source_target_pairs={{0,1},{1,0},{2,3},{3,2},{4,5},{5,4},{6,7},{7,6}} | collective-permute-start | bytes 1966088 | tf_op jit(solution)/shard_map/ppermute | solution.py:330
  296.7 50.3 %collective-permute-start.22 = (bf16[4,5,128,128]{3,2,1,0:T(8,128)(2,1)}, bf16[4,5,128,128]{3,2,1,0:T(8,128)(2,1)}, u32[]{:S(2)}, u32[]{:S(2)}) collective-permute-start(bf16[4,5,128,128]{3,2,1,0:T(8,128)(2,1)} %get-tuple-element.148.refs_0_), channel_id=1, source_target_pairs={{0,2},{1,3},{2,0},{3,1},{4,6},{5,7},{6,4},{7,5}} | collective-permute-start | bytes 1966088 | tf_op jit(solution)/shard_map/ppermute | solution.py:330
  297.9 52.6 %collective-permute-start.40 = (bf16[4,5,128,128]{3,2,1,0:T(8,128)(2,1)}, bf16[4,5,128,128]{3,2,1,0:T(8,128)(2,1)}, u32[]{:S(2)}, u32[]{:S(2)}) collective-permute-start(bf16[4,5,128,128]{3,2,1,0:T(8,128)(2,1)} %collective-permute-done.36.refs_2_), channel_id=1, source_target_pairs={{0,4},{1,5},{2,6},{3,7},{4,0},{5,1},{6,2},{7,3}} | collective-permute-start | bytes 1966088 | tf_op jit(solution)/shard_map/ppermute | solution.py:330
  298.7 51.9 %collective-permute-start.41 = (bf16[4,5,128,128]{3,2,1,0:T(8,128)(2,1)S(1)}, bf16[4,5,128,128]{3,2,1,0:T(8,128)(2,1)}, u32[]{:S(2)}, u32[]{:S(2)}) collective-permute-start(bf16[4,5,128,128]{3,2,1,0:T(8,128)(2,1)S(1)} %copy-done.13), channel_id=1, source_target_pairs={{0,2},{1,3},{2,0},{3,1},{4,6},{5,7},{6,4},{7,5}} | collective-permute-start | bytes 1966088 | tf_op jit(solution)/shard_map/ppermute | solution.py:330
  347.0 46.9 %collective-permute-start.23 = (bf16[4,5,128,128]{3,2,1,0:T(8,128)(2,1)S(1)}, bf16[4,5,128,128]{3,2,1,0:T(8,128)(2,1)S(1)}, u32[]{:S(2)}, u32[]{:S(2)}) collective-permute-start(bf16[4,5,128,128]{3,2,1,0:T(8,128)(2,1)S(1)} %copy-done.51), channel_id=1, source_target_pairs={{0,3},{1,2},{2,1},{3,0},{4,7},{5,6},{6,5},{7,4}} | collective-permute-start | bytes 1966088 | tf_op jit(solution)/shard_map/ppermute | solution.py:330
  347.9 46.9 %collective-permute-start.24 = (bf16[4,5,128,128]{3,2,1,0:T(8,128)(2,1)}, bf16[4,5,128,128]{3,2,1,0:T(8,128)(2,1)}, u32[]{:S(2)}, u32[]{:S(2)}) collective-permute-start(bf16[4,5,128,128]{3,2,1,0:T(8,128)(2,1)} %get-tuple-element.148.refs_0_), channel_id=1, source_target_pairs={{0,4},{1,5},{2,6},{3,7},{4,0},{5,1},{6,2},{7,3}} | collective-permute-start | bytes 1966088 | tf_op jit(solution)/shard_map/ppermute | solution.py:330
  349.3 45.9 %collective-permute-start.15 = (bf16[4,5,128,128]{3,2,1,0:T(8,128)(2,1)S(1)}, bf16[4,5,128,128]{3,2,1,0:T(8,128)(2,1)}, u32[]{:S(2)}, u32[]{:S(2)}) collective-permute-start(bf16[4,5,128,128]{3,2,1,0:T(8,128)(2,1)S(1)} %copy-done.4), channel_id=1, source_target_pairs={{0,2},{1,3},{2,0},{3,1},{4,6},{5,7},{6,4},{7,5}} | collective-permute-start | bytes 1966088 | tf_op jit(solution)/shard_map/ppermute | solution.py:330
  350.6 68.1 %collective-permute-start.71 = (f32[512,8,128]{2,1,0:T(8,128)}, f32[512,8,128]{2,1,0:T(8,128)}, u32[]{:S(2)}, u32[]{:S(2)}) collective-permute-start(f32[512,8,128]{2,1,0:T(8,128)} %get-tuple-element.196), channel_id=1, source_target_pairs={{0,1},{1,0},{2,3},{3,2},{4,5},{5,4},{6,7},{7,6}} | collective-permute-start | bytes 6291464 | tf_op jit(solution)/shard_map/ppermute | solution.py:330
  350.6 68.0 %collective-permute-start.72 = (f32[512,8,128]{2,1,0:T(8,128)}, f32[512,8,128]{2,1,0:T(8,128)}, u32[]{:S(2)}, u32[]{:S(2)}) collective-permute-start(f32[512,8,128]{2,1,0:T(8,128)} %get-tuple-element.197), channel_id=1, source_target_pairs={{0,1},{1,0},{2,3},{3,2},{4,5},{5,4},{6,7},{7,6}} | collective-permute-start | bytes 6291464 | tf_op jit(solution)/shard_map/ppermute | solution.py:330
  394.8 41.5 %collective-permute-start.75 = (f32[512,8,128]{2,1,0:T(8,128)}, f32[512,8,128]{2,1,0:T(8,128)S(1)}, u32[]{:S(2)}, u32[]{:S(2)}) collective-permute-start(f32[512,8,128]{2,1,0:T(8,128)} %get-tuple-element.210), channel_id=1, source_target_pairs={{0,1},{1,0},{2,3},{3,2},{4,5},{5,4},{6,7},{7,6}} | collective-permute-start | bytes 6291464 | tf_op jit(solution)/shard_map/ppermute | solution.py:330
  394.8 42.7 %collective-permute-start.76 = (f32[512,8,128]{2,1,0:T(8,128)}, f32[512,8,128]{2,1,0:T(8,128)}, u32[]{:S(2)}, u32[]{:S(2)}) collective-permute-start(f32[512,8,128]{2,1,0:T(8,128)} %get-tuple-element.211), channel_id=1, source_target_pairs={{0,1},{1,0},{2,3},{3,2},{4,5},{5,4},{6,7},{7,6}} | collective-permute-start | bytes 6291464 | tf_op jit(solution)/shard_map/ppermute | solution.py:330
  434.0 52.1 %collective-permute-start.18 = (bf16[4,5,128,128]{3,2,1,0:T(8,128)(2,1)}, bf16[4,5,128,128]{3,2,1,0:T(8,128)(2,1)}, u32[]{:S(2)}, u32[]{:S(2)}) collective-permute-start(bf16[4,5,128,128]{3,2,1,0:T(8,128)(2,1)} %get-tuple-element.147), channel_id=1, source_target_pairs={{0,5},{1,4},{2,7},{3,6},{4,1},{5,0},{6,3},{7,2}} | collective-permute-start | bytes 1966088 | tf_op jit(solution)/shard_map/ppermute | solution.py:330
  434.0 53.2 %collective-permute-start.14 = (bf16[4,5,128,128]{3,2,1,0:T(8,128)(2,1)}, bf16[4,5,128,128]{3,2,1,0:T(8,128)(2,1)}, u32[]{:S(2)}, u32[]{:S(2)}) collective-permute-start(bf16[4,5,128,128]{3,2,1,0:T(8,128)(2,1)} %get-tuple-element.147), channel_id=1, source_target_pairs={{0,1},{1,0},{2,3},{3,2},{4,5},{5,4},{6,7},{7,6}} | collective-permute-start | bytes 1966088 | tf_op jit(solution)/shard_map/ppermute | solution.py:330
  434.9 54.1 %collective-permute-start.16 = (bf16[4,5,128,128]{3,2,1,0:T(8,128)(2,1)}, bf16[4,5,128,128]{3,2,1,0:T(8,128)(2,1)}, u32[]{:S(2)}, u32[]{:S(2)}) collective-permute-start(bf16[4,5,128,128]{3,2,1,0:T(8,128)(2,1)} %get-tuple-element.147), channel_id=1, source_target_pairs={{0,3},{1,2},{2,1},{3,0},{4,7},{5,6},{6,5},{7,4}} | collective-permute-start | bytes 1966088 | tf_op jit(solution)/shard_map/ppermute | solution.py:330
  436.3 52.9 %collective-permute-start.26 = (bf16[4,5,128,128]{3,2,1,0:T(8,128)(2,1)}, bf16[4,5,128,128]{3,2,1,0:T(8,128)(2,1)}, u32[]{:S(2)}, u32[]{:S(2)}) collective-permute-start(bf16[4,5,128,128]{3,2,1,0:T(8,128)(2,1)} %collective-permute-done.22.refs_2_), channel_id=1, source_target_pairs={{0,4},{1,5},{2,6},{3,7},{4,0},{5,1},{6,2},{7,3}} | collective-permute-start | bytes 1966088 | tf_op jit(solution)/shard_map/ppermute | solution.py:330
  437.5 52.8 %collective-permute-start.27 = (bf16[4,5,128,128]{3,2,1,0:T(8,128)(2,1)S(1)}, bf16[4,5,128,128]{3,2,1,0:T(8,128)(2,1)}, u32[]{:S(2)}, u32[]{:S(2)}) collective-permute-start(bf16[4,5,128,128]{3,2,1,0:T(8,128)(2,1)S(1)} %copy-done.20), channel_id=1, source_target_pairs={{0,2},{1,3},{2,0},{3,1},{4,6},{5,7},{6,4},{7,5}} | collective-permute-start | bytes 1966088 | tf_op jit(solution)/shard_map/ppermute | solution.py:330
  486.1 46.9 %collective-permute-start.17 = (bf16[4,5,128,128]{3,2,1,0:T(8,128)(2,1)S(1)}, bf16[4,5,128,128]{3,2,1,0:T(8,128)(2,1)S(1)}, u32[]{:S(2)}, u32[]{:S(2)}) collective-permute-start(bf16[4,5,128,128]{3,2,1,0:T(8,128)(2,1)S(1)} %copy-done.4), channel_id=1, source_target_pairs={{0,4},{1,5},{2,6},{3,7},{4,0},{5,1},{6,2},{7,3}} | collective-permute-start | bytes 1966088 | tf_op jit(solution)/shard_map/ppermute | solution.py:330
  487.2 47.0 %collective-permute-start.2 = (bf16[4,5,128,128]{3,2,1,0:T(8,128)(2,1)S(1)}, bf16[4,5,128,128]{3,2,1,0:T(8,128)(2,1)}, u32[]{:S(2)}, u32[]{:S(2)}) collective-permute-start(bf16[4,5,128,128]{3,2,1,0:T(8,128)(2,1)S(1)} %copy-done.17), channel_id=1, source_target_pairs={{0,2},{1,3},{2,0},{3,1},{4,6},{5,7},{6,4},{7,5}} | collective-permute-start | bytes 1966088 | tf_op jit(solution)/shard_map/ppermute | solution.py:330
  489.1 45.3 %collective-permute-start.5 = (bf16[4,5,128,128]{3,2,1,0:T(8,128)(2,1)}, bf16[4,5,128,128]{3,2,1,0:T(8,128)(2,1)}, u32[]{:S(2)}, u32[]{:S(2)}) collective-permute-start(bf16[4,5,128,128]{3,2,1,0:T(8,128)(2,1)} %get-tuple-element.141), channel_id=1, source_target_pairs={{0,5},{1,4},{2,7},{3,6},{4,1},{5,0},{6,3},{7,2}} | collective-permute-start | bytes 1966088 | tf_op jit(solution)/shard_map/ppermute | solution.py:330
  489.2 66.7 %collective-permute-start.79 = (f32[512,8,128]{2,1,0:T(8,128)}, f32[512,8,128]{2,1,0:T(8,128)}, u32[]{:S(2)}, u32[]{:S(2)}) collective-permute-start(f32[512,8,128]{2,1,0:T(8,128)} %get-tuple-element.224), channel_id=1, source_target_pairs={{0,1},{1,0},{2,3},{3,2},{4,5},{5,4},{6,7},{7,6}} | collective-permute-start | bytes 6291464 | tf_op jit(solution)/shard_map/ppermute | solution.py:330
  490.3 65.6 %collective-permute-start.80 = (f32[512,8,128]{2,1,0:T(8,128)}, f32[512,8,128]{2,1,0:T(8,128)}, u32[]{:S(2)}, u32[]{:S(2)}) collective-permute-start(f32[512,8,128]{2,1,0:T(8,128)} %get-tuple-element.225), channel_id=1, source_target_pairs={{0,1},{1,0},{2,3},{3,2},{4,5},{5,4},{6,7},{7,6}} | collective-permute-start | bytes 6291464 | tf_op jit(solution)/shard_map/ppermute | solution.py:330
  533.9 40.5 %collective-permute-start.83 = (f32[512,8,128]{2,1,0:T(8,128)}, f32[512,8,128]{2,1,0:T(8,128)S(1)}, u32[]{:S(2)}, u32[]{:S(2)}) collective-permute-start(f32[512,8,128]{2,1,0:T(8,128)} %get-tuple-element.238), channel_id=1, source_target_pairs={{0,1},{1,0},{2,3},{3,2},{4,5},{5,4},{6,7},{7,6}} | collective-permute-start | bytes 6291464 | tf_op jit(solution)/shard_map/ppermute | solution.py:330
  534.3 40.9 %collective-permute-start.84 = (f32[512,8,128]{2,1,0:T(8,128)}, f32[512,8,128]{2,1,0:T(8,128)}, u32[]{:S(2)}, u32[]{:S(2)}) collective-permute-start(f32[512,8,128]{2,1,0:T(8,128)} %get-tuple-element.239), channel_id=1, source_target_pairs={{0,1},{1,0},{2,3},{3,2},{4,5},{5,4},{6,7},{7,6}} | collective-permute-start | bytes 6291464 | tf_op jit(solution)/shard_map/ppermute | solution.py:330
  572.5 51.9 %collective-permute-start.1 = (bf16[4,5,128,128]{3,2,1,0:T(8,128)(2,1)}, bf16[4,5,128,128]{3,2,1,0:T(8,128)(2,1)S(1)}, u32[]{:S(2)}, u32[]{:S(2)}) collective-permute-start(bf16[4,5,128,128]{3,2,1,0:T(8,128)(2,1)} %get-tuple-element.141), channel_id=1, source_target_pairs={{0,1},{1,0},{2,3},{3,2},{4,5},{5,4},{6,7},{7,6}} | collective-permute-start | bytes 1966088 | tf_op jit(solution)/shard_map/ppermute | solution.py:330
  572.5 52.0 %collective-permute-start.3 = (bf16[4,5,128,128]{3,2,1,0:T(8,128)(2,1)}, bf16[4,5,128,128]{3,2,1,0:T(8,128)(2,1)}, u32[]{:S(2)}, u32[]{:S(2)}) collective-permute-start(bf16[4,5,128,128]{3,2,1,0:T(8,128)(2,1)} %get-tuple-element.141), channel_id=1, source_target_pairs={{0,3},{1,2},{2,1},{3,0},{4,7},{5,6},{6,5},{7,4}} | collective-permute-start | bytes 1966088 | tf_op jit(solution)/shard_map/ppermute | solution.py:330
  573.1 51.9 %collective-permute-start.4 = (bf16[4,5,128,128]{3,2,1,0:T(8,128)(2,1)S(1)}, bf16[4,5,128,128]{3,2,1,0:T(8,128)(2,1)}, u32[]{:S(2)}, u32[]{:S(2)}) collective-permute-start(bf16[4,5,128,128]{3,2,1,0:T(8,128)(2,1)S(1)} %copy-done.17), channel_id=1, source_target_pairs={{0,4},{1,5},{2,6},{3,7},{4,0},{5,1},{6,2},{7,3}} | collective-permute-start | bytes 1966088 | tf_op jit(solution)/shard_map/ppermute | solution.py:330
  574.3 50.6 %collective-permute-start.6 = (bf16[4,5,128,128]{3,2,1,0:T(8,128)(2,1)}, bf16[4,5,128,128]{3,2,1,0:T(8,128)(2,1)}, u32[]{:S(2)}, u32[]{:S(2)}) collective-permute-start(bf16[4,5,128,128]{3,2,1,0:T(8,128)(2,1)} %collective-permute-done.2.refs_2_), channel_id=1, source_target_pairs={{0,4},{1,5},{2,6},{3,7},{4,0},{5,1},{6,2},{7,3}} | collective-permute-start | bytes 1966088 | tf_op jit(solution)/shard_map/ppermute | solution.py:330
  575.1 49.8 %collective-permute-start.7 = (bf16[4,5,128,128]{3,2,1,0:T(8,128)(2,1)}, bf16[4,5,128,128]{3,2,1,0:T(8,128)(2,1)}, u32[]{:S(2)}, u32[]{:S(2)}) collective-permute-start(bf16[4,5,128,128]{3,2,1,0:T(8,128)(2,1)} %collective-permute-done.5.refs_5_), channel_id=1, source_target_pairs={{0,2},{1,3},{2,0},{3,1},{4,6},{5,7},{6,4},{7,5}} | collective-permute-start | bytes 1966088 | tf_op jit(solution)/shard_map/ppermute | solution.py:330
  624.4 56.4 %collective-permute-start.91 = (f32[512,8,128]{2,1,0:T(8,128)}, f32[512,8,128]{2,1,0:T(8,128)S(1)}, u32[]{:S(2)}, u32[]{:S(2)}) collective-permute-start(f32[512,8,128]{2,1,0:T(8,128)} %get-tuple-element.254), channel_id=1, source_target_pairs={{0,1},{1,0},{2,3},{3,2},{4,5},{5,4},{6,7},{7,6}} | collective-permute-start | bytes 6291464 | tf_op jit(solution)/shard_map/ppermute | solution.py:330
  624.5 58.9 %collective-permute-start.92 = (f32[512,8,128]{2,1,0:T(8,128)}, f32[512,8,128]{2,1,0:T(8,128)}, u32[]{:S(2)}, u32[]{:S(2)}) collective-permute-start(f32[512,8,128]{2,1,0:T(8,128)} %get-tuple-element.255), channel_id=1, source_target_pairs={{0,1},{1,0},{2,3},{3,2},{4,5},{5,4},{6,7},{7,6}} | collective-permute-start | bytes 6291464 | tf_op jit(solution)/shard_map/ppermute | solution.py:330
  (104 other events, 1600.0 us)
where the time goes:
time: 711 us; the launch traced here: 705 us
  Pallas kernels  410 us (58%)
  waiting for transfers between devices  184 us (26%)
  starting transfers between devices  71.3 us (10%)
  local copies, waits for them, and re-layouts  33.4 us (5%)
    pallas_call x8, Pallas kernels, main_chunk(): pl.pallas_call(functools.partial(main_kernel, aliased, score_scale), grid...  342 us
    ppermute x97, waiting for transfers between devices, hop(): return lax.ppermute(x, 'cp', perm)  184 us
    ppermute x97, starting transfers between devices, hop(): return lax.ppermute(x, 'cp', perm)  71.3 us
    pallas_call x8, Pallas kernels, place(): pl.pallas_call(place_kernel, grid_spec=pltpu.PrefetchScalarGridSpec(num_s...  41 us
    pallas_call x8, Pallas kernels, pack_chunk(): pl.pallas_call(pack_kernel, grid_spec=pltpu.PrefetchScalarGridSpec(num_sc...  23.8 us
    unnamed x112, local copies, waits for them, and re-layouts  20.5 us
  transfers between devices with their start and end apart: 97, of which 36 were waited for; matrix products, arithmetic and copies ran while one was open for 1% of the time, Pallas kernels for 57%

commit v1 on v0

--- a/solution.py
+++ b/solution.py
@@ -92,17 +92,51 @@
     )(me, *blocks)
 
 
-def main_kernel(aliased, score_scale, me_ref, *refs):
-    n_big = 4 if aliased else 0
+def partner_dw(h0, scale, ct_ref, dkv_in, bigs):
+    for w in range(2):
+        view = bigs[w].reshape(L * HC, D)
+        for t in range(2):
+            dw = dot(ct_ref[t * QB:(t + 1) * QB, :], dkv_in[0, w], 1, 0)
+            dw = dw * scale if w == 0 else dw
+            for k in range(2):
+                view[pl.ds(t * QB * HC + h0 + k, QB, stride=HC), :] = dw[:, k * D:(k + 1) * D]
+
+
+def main_kernel(aliased, prev, score_scale, me_ref, *refs):
+    _, ct_ref, _, _, _, _, _ = refs[ND:ND + 7]
+    n_in = ND + 7
+    if prev:
+        dkv_in, o_in, dq_in = refs[n_in:n_in + 3]
+        n_in += 3
+    outs = refs[n_in + (4 if aliased else 0):]
+    (dwk_big, dwv_big, o_big, dq_big, dkv_out, o_par, dq_par, dc_out, dr_out, *scratch) = outs
+    step = pl.program_id(0)
+    if not prev:
+        main_body(step, score_scale, me_ref, refs, outs)
+        return
+
+    @pl.when(step < NP)
+    def _():
+        partner_dw(2 * step, score_scale, ct_ref, dkv_in, (dwk_big, dwv_big))
+
+    @pl.when(step == 0)
+    def _():
+        o_big[...] = o_in[...]
+        dq_big[...] = dq_in[...]
+
+    @pl.when(step >= NP)
+    def _():
+        main_body(step - NP, score_scale, me_ref, refs, outs)
+
+
+def main_body(p, score_scale, me_ref, refs, outs):
     a_refs = refs[:ND]
     c_ref, ct_ref, r_ref, wk_ref, wv_ref, dc_in, dr_in = refs[ND:ND + 7]
-    outs = refs[ND + 7 + n_big:]
-    (dwk_big, dwv_big, o_big, dq_big, dwk_out, dwv_out, o_par, dq_par, dc_out, dr_out,
-     wsc, wk, wv, kr, vs, qa, do, pt, dst, st, dp, dkr, dkb, dvb, osc, dqn, dqr, oacc, dqacc) = outs
+    (dwk_big, dwv_big, o_big, dq_big, dkv_out, o_par, dq_par, dc_out, dr_out,
+     wsc, wk, wv, kr, vs, qa, do, pt, dst, st, dp, dkr, osc, dqn, dqr, oacc, dqacc) = outs
     me = me_ref[0]
     core = jnp.bitwise_and(me, 1)
     chip = me // 2
-    p = pl.program_id(0)
     own_rows = pl.ds(pl.multiple_of(chip * QB, QB), QB)
     k2 = score_scale * math.log2(math.e)
 
@@ -179,8 +213,9 @@
             rows = slice(t * QB, (t + 1) * QB)
             grad = dot(dst[rows, t * QB:], qa[k, t * QB:, :], 1, 0)
             dkr[rows, :] = grad[:, D:]
-            dkb[k, rows, :] = grad[:, :D].astype(BF)
-            dvb[k, rows, :] = dot(pt[rows, t * QB:], do[k, t * QB:, :], 1, 0).astype(BF)
+            lanes = pl.ds(pl.multiple_of(k * D, D), D)
+            dkv_out[0, 0, rows, lanes] = grad[:, :D].astype(BF)
+            dkv_out[0, 1, rows, lanes] = dot(pt[rows, t * QB:], do[k, t * QB:, :], 1, 0).astype(BF)
 
         scores(NQ - 1)
         for i in range(NQ - 1, -1, -1):
@@ -203,19 +238,10 @@
             rope = dqacc[tok, D:]
             dqr[side, rows, :] = jnp.where(k == 0, rope, pltpu.roll(rope, R, 1))
 
-    for w, grad_b, big, out, mul in ((wk, dkb, dwk_big, dwk_out, score_scale), (wv, dvb, dwv_big, dwv_out, None)):
-        own = jnp.concatenate([grad_b[0, own_rows, :], grad_b[1, own_rows, :]], axis=1)
-        d_lat = dot(own, w[p], 1, 1)
-        dc_out[...] += d_lat if mul is None else d_lat * mul
-        both = jnp.concatenate([grad_b[0], grad_b[1]], axis=1)
-        for t in range(2):
-            rows = slice(t * QB, (t + 1) * QB)
-            dw = dot(ct_ref[rows, :], both, 1, 0)
-            dw = dw if mul is None else dw * mul
-            for k in range(2):
-                view = pl.ds(t * QB * HC + 2 * p + k, QB, stride=HC)
-                big.reshape(L * HC, D)[view, :] = dw[:, k * D:(k + 1) * D]
-                out.reshape(L * HC, D)[view, :] = dw[:, k * D:(k + 1) * D]
+    for g, w in enumerate((wk, wv)):
+        d_lat = dot(dkv_out[0, g, own_rows, :], w[p], 1, 1)
+        dc_out[...] += d_lat if g else d_lat * score_scale
+    partner_dw(2 * p, score_scale, ct_ref, dkv_out, (dwk_big, dwv_big))
 
     @pl.when(p == NP - 1)
     def _():
@@ -231,9 +257,24 @@
             jax.ShapeDtypeStruct((TB, 128, D), BF), jax.ShapeDtypeStruct((TB, 128, D + R), BF)]
 
 
-def main_chunk(j, score_scale, me, blocks, c_abs, c_t, r_abs, w_uk, w_uv, dc, dr, big):
+def main_chunk(j, score_scale, me, blocks, c_abs, c_t, r_abs, w_uk, w_uv, dc, dr, big, prev):
+    per = 64 // HC
+    lead = NP if prev is not None else 0
+
     def head_block(i, m):
-        return (0, (m[0] % 2) * (64 // HC) + j, 0)
+        return (0, (m[0] % 2) * per + j, 0)
+
+    def out_block(i, m):
+        own = (m[0] % 2) * per + j
+        if not lead:
+            return (0, own, 0)
+        return (0, jnp.where(i < lead, (1 - m[0] % 2) * per + j - 2, own), 0)
+
+    def main_step(i, m):
+        return (jnp.maximum(i - lead, 0), 0, 0, 0)
+
+    def prev_step(i, m):
+        return (jnp.minimum(i, NP - 1), 0, 0, 0)
 
     def full2(i, m):
         return (0, 0)
@@ -241,9 +282,8 @@
     def full3(i, m):
         return (0, 0, 0)
 
-    aliased = big is not None
     once = pl.Buffered(1)
-    in_specs = ([pl.BlockSpec((1, 5, TB, D), lambda i, m: (i, 0, 0, 0))] * ND
+    in_specs = ([pl.BlockSpec((1, 5, TB, D), main_step)] * ND
                 + [pl.BlockSpec((S, L), full2, pipeline_mode=once),
                    pl.BlockSpec((L, S), full2, pipeline_mode=once),
                    pl.BlockSpec((S, D), full2, pipeline_mode=once),
@@ -252,22 +292,27 @@
                    pl.BlockSpec((QB, L), full2, pipeline_mode=once),
                    pl.BlockSpec((2, QB, D), full3, pipeline_mode=once)])
     args = list(blocks) + [c_abs, c_t, r_abs, w_uk, w_uv, dc, dr]
+    if prev is not None:
+        in_specs += [pl.BlockSpec((1, 2, S, 2 * D), prev_step),
+                     pl.BlockSpec((TB, HC, D), full3, pipeline_mode=once),
+                     pl.BlockSpec((TB, HC, D + R), full3, pipeline_mode=once)]
+        args += list(prev)
     aliases = {}
-    if aliased:
+    if big is not None:
         in_specs += [pl.BlockSpec(memory_space=pl.ANY)] * 4
         aliases = {1 + len(args) + b: b for b in range(4)}
         args += list(big)
+    tri = QB * NQ * (NQ + 1) // 2
     outs = pl.pallas_call(
-        functools.partial(main_kernel, aliased, score_scale),
+        functools.partial(main_kernel, big is not None, prev is not None, score_scale),
         grid_spec=pltpu.PrefetchScalarGridSpec(
-            num_scalar_prefetch=1, grid=(NP,),
+            num_scalar_prefetch=1, grid=(NP + lead,),
             in_specs=in_specs,
-            out_specs=[pl.BlockSpec((L, HC, D), head_block, pipeline_mode=once),
-                       pl.BlockSpec((L, HC, D), head_block, pipeline_mode=once),
-                       pl.BlockSpec((TB, HC, D), head_block, pipeline_mode=once),
-                       pl.BlockSpec((TB, HC, D + R), head_block, pipeline_mode=once),
-                       pl.BlockSpec((L, HC, D), full3, pipeline_mode=once),
-                       pl.BlockSpec((L, HC, D), full3, pipeline_mode=once),
+            out_specs=[pl.BlockSpec((L, HC, D), out_block),
+                       pl.BlockSpec((L, HC, D), out_block),
+                       pl.BlockSpec((TB, HC, D), out_block),
+                       pl.BlockSpec((TB, HC, D + R), out_block),
+                       pl.BlockSpec((1, 2, S, 2 * D), main_step),
                        pl.BlockSpec((TB, HC, D), full3, pipeline_mode=once),
                        pl.BlockSpec((TB, HC, D + R), full3, pipeline_mode=once),
                        pl.BlockSpec((QB, L), full2, pipeline_mode=once),
@@ -278,14 +323,13 @@
                 pltpu.VMEM((2, S, 2 * D), BF), pltpu.VMEM((2, S, D), BF),
                 pltpu.VMEM((2, S, 2 * D), BF), pltpu.VMEM((2, S, D), BF),
                 pltpu.VMEM((S, S), BF), pltpu.VMEM((S, S), BF),
-                pltpu.VMEM((QB * NQ * (NQ + 1) // 2, QB), F32), pltpu.VMEM((QB * NQ * (NQ + 1) // 2, QB), F32),
+                pltpu.VMEM((tri, QB), F32), pltpu.VMEM((tri, QB), F32),
                 pltpu.VMEM((S, D), F32),
-                pltpu.VMEM((2, S, D), BF), pltpu.VMEM((2, S, D), BF),
                 pltpu.VMEM((2, TB * HC, D), F32), pltpu.VMEM((2, TB * HC, D), F32),
                 pltpu.VMEM((2, TB * HC, D), F32),
                 pltpu.VMEM((QB, D), F32), pltpu.VMEM((QB, 2 * D), F32)]),
         out_shape=big_shapes() + [
-            jax.ShapeDtypeStruct((L, HC, D), F32), jax.ShapeDtypeStruct((L, HC, D), F32),
+            jax.ShapeDtypeStruct((NP, 2, S, 2 * D), BF),
             jax.ShapeDtypeStruct((TB, HC, D), BF), jax.ShapeDtypeStruct((TB, HC, D + R), BF),
             jax.ShapeDtypeStruct((QB, L), F32), jax.ShapeDtypeStruct((2, QB, D), F32)],
         input_output_aliases=aliases,
@@ -293,35 +337,43 @@
         name="mla_chunk",
         cost_estimate=pl.CostEstimate(flops=25 * 10 ** 9, bytes_accessed=20 * 10 ** 6, transcendentals=0),
     )(me, *args)
-    return outs[:4], outs[4:8], outs[8], outs[9]
-
-
-def place_kernel(core_ref, *refs):
-    ins, outs = refs[:4], refs[8:]
-    for a, b in zip(ins, outs):
-        b[...] = a[...]
-
-
-def place(j, core, received, big):
+    return outs[:4], outs[4:7], outs[7], outs[8]
+
+
+def last_kernel(score_scale, core_ref, ct_ref, dkv_in, o_in, dq_in, *refs):
+    dwk_big, dwv_big, o_big, dq_big = refs[4:]
+    step = pl.program_id(0)
+    partner_dw(2 * step, score_scale, ct_ref, dkv_in, (dwk_big, dwv_big))
+
+    @pl.when(step == 0)
+    def _():
+        o_big[...] = o_in[...]
+        dq_big[...] = dq_in[...]
+
+
+def last_chunk(j, score_scale, core, c_t, prev, big):
     def at(i, c):
-        return (i, (1 - c[0]) * (64 // HC) + j, 0)
-
-    def src(i, c):
-        return (i, 0, 0)
-
-    steps = 4
-    shapes = [(L // steps, HC, D), (L // steps, HC, D), (TB // steps, HC, D), (TB // steps, HC, D + R)]
+        return (0, (1 - c[0]) * (64 // HC) + j, 0)
+
+    def full3(i, c):
+        return (0, 0, 0)
+
     return pl.pallas_call(
-        place_kernel,
+        functools.partial(last_kernel, score_scale),
         grid_spec=pltpu.PrefetchScalarGridSpec(
-            num_scalar_prefetch=1, grid=(steps,),
-            in_specs=[pl.BlockSpec(s, src) for s in shapes] + [pl.BlockSpec(memory_space=pl.ANY)] * 4,
-            out_specs=[pl.BlockSpec(s, at) for s in shapes]),
+            num_scalar_prefetch=1, grid=(NP,),
+            in_specs=[pl.BlockSpec((L, S), lambda i, c: (0, 0), pipeline_mode=pl.Buffered(1)),
+                      pl.BlockSpec((1, 2, S, 2 * D), lambda i, c: (i, 0, 0, 0)),
+                      pl.BlockSpec((TB, HC, D), full3), pl.BlockSpec((TB, HC, D + R), full3)]
+                     + [pl.BlockSpec(memory_space=pl.ANY)] * 4,
+            out_specs=[pl.BlockSpec((L, HC, D), at), pl.BlockSpec((L, HC, D), at),
+                       pl.BlockSpec((TB, HC, D), at), pl.BlockSpec((TB, HC, D + R), at)]),
         out_shape=big_shapes(),
         input_output_aliases={5 + b: b for b in range(4)},
-        name="place",
+        compiler_params=pltpu.CompilerParams(vmem_limit_bytes=40 * 2 ** 20),
+        name="last",
         cost_estimate=pl.CostEstimate(flops=2 * 10 ** 9, bytes_accessed=10 ** 7, transcendentals=0),
-    )(core, *received, *big)
+    )(core, c_t, *prev, *big)
 
 
 def solution(mesh):
@@ -342,9 +394,10 @@
         lats[1] = lat1
         c_abs, c_t, r_abs = prep(me, lats)
 
+        packs = [pack_chunk(j, core, queries, d_out) for j in range(n_chunks)]
+        me0 = lax.optimization_barrier((me, *[own for own, _ in packs]))[0]
         recv = []
-        for j in range(n_chunks):
-            own, oth = pack_chunk(j, core, queries, d_out)
+        for own, oth in packs:
             a1, a2, a5, a3, a4 = [hop(x, k)
                                   for x, k in ((oth, 1), (own, 2), (oth, 5), (oth, 3), (own, 4))]
             a6, a7 = hop(a2, 4), hop(a5, 2)
@@ -353,13 +406,12 @@
         dc = jnp.zeros((QB, L), F32)
         dr = jnp.zeros((2, QB, D), F32)
         big = None
-        pending = None
+        sent = []
         for j in range(n_chunks):
-            big, send, dc, dr = main_chunk(j, score_scale, me, recv[j], c_abs, c_t, r_abs,
-                                           w_uk, w_uv, dc, dr, big)
-            if pending is not None:
-                big = place(j - 1, core, pending, big)
-            pending = [hop(x, 1) for x in send]
+            big, send, dc, dr = main_chunk(j, score_scale, me0 if j == 0 else me, recv[j],
+                                           c_abs, c_t, r_abs, w_uk, w_uv, dc, dr, big,
+                                           sent[j - 2] if j >= 2 else None)
+            sent.append([hop(x, 1) for x in send])
         dc = dc.reshape(2, TB, L)
         dr = dr[0, :, :R] + dr[1, :, R:]
         dr = dr.reshape(2, TB, R)
@@ -372,7 +424,9 @@
 
         d_latent = swap_sum(dc)
         d_key_rope = swap_sum(dr)
-        d_w_uk, d_w_uv, attn_out, d_query = place(n_chunks - 1, core, pending, big)
+        for j in (n_chunks - 2, n_chunks - 1):
+            big = last_chunk(j, score_scale, core, c_t, sent[j], big)
+        d_w_uk, d_w_uv, attn_out, d_query = big
         return attn_out, d_query, d_latent, d_key_rope, d_w_uk, d_w_uv
 
     seq = P("cp")

time: 711 us -> 695 us (0.977)
  Pallas kernels: 410 us -> 399 us
  waiting for transfers between devices: 184 us -> 176 us
    pallas_call x16 -> x10, Pallas kernels: 383 us -> 373 us  [the longest x8 359 us: main_chunk(): pl.pallas_call(functools.partial(main_kernel, big is not None, prev is no...]
    ppermute x97 -> x89, waiting for transfers between devices: 184 us -> 176 us  [hop(): return lax.ppermute(x, 'cp', perm)]
    ppermute x97 -> x89, starting transfers between devices: 71.3 us -> 73.1 us  [hop(): return lax.ppermute(x, 'cp', perm)]
    unnamed x112 -> x132, local copies, waits for them, and re-layouts: 20.5 us -> 21.2 us
  transfers between devices with their start and end apart: 97 -> 89, of which waited for: 36 -> 22; matrix products, arithmetic and copies ran while one was open for 1% -> 2% of each run, Pallas kernels for 57% -> 57%
where the time goes in v1:
time: 695 us; the launch traced here: 688 us
  Pallas kernels  399 us (57%)
  waiting for transfers between devices  176 us (25%)
  starting transfers between devices  73.1 us (11%)
  local copies, waits for them, and re-layouts  34 us (5%)
    pallas_call x8, Pallas kernels, main_chunk(): pl.pallas_call(functools.partial(main_kernel, big is not None, prev is no...  359 us
    ppermute x89, waiting for transfers between devices, hop(): return lax.ppermute(x, 'cp', perm)  176 us
    ppermute x89, starting transfers between devices, hop(): return lax.ppermute(x, 'cp', perm)  73.1 us
    pallas_call x8, Pallas kernels, pack_chunk(): pl.pallas_call(pack_kernel, grid_spec=pltpu.PrefetchScalarGridSpec(num_sc...  23.5 us
    unnamed x132, local copies, waits for them, and re-layouts  21.2 us
    pallas_call x2, Pallas kernels, last_chunk(): pl.pallas_call(functools.partial(last_kernel, score_scale), grid_spec=plt...  14.1 us
  transfers between devices with their start and end apart: 89, of which 22 were waited for; matrix products, arithmetic and copies ran while one was open for 2% of the time, Pallas kernels for 57%

profile of v1, /device:TPU:0, one launch (start us, length us, event | category | flops | bytes accessed | tf_op | source)
XLA Modules:
  0.0 688.2 jit_solution(6214791628987079926)
XLA Ops:
  3.4 2.5 collective-permute-start.1
  7.7 2.6 collective-permute-start.5
  12.6 10.0 %copy.49.qo_ref.qp_ref = bf16[128,128,192]{2,1,0:T(8,128)(2,1)} copy(bf16[128,128,192]{1,2,0:T(8,128)(2,1)} %param.6) | data formatting | bytes 12582912 | tf_op jit(solution)/shard_map/optimization_barrier | solution.py:393
  22.6 2.9 pack.15
  30.5 2.9 pack.14
  33.4 9.6 %collective-permute-done.57.refs_2_ = bf16[4,5,128,128]{3,2,1,0:T(8,128)(2,1)S(1)} collective-permute-done((bf16[4,5,128,128]{3,2,1,0:T(8,128)(2,1)}, bf16[4,5,128,128]{3,2,1,0:T(8,128)(2,1)S(1)}, u32[]{:S(2)}, u32[]{:S(2)}) %collective-permute-start.57) | collective-permute-done | bytes 655392 | tf_op jit(solution)/shard_map/ppermute | solution.py:382
  46.0 11.9 %collective-permute-done.58.refs_3_ = bf16[4,5,128,128]{3,2,1,0:T(8,128)(2,1)} collective-permute-done((bf16[4,5,128,128]{3,2,1,0:T(8,128)(2,1)}, bf16[4,5,128,128]{3,2,1,0:T(8,128)(2,1)}, u32[]{:S(2)}, u32[]{:S(2)}) %collective-permute-start.58) | collective-permute-done | bytes 655392 | tf_op jit(solution)/shard_map/ppermute | solution.py:382
  59.7 3.0 pack.13
  62.7 8.5 %collective-permute-done.50.refs_2_ = bf16[4,5,128,128]{3,2,1,0:T(8,128)(2,1)} collective-permute-done((bf16[4,5,128,128]{3,2,1,0:T(8,128)(2,1)}, bf16[4,5,128,128]{3,2,1,0:T(8,128)(2,1)}, u32[]{:S(2)}, u32[]{:S(2)}) %collective-permute-start.50) | collective-permute-done | bytes 655392 | tf_op jit(solution)/shard_map/ppermute | solution.py:382
  74.2 11.8 %collective-permute-done.51.refs_3_ = bf16[4,5,128,128]{3,2,1,0:T(8,128)(2,1)S(1)} collective-permute-done((bf16[4,5,128,128]{3,2,1,0:T(8,128)(2,1)}, bf16[4,5,128,128]{3,2,1,0:T(8,128)(2,1)S(1)}, u32[]{:S(2)}, u32[]{:S(2)}) %collective-permute-start.51) | collective-permute-done | bytes 655392 | tf_op jit(solution)/shard_map/ppermute | solution.py:382
  88.4 2.9 pack.8
  91.3 2.9 pack.9
  94.2 2.9 pack.10
  97.1 2.9 pack.11
  100.1 3.0 pack.12
  103.1 3.1 prep.1
  107.9 7.1 %collective-permute-done.61.refs_6_ = bf16[4,5,128,128]{3,2,1,0:T(8,128)(2,1)} collective-permute-done((bf16[4,5,128,128]{3,2,1,0:T(8,128)(2,1)}, bf16[4,5,128,128]{3,2,1,0:T(8,128)(2,1)}, u32[]{:S(2)}, u32[]{:S(2)}) %collective-permute-start.61) | collective-permute-done | bytes 655392 | tf_op jit(solution)/shard_map/ppermute | solution.py:382
  115.0 2.0 collective-permute-start.55
  118.6 41.1 %mla_chunk.8 = (f32[512,128,128]{2,1,0:T(8,128)}, f32[512,128,128]{2,1,0:T(8,128)}, bf16[128,128,128]{2,1,0:T(8,128)(2,1)}, bf16[128,128,192]{2,1,0:T(8,128)(2,1...) custom-call(s32[1]{0:T(128)} %bitcast.me_ref, ...), custom_call_target="tpu_custom_call" | custom-call | flops 24999999488 | bytes 20000000 | tf_op jit(solution)/shard_map/mla_chunk/pallas_call | solution.py:306
  159.7 2.0 collective-permute-start.39
  162.7 41.1 %mla_chunk.9 = (f32[512,128,128]{2,1,0:T(8,128)}, f32[512,128,128]{2,1,0:T(8,128)}, bf16[128,128,128]{2,1,0:T(8,128)(2,1)}, bf16[128,128,192]{2,1,0:T(8,128)(2,1...) custom-call(s32[1]{0:T(128)} %bitcast.me_ref, ...), custom_call_target="tpu_custom_call", output_to_operand_aliasing={{0}: (16, {}), {1}: (17, {}), {2}: (18, {}), {3}: (19, {})} | custom-call | flops 24999999488 | bytes 20000000 | tf_op jit(solution)/shard_map/mla_chunk/pallas_call | solution.py:306
  205.6 2.0 collective-permute-start.32
  207.9 13.1 %collective-permute-done.29.refs_2_ = bf16[4,5,128,128]{3,2,1,0:T(8,128)(2,1)S(1)} collective-permute-done((bf16[4,5,128,128]{3,2,1,0:T(8,128)(2,1)S(1)}, bf16[4,5,128,128]{3,2,1,0:T(8,128)(2,1)S(1)}, u32[]{:S(2)}, u32[]{:S(2)}) %collective-permute-start.29) | collective-permute-done | bytes 655392 | tf_op jit(solution)/shard_map/ppermute | solution.py:382
  222.6 2.0 collective-permute-start.47
  225.2 12.8 %collective-permute-done.30.refs_3_ = bf16[4,5,128,128]{3,2,1,0:T(8,128)(2,1)S(1)} collective-permute-done((bf16[4,5,128,128]{3,2,1,0:T(8,128)(2,1)}, bf16[4,5,128,128]{3,2,1,0:T(8,128)(2,1)S(1)}, u32[]{:S(2)}, u32[]{:S(2)}) %collective-permute-start.30) | collective-permute-done | bytes 655392 | tf_op jit(solution)/shard_map/ppermute | solution.py:382
  239.9 12.4 %collective-permute-done.48.refs_7_ = bf16[4,5,128,128]{3,2,1,0:T(8,128)(2,1)S(1)} collective-permute-done((bf16[4,5,128,128]{3,2,1,0:T(8,128)(2,1)S(1)}, bf16[4,5,128,128]{3,2,1,0:T(8,128)(2,1)S(1)}, u32[]{:S(2)}, u32[]{:S(2)}) %collective-permute-start.48) | collective-permute-done | bytes 655392 | tf_op jit(solution)/shard_map/ppermute | solution.py:382
  252.3 2.4 collective-permute-start.40
  256.5 46.0 %mla_chunk.10 = (f32[512,128,128]{2,1,0:T(8,128)}, f32[512,128,128]{2,1,0:T(8,128)}, bf16[128,128,128]{2,1,0:T(8,128)(2,1)}, bf16[128,128,192]{2,1,0:T(8,128)(2,...) custom-call(s32[1]{0:T(128)} %bitcast.me_ref, ...), custom_call_target="tpu_custom_call", output_to_operand_aliasing={{0}: (19, {}), {1}: (20, {}), {2}: (21, {}), {3}: (22, {})} | custom-call | flops 24999999488 | bytes 20000000 | tf_op jit(solution)/shard_map/mla_chunk/pallas_call | solution.py:306
  306.1 46.3 %mla_chunk.11 = (f32[512,128,128]{2,1,0:T(8,128)}, f32[512,128,128]{2,1,0:T(8,128)}, bf16[128,128,128]{2,1,0:T(8,128)(2,1)}, bf16[128,128,192]{2,1,0:T(8,128)(2,...) custom-call(s32[1]{0:T(128)} %bitcast.me_ref, ...), custom_call_target="tpu_custom_call", output_to_operand_aliasing={{0}: (19, {}), {1}: (20, {}), {2}: (21, {}), {3}: (22, {})} | custom-call | flops 24999999488 | bytes 20000000 | tf_op jit(solution)/shard_map/mla_chunk/pallas_call | solution.py:306
  355.6 13.5 %collective-permute-done.23.refs_3_ = bf16[4,5,128,128]{3,2,1,0:T(8,128)(2,1)S(1)} collective-permute-done((bf16[4,5,128,128]{3,2,1,0:T(8,128)(2,1)}, bf16[4,5,128,128]{3,2,1,0:T(8,128)(2,1)S(1)}, u32[]{:S(2)}, u32[]{:S(2)}) %collective-permute-start.23) | collective-permute-done | bytes 655392 | tf_op jit(solution)/shard_map/ppermute | solution.py:382
  369.9 1.8 collective-permute-start.18
  372.9 10.9 %collective-permute-done.15.refs_2_ = bf16[4,5,128,128]{3,2,1,0:T(8,128)(2,1)S(1)} collective-permute-done((bf16[4,5,128,128]{3,2,1,0:T(8,128)(2,1)S(1)}, bf16[4,5,128,128]{3,2,1,0:T(8,128)(2,1)S(1)}, u32[]{:S(2)}, u32[]{:S(2)}) %collective-permute-start.15) | collective-permute-done | bytes 655392 | tf_op jit(solution)/shard_map/ppermute | solution.py:382
  384.8 2.4 collective-permute-done.18.refs_5_
  388.8 12.5 %collective-permute-done.33.refs_6_ = bf16[4,5,128,128]{3,2,1,0:T(8,128)(2,1)S(1)} collective-permute-done((bf16[4,5,128,128]{3,2,1,0:T(8,128)(2,1)S(1)}, bf16[4,5,128,128]{3,2,1,0:T(8,128)(2,1)S(1)}, u32[]{:S(2)}, u32[]{:S(2)}) %collective-permute-start.33) | collective-permute-done | bytes 655392 | tf_op jit(solution)/shard_map/ppermute | solution.py:382
  405.0 45.9 %mla_chunk.12 = (f32[512,128,128]{2,1,0:T(8,128)}, f32[512,128,128]{2,1,0:T(8,128)}, bf16[128,128,128]{2,1,0:T(8,128)(2,1)}, bf16[128,128,192]{2,1,0:T(8,128)(2,...) custom-call(s32[1]{0:T(128)} %bitcast.me_ref, ...), custom_call_target="tpu_custom_call", output_to_operand_aliasing={{0}: (19, {}), {1}: (20, {}), {2}: (21, {}), {3}: (22, {})} | custom-call | flops 24999999488 | bytes 20000000 | tf_op jit(solution)/shard_map/mla_chunk/pallas_call | solution.py:306
  454.6 46.0 %mla_chunk.13 = (f32[512,128,128]{2,1,0:T(8,128)}, f32[512,128,128]{2,1,0:T(8,128)}, bf16[128,128,128]{2,1,0:T(8,128)(2,1)}, bf16[128,128,192]{2,1,0:T(8,128)(2,...) custom-call(s32[1]{0:T(128)} %bitcast.me_ref, ...), custom_call_target="tpu_custom_call", output_to_operand_aliasing={{0}: (19, {}), {1}: (20, {}), {2}: (21, {}), {3}: (22, {})} | custom-call | flops 24999999488 | bytes 20000000 | tf_op jit(solution)/shard_map/mla_chunk/pallas_call | solution.py:306
  502.8 14.6 %collective-permute-done.11.refs_5_ = bf16[4,5,128,128]{3,2,1,0:T(8,128)(2,1)} collective-permute-done((bf16[4,5,128,128]{3,2,1,0:T(8,128)(2,1)}, bf16[4,5,128,128]{3,2,1,0:T(8,128)(2,1)}, u32[]{:S(2)}, u32[]{:S(2)}) %collective-permute-start.11) | collective-permute-done | bytes 655392 | tf_op jit(solution)/shard_map/ppermute | solution.py:382
  517.4 2.3 collective-permute-start.9
  519.6 12.3 %collective-permute-done.10.refs_4_ = bf16[4,5,128,128]{3,2,1,0:T(8,128)(2,1)S(1)} collective-permute-done((bf16[4,5,128,128]{3,2,1,0:T(8,128)(2,1)S(1)}, bf16[4,5,128,128]{3,2,1,0:T(8,128)(2,1)S(1)}, u32[]{:S(2)}, u32[]{:S(2)}) %collective-permute-start.10) | collective-permute-done | bytes 655392 | tf_op jit(solution)/shard_map/ppermute | solution.py:382
  535.3 12.8 %collective-permute-done.19.refs_6_ = bf16[4,5,128,128]{3,2,1,0:T(8,128)(2,1)S(1)} collective-permute-done((bf16[4,5,128,128]{3,2,1,0:T(8,128)(2,1)S(1)}, bf16[4,5,128,128]{3,2,1,0:T(8,128)(2,1)S(1)}, u32[]{:S(2)}, u32[]{:S(2)}) %collective-permute-start.19) | collective-permute-done | bytes 655392 | tf_op jit(solution)/shard_map/ppermute | solution.py:382
  552.0 46.0 %mla_chunk.14 = (f32[512,128,128]{2,1,0:T(8,128)}, f32[512,128,128]{2,1,0:T(8,128)}, bf16[128,128,128]{2,1,0:T(8,128)(2,1)}, bf16[128,128,192]{2,1,0:T(8,128)(2,...) custom-call(s32[1]{0:T(128)} %bitcast.me_ref, ...), custom_call_target="tpu_custom_call", output_to_operand_aliasing={{0}: (19, {}), {1}: (20, {}), {2}: (21, {}), {3}: (22, {})} | custom-call | flops 24999999488 | bytes 20000000 | tf_op jit(solution)/shard_map/mla_chunk/pallas_call | solution.py:306
  599.3 46.2 %mla_chunk.15 = (f32[512,128,128]{2,1,0:T(8,128)}, f32[512,128,128]{2,1,0:T(8,128)}, bf16[128,128,128]{2,1,0:T(8,128)(2,1)}, bf16[128,128,192]{2,1,0:T(8,128)(2,...) custom-call(s32[1]{0:T(128)} %bitcast.me_ref, ...), custom_call_target="tpu_custom_call", output_to_operand_aliasing={{0}: (19, {}), {1}: (20, {}), {2}: (21, {}), {3}: (22, {})} | custom-call | flops 24999999488 | bytes 20000000 | tf_op jit(solution)/shard_map/mla_chunk/pallas_call | solution.py:306
  648.7 4.9 collective-permute-done.88
  656.7 3.4 copy-done
  660.1 7.0 %last.2 = (f32[512,128,128]{2,1,0:T(8,128)}, f32[512,128,128]{2,1,0:T(8,128)}, bf16[128,128,128]{2,1,0:T(8,128)(2,1)}, bf16[128,128,192]{2,1,0:T(8,128)(2,1)S(1)}) custom-call(s32[1]{0:T(128)} %select_n.17.core_ref, bf16[512,1024]{1,0:T(8,128)(2,1)S(1)} %copy-done.2, ...), custom_call_target="tpu_custom_call", output_to_operand_aliasing={{0}: (5, {}), {1}: (6, {}), {2}: (7, {}), {3}: (8, {})} | custom-call | flops 2000000000 | bytes 10000000 | tf_op jit(solution)/shard_map/last/pallas_call | solution.py:361
  667.2 7.1 %last.3 = (f32[512,128,128]{2,1,0:T(8,128)}, f32[512,128,128]{2,1,0:T(8,128)}, bf16[128,128,128]{2,1,0:T(8,128)(2,1)}, bf16[128,128,192]{2,1,0:T(8,128)(2,1)S(1)}) custom-call(s32[1]{0:T(128)} %select_n.17.core_ref, bf16[512,1024]{1,0:T(8,128)(2,1)S(1)} %copy-done.2, ...), custom_call_target="tpu_custom_call", output_to_operand_aliasing={{0}: (5, {}), {1}: (6, {}), {2}: (7, {}), {3}: (8, {})} | custom-call | flops 2000000000 | bytes 10000000 | tf_op jit(solution)/shard_map/last/pallas_call | solution.py:361
  674.2 3.4 copy-done.1
  677.6 10.1 %copy.67 = bf16[128,128,192]{1,2,0:T(8,128)(2,1)} copy(bf16[128,128,192]{2,1,0:T(8,128)(2,1)} %copy-done.1) | data formatting | bytes 12582912
  (294 shorter events, 69.9 us)
Async XLA Ops:
  28.2 29.8 %collective-permute-start.58 = (bf16[4,5,128,128]{3,2,1,0:T(8,128)(2,1)}, bf16[4,5,128,128]{3,2,1,0:T(8,128)(2,1)}, u32[]{:S(2)}, u32[]{:S(2)}) collective-permute-start(bf16[4,5,128,128]{3,2,1,0:T(8,128)(2,1)} %get-tuple-element.129), channel_id=1, source_target_pairs={{0,3},{1,2},{2,1},{3,0},{4,7},{5,6},{6,5},{7,4}} | collective-permute-start | bytes 1966088 | tf_op jit(solution)/shard_map/ppermute | solution.py:382
  28.9 29.7 %collective-permute-start.59 = (bf16[4,5,128,128]{3,2,1,0:T(8,128)(2,1)}, bf16[4,5,128,128]{3,2,1,0:T(8,128)(2,1)S(1)}, u32[]{:S(2)}, u32[]{:S(2)}) collective-permute-start(bf16[4,5,128,128]{3,2,1,0:T(8,128)(2,1)} %get-tuple-element.127.refs_0_), channel_id=1, source_target_pairs={{0,4},{1,5},{2,6},{3,7},{4,0},{5,1},{6,2},{7,3}} | collective-permute-start | bytes 1966088 | tf_op jit(solution)/shard_map/ppermute | solution.py:382
  43.0 28.2 %collective-permute-start.50 = (bf16[4,5,128,128]{3,2,1,0:T(8,128)(2,1)}, bf16[4,5,128,128]{3,2,1,0:T(8,128)(2,1)}, u32[]{:S(2)}, u32[]{:S(2)}) collective-permute-start(bf16[4,5,128,128]{3,2,1,0:T(8,128)(2,1)} %get-tuple-element.125.refs_0_), channel_id=1, source_target_pairs={{0,2},{1,3},{2,0},{3,1},{4,6},{5,7},{6,4},{7,5}} | collective-permute-start | bytes 1966088 | tf_op jit(solution)/shard_map/ppermute | solution.py:382
  58.7 28.2 %collective-permute-start.52 = (bf16[4,5,128,128]{3,2,1,0:T(8,128)(2,1)}, bf16[4,5,128,128]{3,2,1,0:T(8,128)(2,1)}, u32[]{:S(2)}, u32[]{:S(2)}) collective-permute-start(bf16[4,5,128,128]{3,2,1,0:T(8,128)(2,1)} %get-tuple-element.125.refs_0_), channel_id=1, source_target_pairs={{0,4},{1,5},{2,6},{3,7},{4,0},{5,1},{6,2},{7,3}} | collective-permute-start | bytes 1966088 | tf_op jit(solution)/shard_map/ppermute | solution.py:382
  71.1 35.0 %collective-permute-start.43 = (bf16[4,5,128,128]{3,2,1,0:T(8,128)(2,1)}, bf16[4,5,128,128]{3,2,1,0:T(8,128)(2,1)S(1)}, u32[]{:S(2)}, u32[]{:S(2)}) collective-permute-start(bf16[4,5,128,128]{3,2,1,0:T(8,128)(2,1)} %get-tuple-element.123.refs_0_), channel_id=1, source_target_pairs={{0,2},{1,3},{2,0},{3,1},{4,6},{5,7},{6,4},{7,5}} | collective-permute-start | bytes 1966088 | tf_op jit(solution)/shard_map/ppermute | solution.py:382
  72.5 33.7 %collective-permute-start.46 = (bf16[4,5,128,128]{3,2,1,0:T(8,128)(2,1)}, bf16[4,5,128,128]{3,2,1,0:T(8,128)(2,1)S(1)}, u32[]{:S(2)}, u32[]{:S(2)}) collective-permute-start(bf16[4,5,128,128]{3,2,1,0:T(8,128)(2,1)} %get-tuple-element.124), channel_id=1, source_target_pairs={{0,5},{1,4},{2,7},{3,6},{4,1},{5,0},{6,3},{7,2}} | collective-permute-start | bytes 1966088 | tf_op jit(solution)/shard_map/ppermute | solution.py:382
  72.6 34.2 %collective-permute-start.42 = (bf16[4,5,128,128]{3,2,1,0:T(8,128)(2,1)}, bf16[4,5,128,128]{3,2,1,0:T(8,128)(2,1)S(1)}, u32[]{:S(2)}, u32[]{:S(2)}) collective-permute-start(bf16[4,5,128,128]{3,2,1,0:T(8,128)(2,1)} %get-tuple-element.124), channel_id=1, source_target_pairs={{0,1},{1,0},{2,3},{3,2},{4,5},{5,4},{6,7},{7,6}} | collective-permute-start | bytes 1966088 | tf_op jit(solution)/shard_map/ppermute | solution.py:382
  85.9 29.0 %collective-permute-start.61 = (bf16[4,5,128,128]{3,2,1,0:T(8,128)(2,1)}, bf16[4,5,128,128]{3,2,1,0:T(8,128)(2,1)}, u32[]{:S(2)}, u32[]{:S(2)}) collective-permute-start(bf16[4,5,128,128]{3,2,1,0:T(8,128)(2,1)} %copy-done.58), channel_id=1, source_target_pairs={{0,4},{1,5},{2,6},{3,7},{4,0},{5,1},{6,2},{7,3}} | collective-permute-start | bytes 1966088 | tf_op jit(solution)/shard_map/ppermute | solution.py:382
  106.2 53.5 %collective-permute-start.44 = (bf16[4,5,128,128]{3,2,1,0:T(8,128)(2,1)}, bf16[4,5,128,128]{3,2,1,0:T(8,128)(2,1)}, u32[]{:S(2)}, u32[]{:S(2)}) collective-permute-start(bf16[4,5,128,128]{3,2,1,0:T(8,128)(2,1)} %get-tuple-element.124), channel_id=1, source_target_pairs={{0,3},{1,2},{2,1},{3,0},{4,7},{5,6},{6,5},{7,4}} | collective-permute-start | bytes 1966088 | tf_op jit(solution)/shard_map/ppermute | solution.py:382
  106.2 53.5 %collective-permute-start.45 = (bf16[4,5,128,128]{3,2,1,0:T(8,128)(2,1)S(1)}, bf16[4,5,128,128]{3,2,1,0:T(8,128)(2,1)}, u32[]{:S(2)}, u32[]{:S(2)}) collective-permute-start(bf16[4,5,128,128]{3,2,1,0:T(8,128)(2,1)S(1)} %copy-done.8), channel_id=1, source_target_pairs={{0,4},{1,5},{2,6},{3,7},{4,0},{5,1},{6,2},{7,3}} | collective-permute-start | bytes 1966088 | tf_op jit(solution)/shard_map/ppermute | solution.py:382
  106.8 55.0 %collective-permute-start.36 = (bf16[4,5,128,128]{3,2,1,0:T(8,128)(2,1)}, bf16[4,5,128,128]{3,2,1,0:T(8,128)(2,1)}, u32[]{:S(2)}, u32[]{:S(2)}) collective-permute-start(bf16[4,5,128,128]{3,2,1,0:T(8,128)(2,1)} %get-tuple-element.121.refs_0_), channel_id=1, source_target_pairs={{0,2},{1,3},{2,0},{3,1},{4,6},{5,7},{6,4},{7,5}} | collective-permute-start | bytes 1966088 | tf_op jit(solution)/shard_map/ppermute | solution.py:382
  115.0 46.8 %collective-permute-start.54 = (bf16[4,5,128,128]{3,2,1,0:T(8,128)(2,1)}, bf16[4,5,128,128]{3,2,1,0:T(8,128)(2,1)}, u32[]{:S(2)}, u32[]{:S(2)}) collective-permute-start(bf16[4,5,128,128]{3,2,1,0:T(8,128)(2,1)} %collective-permute-done.50.refs_2_), channel_id=1, source_target_pairs={{0,4},{1,5},{2,6},{3,7},{4,0},{5,1},{6,2},{7,3}} | collective-permute-start | bytes 1966088 | tf_op jit(solution)/shard_map/ppermute | solution.py:382
  115.0 47.7 %collective-permute-start.55 = (bf16[4,5,128,128]{3,2,1,0:T(8,128)(2,1)}, bf16[4,5,128,128]{3,2,1,0:T(8,128)(2,1)}, u32[]{:S(2)}, u32[]{:S(2)}) collective-permute-start(bf16[4,5,128,128]{3,2,1,0:T(8,128)(2,1)} %collective-permute-done.53.refs_5_), channel_id=1, source_target_pairs={{0,2},{1,3},{2,0},{3,1},{4,6},{5,7},{6,4},{7,5}} | collective-permute-start | bytes 1966088 | tf_op jit(solution)/shard_map/ppermute | solution.py:382
  159.7 96.0 %collective-permute-start.63 = (bf16[4,2,1024,256]{3,2,1,0:T(8,128)(2,1)}, bf16[4,2,1024,256]{3,2,1,0:T(8,128)(2,1)}, u32[]{:S(2)}, u32[]{:S(2)}) collective-permute-start(bf16[4,2,1024,256]{3,2,1,0:T(8,128)(2,1)} %get-tuple-element.138), channel_id=1, source_target_pairs={{0,1},{1,0},{2,3},{3,2},{4,5},{5,4},{6,7},{7,6}} | collective-permute-start | bytes 12582920 | tf_op jit(solution)/shard_map/ppermute | solution.py:382
  159.7 44.1 %collective-permute-start.39 = (bf16[4,5,128,128]{3,2,1,0:T(8,128)(2,1)}, bf16[4,5,128,128]{3,2,1,0:T(8,128)(2,1)}, u32[]{:S(2)}, u32[]{:S(2)}) collective-permute-start(bf16[4,5,128,128]{3,2,1,0:T(8,128)(2,1)} %get-tuple-element.122), channel_id=1, source_target_pairs={{0,5},{1,4},{2,7},{3,6},{4,1},{5,0},{6,3},{7,2}} | collective-permute-start | bytes 1966088 | tf_op jit(solution)/shard_map/ppermute | solution.py:382
  161.7 42.2 %collective-permute-start.35 = (bf16[4,5,128,128]{3,2,1,0:T(8,128)(2,1)}, bf16[4,5,128,128]{3,2,1,0:T(8,128)(2,1)}, u32[]{:S(2)}, u32[]{:S(2)}) collective-permute-start(bf16[4,5,128,128]{3,2,1,0:T(8,128)(2,1)} %get-tuple-element.122), channel_id=1, source_target_pairs={{0,1},{1,0},{2,3},{3,2},{4,5},{5,4},{6,7},{7,6}} | collective-permute-start | bytes 1966088 | tf_op jit(solution)/shard_map/ppermute | solution.py:382
  161.8 43.8 %collective-permute-start.37 = (bf16[4,5,128,128]{3,2,1,0:T(8,128)(2,1)}, bf16[4,5,128,128]{3,2,1,0:T(8,128)(2,1)}, u32[]{:S(2)}, u32[]{:S(2)}) collective-permute-start(bf16[4,5,128,128]{3,2,1,0:T(8,128)(2,1)} %get-tuple-element.122), channel_id=1, source_target_pairs={{0,3},{1,2},{2,1},{3,0},{4,7},{5,6},{6,5},{7,4}} | collective-permute-start | bytes 1966088 | tf_op jit(solution)/shard_map/ppermute | solution.py:382
  162.6 44.9 %collective-permute-start.38 = (bf16[4,5,128,128]{3,2,1,0:T(8,128)(2,1)S(1)}, bf16[4,5,128,128]{3,2,1,0:T(8,128)(2,1)}, u32[]{:S(2)}, u32[]{:S(2)}) collective-permute-start(bf16[4,5,128,128]{3,2,1,0:T(8,128)(2,1)S(1)} %copy-done.7), channel_id=1, source_target_pairs={{0,4},{1,5},{2,6},{3,7},{4,0},{5,1},{6,2},{7,3}} | collective-permute-start | bytes 1966088 | tf_op jit(solution)/shard_map/ppermute | solution.py:382
  203.8 101.7 %collective-permute-start.66 = (bf16[4,2,1024,256]{3,2,1,0:T(8,128)(2,1)}, bf16[4,2,1024,256]{3,2,1,0:T(8,128)(2,1)}, u32[]{:S(2)}, u32[]{:S(2)}) collective-permute-start(bf16[4,2,1024,256]{3,2,1,0:T(8,128)(2,1)} %get-tuple-element.147), channel_id=1, source_target_pairs={{0,1},{1,0},{2,3},{3,2},{4,5},{5,4},{6,7},{7,6}} | collective-permute-start | bytes 12582920 | tf_op jit(solution)/shard_map/ppermute | solution.py:382
  252.3 50.2 %collective-permute-start.40 = (bf16[4,5,128,128]{3,2,1,0:T(8,128)(2,1)}, bf16[4,5,128,128]{3,2,1,0:T(8,128)(2,1)S(1)}, u32[]{:S(2)}, u32[]{:S(2)}) collective-permute-start(bf16[4,5,128,128]{3,2,1,0:T(8,128)(2,1)} %collective-permute-done.36.refs_2_), channel_id=1, source_target_pairs={{0,4},{1,5},{2,6},{3,7},{4,0},{5,1},{6,2},{7,3}} | collective-permute-start | bytes 1966088 | tf_op jit(solution)/shard_map/ppermute | solution.py:382
  254.7 47.9 %collective-permute-start.41 = (bf16[4,5,128,128]{3,2,1,0:T(8,128)(2,1)}, bf16[4,5,128,128]{3,2,1,0:T(8,128)(2,1)S(1)}, u32[]{:S(2)}, u32[]{:S(2)}) collective-permute-start(bf16[4,5,128,128]{3,2,1,0:T(8,128)(2,1)} %collective-permute-done.39.refs_5_), channel_id=1, source_target_pairs={{0,2},{1,3},{2,0},{3,1},{4,6},{5,7},{6,4},{7,5}} | collective-permute-start | bytes 1966088 | tf_op jit(solution)/shard_map/ppermute | solution.py:382
  255.7 48.6 %collective-permute-start.68 = (bf16[128,8,192]{2,1,0:T(8,128)(2,1)}, bf16[128,8,192]{2,1,0:T(8,128)(2,1)S(1)}, u32[]{:S(2)}, u32[]{:S(2)}) collective-permute-start(bf16[128,8,192]{2,1,0:T(8,128)(2,1)} %get-tuple-element.149), channel_id=1, source_target_pairs={{0,1},{1,0},{2,3},{3,2},{4,5},{5,4},{6,7},{7,6}} | collective-permute-start | bytes 1179656 | tf_op jit(solution)/shard_map/ppermute | solution.py:382
  255.7 47.3 %collective-permute-start.67 = (bf16[128,8,128]{2,1,0:T(8,128)(2,1)}, bf16[128,8,128]{2,1,0:T(8,128)(2,1)S(1)}, u32[]{:S(2)}, u32[]{:S(2)}) collective-permute-start(bf16[128,8,128]{2,1,0:T(8,128)(2,1)} %get-tuple-element.148), channel_id=1, source_target_pairs={{0,1},{1,0},{2,3},{3,2},{4,5},{5,4},{6,7},{7,6}} | collective-permute-start | bytes 786440 | tf_op jit(solution)/shard_map/ppermute | solution.py:382
  302.5 101.8 %collective-permute-start.69 = (bf16[4,2,1024,256]{3,2,1,0:T(8,128)(2,1)}, bf16[4,2,1024,256]{3,2,1,0:T(8,128)(2,1)}, u32[]{:S(2)}, u32[]{:S(2)}) collective-permute-start(bf16[4,2,1024,256]{3,2,1,0:T(8,128)(2,1)} %get-tuple-element.156), channel_id=1, source_target_pairs={{0,1},{1,0},{2,3},{3,2},{4,5},{5,4},{6,7},{7,6}} | collective-permute-start | bytes 12582920 | tf_op jit(solution)/shard_map/ppermute | solution.py:382
  302.6 49.9 %collective-permute-start.31 = (bf16[4,5,128,128]{3,2,1,0:T(8,128)(2,1)S(1)}, bf16[4,5,128,128]{3,2,1,0:T(8,128)(2,1)}, u32[]{:S(2)}, u32[]{:S(2)}) collective-permute-start(bf16[4,5,128,128]{3,2,1,0:T(8,128)(2,1)S(1)} %copy-done.6), channel_id=1, source_target_pairs={{0,4},{1,5},{2,6},{3,7},{4,0},{5,1},{6,2},{7,3}} | collective-permute-start | bytes 1966088 | tf_op jit(solution)/shard_map/ppermute | solution.py:382
  303.0 49.5 %collective-permute-start.22 = (bf16[4,5,128,128]{3,2,1,0:T(8,128)(2,1)S(1)}, bf16[4,5,128,128]{3,2,1,0:T(8,128)(2,1)}, u32[]{:S(2)}, u32[]{:S(2)}) collective-permute-start(bf16[4,5,128,128]{3,2,1,0:T(8,128)(2,1)S(1)} %copy-done.5), channel_id=1, source_target_pairs={{0,2},{1,3},{2,0},{3,1},{4,6},{5,7},{6,4},{7,5}} | collective-permute-start | bytes 1966088 | tf_op jit(solution)/shard_map/ppermute | solution.py:382
  304.3 49.3 %collective-permute-start.25 = (bf16[4,5,128,128]{3,2,1,0:T(8,128)(2,1)}, bf16[4,5,128,128]{3,2,1,0:T(8,128)(2,1)}, u32[]{:S(2)}, u32[]{:S(2)}) collective-permute-start(bf16[4,5,128,128]{3,2,1,0:T(8,128)(2,1)} %get-tuple-element.118), channel_id=1, source_target_pairs={{0,5},{1,4},{2,7},{3,6},{4,1},{5,0},{6,3},{7,2}} | collective-permute-start | bytes 1966088 | tf_op jit(solution)/shard_map/ppermute | solution.py:382
  305.5 49.0 %collective-permute-start.21 = (bf16[4,5,128,128]{3,2,1,0:T(8,128)(2,1)}, bf16[4,5,128,128]{3,2,1,0:T(8,128)(2,1)}, u32[]{:S(2)}, u32[]{:S(2)}) collective-permute-start(bf16[4,5,128,128]{3,2,1,0:T(8,128)(2,1)} %get-tuple-element.118), channel_id=1, source_target_pairs={{0,1},{1,0},{2,3},{3,2},{4,5},{5,4},{6,7},{7,6}} | collective-permute-start | bytes 1966088 | tf_op jit(solution)/shard_map/ppermute | solution.py:382
  352.4 101.3 %collective-permute-start.72 = (bf16[4,2,1024,256]{3,2,1,0:T(8,128)(2,1)}, bf16[4,2,1024,256]{3,2,1,0:T(8,128)(2,1)}, u32[]{:S(2)}, u32[]{:S(2)}) collective-permute-start(bf16[4,2,1024,256]{3,2,1,0:T(8,128)(2,1)} %get-tuple-element.165), channel_id=1, source_target_pairs={{0,1},{1,0},{2,3},{3,2},{4,5},{5,4},{6,7},{7,6}} | collective-permute-start | bytes 12582920 | tf_op jit(solution)/shard_map/ppermute | solution.py:382
  354.5 29.3 %collective-permute-start.15 = (bf16[4,5,128,128]{3,2,1,0:T(8,128)(2,1)S(1)}, bf16[4,5,128,128]{3,2,1,0:T(8,128)(2,1)S(1)}, u32[]{:S(2)}, u32[]{:S(2)}) collective-permute-start(bf16[4,5,128,128]{3,2,1,0:T(8,128)(2,1)S(1)} %copy-done.4), channel_id=1, source_target_pairs={{0,2},{1,3},{2,0},{3,1},{4,6},{5,7},{6,4},{7,5}} | collective-permute-start | bytes 1966088 | tf_op jit(solution)/shard_map/ppermute | solution.py:382
  371.7 29.5 %collective-permute-start.33 = (bf16[4,5,128,128]{3,2,1,0:T(8,128)(2,1)S(1)}, bf16[4,5,128,128]{3,2,1,0:T(8,128)(2,1)S(1)}, u32[]{:S(2)}, u32[]{:S(2)}) collective-permute-start(bf16[4,5,128,128]{3,2,1,0:T(8,128)(2,1)S(1)} %collective-permute-done.29.refs_2_), channel_id=1, source_target_pairs={{0,4},{1,5},{2,6},{3,7},{4,0},{5,1},{6,2},{7,3}} | collective-permute-start | bytes 1966088 | tf_op jit(solution)/shard_map/ppermute | solution.py:382
  402.1 48.8 %collective-permute-start.26 = (bf16[4,5,128,128]{3,2,1,0:T(8,128)(2,1)}, bf16[4,5,128,128]{3,2,1,0:T(8,128)(2,1)S(1)}, u32[]{:S(2)}, u32[]{:S(2)}) collective-permute-start(bf16[4,5,128,128]{3,2,1,0:T(8,128)(2,1)} %collective-permute-done.22.refs_2_), channel_id=1, source_target_pairs={{0,4},{1,5},{2,6},{3,7},{4,0},{5,1},{6,2},{7,3}} | collective-permute-start | bytes 1966088 | tf_op jit(solution)/shard_map/ppermute | solution.py:382
  403.2 47.8 %collective-permute-start.27 = (bf16[4,5,128,128]{3,2,1,0:T(8,128)(2,1)}, bf16[4,5,128,128]{3,2,1,0:T(8,128)(2,1)S(1)}, u32[]{:S(2)}, u32[]{:S(2)}) collective-permute-start(bf16[4,5,128,128]{3,2,1,0:T(8,128)(2,1)} %collective-permute-done.25.refs_5_), channel_id=1, source_target_pairs={{0,2},{1,3},{2,0},{3,1},{4,6},{5,7},{6,4},{7,5}} | collective-permute-start | bytes 1966088 | tf_op jit(solution)/shard_map/ppermute | solution.py:382
  404.3 48.3 %collective-permute-start.74 = (bf16[128,8,192]{2,1,0:T(8,128)(2,1)}, bf16[128,8,192]{2,1,0:T(8,128)(2,1)S(1)}, u32[]{:S(2)}, u32[]{:S(2)}) collective-permute-start(bf16[128,8,192]{2,1,0:T(8,128)(2,1)} %get-tuple-element.167), channel_id=1, source_target_pairs={{0,1},{1,0},{2,3},{3,2},{4,5},{5,4},{6,7},{7,6}} | collective-permute-start | bytes 1179656 | tf_op jit(solution)/shard_map/ppermute | solution.py:382
  404.3 47.2 %collective-permute-start.73 = (bf16[128,8,128]{2,1,0:T(8,128)(2,1)}, bf16[128,8,128]{2,1,0:T(8,128)(2,1)S(1)}, u32[]{:S(2)}, u32[]{:S(2)}) collective-permute-start(bf16[128,8,128]{2,1,0:T(8,128)(2,1)} %get-tuple-element.166), channel_id=1, source_target_pairs={{0,1},{1,0},{2,3},{3,2},{4,5},{5,4},{6,7},{7,6}} | collective-permute-start | bytes 786440 | tf_op jit(solution)/shard_map/ppermute | solution.py:382
  451.0 49.6 %collective-permute-start.14 = (bf16[4,5,128,128]{3,2,1,0:T(8,128)(2,1)}, bf16[4,5,128,128]{3,2,1,0:T(8,128)(2,1)}, u32[]{:S(2)}, u32[]{:S(2)}) collective-permute-start(bf16[4,5,128,128]{3,2,1,0:T(8,128)(2,1)} %get-tuple-element.116), channel_id=1, source_target_pairs={{0,1},{1,0},{2,3},{3,2},{4,5},{5,4},{6,7},{7,6}} | collective-permute-start | bytes 1966088 | tf_op jit(solution)/shard_map/ppermute | solution.py:382
  451.0 100.4 %collective-permute-start.75 = (bf16[4,2,1024,256]{3,2,1,0:T(8,128)(2,1)}, bf16[4,2,1024,256]{3,2,1,0:T(8,128)(2,1)}, u32[]{:S(2)}, u32[]{:S(2)}) collective-permute-start(bf16[4,2,1024,256]{3,2,1,0:T(8,128)(2,1)} %get-tuple-element.174), channel_id=1, source_target_pairs={{0,1},{1,0},{2,3},{3,2},{4,5},{5,4},{6,7},{7,6}} | collective-permute-start | bytes 12582920 | tf_op jit(solution)/shard_map/ppermute | solution.py:382
  451.5 49.1 %collective-permute-start.16 = (bf16[4,5,128,128]{3,2,1,0:T(8,128)(2,1)}, bf16[4,5,128,128]{3,2,1,0:T(8,128)(2,1)}, u32[]{:S(2)}, u32[]{:S(2)}) collective-permute-start(bf16[4,5,128,128]{3,2,1,0:T(8,128)(2,1)} %get-tuple-element.116), channel_id=1, source_target_pairs={{0,3},{1,2},{2,1},{3,0},{4,7},{5,6},{6,5},{7,4}} | collective-permute-start | bytes 1966088 | tf_op jit(solution)/shard_map/ppermute | solution.py:382
  452.5 49.3 %collective-permute-start.17 = (bf16[4,5,128,128]{3,2,1,0:T(8,128)(2,1)S(1)}, bf16[4,5,128,128]{3,2,1,0:T(8,128)(2,1)}, u32[]{:S(2)}, u32[]{:S(2)}) collective-permute-start(bf16[4,5,128,128]{3,2,1,0:T(8,128)(2,1)S(1)} %copy-done.4), channel_id=1, source_target_pairs={{0,4},{1,5},{2,6},{3,7},{4,0},{5,1},{6,2},{7,3}} | collective-permute-start | bytes 1966088 | tf_op jit(solution)/shard_map/ppermute | solution.py:382
  453.8 49.0 %collective-permute-start.8 = (bf16[4,5,128,128]{3,2,1,0:T(8,128)(2,1)S(1)}, bf16[4,5,128,128]{3,2,1,0:T(8,128)(2,1)S(1)}, u32[]{:S(2)}, u32[]{:S(2)}) collective-permute-start(bf16[4,5,128,128]{3,2,1,0:T(8,128)(2,1)S(1)} %copy-done.3), channel_id=1, source_target_pairs={{0,2},{1,3},{2,0},{3,1},{4,6},{5,7},{6,4},{7,5}} | collective-permute-start | bytes 1966088 | tf_op jit(solution)/shard_map/ppermute | solution.py:382
  500.6 97.5 %collective-permute-start.78 = (bf16[4,2,1024,256]{3,2,1,0:T(8,128)(2,1)}, bf16[4,2,1024,256]{3,2,1,0:T(8,128)(2,1)}, u32[]{:S(2)}, u32[]{:S(2)}) collective-permute-start(bf16[4,2,1024,256]{3,2,1,0:T(8,128)(2,1)} %get-tuple-element.183), channel_id=1, source_target_pairs={{0,1},{1,0},{2,3},{3,2},{4,5},{5,4},{6,7},{7,6}} | collective-permute-start | bytes 12582920 | tf_op jit(solution)/shard_map/ppermute | solution.py:382
  501.8 30.2 %collective-permute-start.10 = (bf16[4,5,128,128]{3,2,1,0:T(8,128)(2,1)S(1)}, bf16[4,5,128,128]{3,2,1,0:T(8,128)(2,1)S(1)}, u32[]{:S(2)}, u32[]{:S(2)}) collective-permute-start(bf16[4,5,128,128]{3,2,1,0:T(8,128)(2,1)S(1)} %copy-done.3), channel_id=1, source_target_pairs={{0,4},{1,5},{2,6},{3,7},{4,0},{5,1},{6,2},{7,3}} | collective-permute-start | bytes 1966088 | tf_op jit(solution)/shard_map/ppermute | solution.py:382
  502.8 30.2 %collective-permute-start.7 = (bf16[4,5,128,128]{3,2,1,0:T(8,128)(2,1)}, bf16[4,5,128,128]{3,2,1,0:T(8,128)(2,1)S(1)}, u32[]{:S(2)}, u32[]{:S(2)}) collective-permute-start(bf16[4,5,128,128]{3,2,1,0:T(8,128)(2,1)} %get-tuple-element.112), channel_id=1, source_target_pairs={{0,1},{1,0},{2,3},{3,2},{4,5},{5,4},{6,7},{7,6}} | collective-permute-start | bytes 1966088 | tf_op jit(solution)/shard_map/ppermute | solution.py:382
  549.2 48.8 %collective-permute-start.12 = (bf16[4,5,128,128]{3,2,1,0:T(8,128)(2,1)S(1)}, bf16[4,5,128,128]{3,2,1,0:T(8,128)(2,1)S(1)}, u32[]{:S(2)}, u32[]{:S(2)}) collective-permute-start(bf16[4,5,128,128]{3,2,1,0:T(8,128)(2,1)S(1)} %collective-permute-done.8.refs_2_), channel_id=1, source_target_pairs={{0,4},{1,5},{2,6},{3,7},{4,0},{5,1},{6,2},{7,3}} | collective-permute-start | bytes 1966088 | tf_op jit(solution)/shard_map/ppermute | solution.py:382
  550.3 47.7 %collective-permute-start.13 = (bf16[4,5,128,128]{3,2,1,0:T(8,128)(2,1)}, bf16[4,5,128,128]{3,2,1,0:T(8,128)(2,1)S(1)}, u32[]{:S(2)}, u32[]{:S(2)}) collective-permute-start(bf16[4,5,128,128]{3,2,1,0:T(8,128)(2,1)} %collective-permute-done.11.refs_5_), channel_id=1, source_target_pairs={{0,2},{1,3},{2,0},{3,1},{4,6},{5,7},{6,4},{7,5}} | collective-permute-start | bytes 1966088 | tf_op jit(solution)/shard_map/ppermute | solution.py:382
  551.4 46.7 %collective-permute-start.80 = (bf16[128,8,192]{2,1,0:T(8,128)(2,1)}, bf16[128,8,192]{2,1,0:T(8,128)(2,1)}, u32[]{:S(2)}, u32[]{:S(2)}) collective-permute-start(bf16[128,8,192]{2,1,0:T(8,128)(2,1)} %get-tuple-element.185), channel_id=1, source_target_pairs={{0,1},{1,0},{2,3},{3,2},{4,5},{5,4},{6,7},{7,6}} | collective-permute-start | bytes 1179656 | tf_op jit(solution)/shard_map/ppermute | solution.py:382
  551.5 46.7 %collective-permute-start.79 = (bf16[128,8,128]{2,1,0:T(8,128)(2,1)}, bf16[128,8,128]{2,1,0:T(8,128)(2,1)S(1)}, u32[]{:S(2)}, u32[]{:S(2)}) collective-permute-start(bf16[128,8,128]{2,1,0:T(8,128)(2,1)} %get-tuple-element.184), channel_id=1, source_target_pairs={{0,1},{1,0},{2,3},{3,2},{4,5},{5,4},{6,7},{7,6}} | collective-permute-start | bytes 786440 | tf_op jit(solution)/shard_map/ppermute | solution.py:382
  598.0 58.6 %collective-permute-start.84 = (bf16[4,2,1024,256]{3,2,1,0:T(8,128)(2,1)}, bf16[4,2,1024,256]{3,2,1,0:T(8,128)(2,1)}, u32[]{:S(2)}, u32[]{:S(2)}) collective-permute-start(bf16[4,2,1024,256]{3,2,1,0:T(8,128)(2,1)} %get-tuple-element.193), channel_id=1, source_target_pairs={{0,1},{1,0},{2,3},{3,2},{4,5},{5,4},{6,7},{7,6}} | collective-permute-start | bytes 12582920 | tf_op jit(solution)/shard_map/ppermute | solution.py:382
  (106 other events, 2322.3 us)

commit v2 on v1

--- a/solution.py
+++ b/solution.py
@@ -21,6 +21,7 @@
 ROWS = 32
 NEG = -1e30
 BF = jnp.bfloat16
+GROUPS = (1, 1, 2, 2, 1, 1)
 F32 = jnp.float32
 
 
@@ -44,19 +45,21 @@
             out[p, 4] = jnp.concatenate(ropes, axis=1).astype(BF)
 
 
-def pack_chunk(j, core, queries, d_out):
+def pack_chunk(group, core, queries, d_out):
+    j, units = group
+
     def own(i, c):
-        return (0, c[0] * (64 // HC) + j, 0)
+        return (0, c[0] * (64 // HC) + j + i, 0)
 
     def oth(i, c):
-        return (0, (1 - c[0]) * (64 // HC) + j, 0)
-
-    shape = jax.ShapeDtypeStruct((NP, 5, TB, D), BF)
-    spec = pl.BlockSpec((NP, 5, TB, D), lambda i, c: (0, 0, 0, 0))
+        return (0, (1 - c[0]) * (64 // HC) + j + i, 0)
+
+    shape = jax.ShapeDtypeStruct((NP * units, 5, TB, D), BF)
+    spec = pl.BlockSpec((NP, 5, TB, D), lambda i, c: (i, 0, 0, 0))
     return pl.pallas_call(
         pack_kernel,
         grid_spec=pltpu.PrefetchScalarGridSpec(
-            num_scalar_prefetch=1, grid=(1,),
+            num_scalar_prefetch=1, grid=(units,),
             in_specs=[pl.BlockSpec((TB, HC, D + R), own), pl.BlockSpec((TB, HC, D), own),
                       pl.BlockSpec((TB, HC, D + R), oth), pl.BlockSpec((TB, HC, D), oth)],
             out_specs=[spec, spec],
@@ -95,14 +98,14 @@
 def partner_dw(h0, scale, ct_ref, dkv_in, bigs):
     for w in range(2):
         view = bigs[w].reshape(L * HC, D)
-        for t in range(2):
-            dw = dot(ct_ref[t * QB:(t + 1) * QB, :], dkv_in[0, w], 1, 0)
-            dw = dw * scale if w == 0 else dw
-            for k in range(2):
-                view[pl.ds(t * QB * HC + h0 + k, QB, stride=HC), :] = dw[:, k * D:(k + 1) * D]
-
-
-def main_kernel(aliased, prev, score_scale, me_ref, *refs):
+        dw = dot(ct_ref[...], dkv_in[0, w], 1, 0)
+        dw = dw * scale if w == 0 else dw
+        for k in range(2):
+            view[pl.ds(h0 + k, L, stride=HC), :] = dw[:, k * D:(k + 1) * D]
+
+
+def main_kernel(aliased, lead, score_scale, me_ref, *refs):
+    prev = lead > 0
     _, ct_ref, _, _, _, _, _ = refs[ND:ND + 7]
     n_in = ND + 7
     if prev:
@@ -115,21 +118,22 @@
         main_body(step, score_scale, me_ref, refs, outs)
         return
 
-    @pl.when(step < NP)
-    def _():
-        partner_dw(2 * step, score_scale, ct_ref, dkv_in, (dwk_big, dwv_big))
-
-    @pl.when(step == 0)
+    @pl.when(step < lead)
+    def _():
+        partner_dw(2 * (step % NP), score_scale, ct_ref, dkv_in, (dwk_big, dwv_big))
+
+    @pl.when((step < lead) & (step % NP == 0))
     def _():
         o_big[...] = o_in[...]
         dq_big[...] = dq_in[...]
 
-    @pl.when(step >= NP)
-    def _():
-        main_body(step - NP, score_scale, me_ref, refs, outs)
-
-
-def main_body(p, score_scale, me_ref, refs, outs):
+    @pl.when(step >= lead)
+    def _():
+        main_body(step - lead, score_scale, me_ref, refs, outs)
+
+
+def main_body(p_all, score_scale, me_ref, refs, outs):
+    p = p_all % NP
     a_refs = refs[:ND]
     c_ref, ct_ref, r_ref, wk_ref, wv_ref, dc_in, dr_in = refs[ND:ND + 7]
     (dwk_big, dwv_big, o_big, dq_big, dkv_out, o_par, dq_par, dc_out, dr_out,
@@ -146,6 +150,9 @@
             wsc[...] = src[...].astype(F32).reshape(L * HC, D)
             for h in range(HC):
                 dst_w[h // 2, :, (h % 2) * D:(h % 2 + 1) * D] = wsc[pl.ds(h, L, stride=HC), :].astype(BF)
+
+    @pl.when(p_all == 0)
+    def _():
         r = r_ref[...]
         zero = jnp.zeros((S, R), BF)
         kr[0, :, D:] = jnp.concatenate([r[:, :R], zero], axis=1)
@@ -163,15 +170,14 @@
             qa[k, slot, D:] = a_refs[d][0, 4]
             do[k, slot, :] = a_refs[d][0, 2 + k]
 
-    for t in range(NQ):
-        rows = slice(t * QB, (t + 1) * QB)
-        keys = dot(c_ref[rows, :], wk[p], 1, 0).astype(BF)
-        vals = dot(c_ref[rows, :], wv[p], 1, 0).astype(BF)
-        for k in range(2):
-            kr[k, rows, :D] = keys[:, k * D:(k + 1) * D]
-            vs[k, rows, :] = vals[:, k * D:(k + 1) * D]
-
-    upper = lax.broadcasted_iota(jnp.int32, (QB, QB), 0) <= lax.broadcasted_iota(jnp.int32, (QB, QB), 1)
+    keys = dot(c_ref[...], wk[p], 1, 0).astype(BF)
+    vals = dot(c_ref[...], wv[p], 1, 0).astype(BF)
+    for k in range(2):
+        kr[k, :, :D] = keys[:, k * D:(k + 1) * D]
+        vs[k] = vals[:, k * D:(k + 1) * D]
+
+    low = lax.broadcasted_iota(jnp.int32, (8, QB), 0)
+    col = lax.broadcasted_iota(jnp.int32, (8, QB), 1)
 
     @pl.loop(0, 2)
     def _(k):
@@ -179,20 +185,22 @@
             q_i = qa[k, i * QB:(i + 1) * QB, :]
             d_i = do[k, i * QB:(i + 1) * QB, :]
             base = QB * (i * (i + 1) // 2)
-            for t in range(i + 1):
-                rows = slice(t * QB, (t + 1) * QB)
-                out = slice(base + t * QB, base + (t + 1) * QB)
-                sc = dot(kr[k, rows, :], q_i, 1, 1)
-                st[out, :] = jnp.where(upper, sc, NEG) if t == i else sc
-                dp[out, :] = dot(vs[k, rows, :], d_i, 1, 1)
+            rows = slice(0, (i + 1) * QB)
+            out = slice(base, base + (i + 1) * QB)
+            st[out, :] = dot(kr[k, rows, :], q_i, 1, 1)
+            dp[out, :] = dot(vs[k, rows, :], d_i, 1, 1)
 
         def soften(i):
             n = (i + 1) * QB
             base = QB * (i * (i + 1) // 2)
-            mxs = [st[base + 8 * a:base + 8 * a + 8, :] for a in range(4)]
-            for r0 in range(32, n, 32):
-                for a in range(4):
-                    mxs[a] = jnp.maximum(mxs[a], st[base + r0 + 8 * a:base + r0 + 8 * a + 8, :])
+            mxs = [None] * 4
+            for r0 in range(0, n, 8):
+                x = st[base + r0:base + r0 + 8, :]
+                if r0 >= i * QB:
+                    x = jnp.where(low + (r0 - i * QB) <= col, x, NEG)
+                    st[base + r0:base + r0 + 8, :] = x
+                a = r0 // 8 % 4
+                mxs[a] = x if mxs[a] is None else jnp.maximum(mxs[a], x)
             mx = jnp.maximum(jnp.maximum(mxs[0], mxs[1]), jnp.maximum(mxs[2], mxs[3]))
             mx = jnp.max(mx, axis=0, keepdims=True)
             ls = jnp.zeros((8, QB), F32)
@@ -257,24 +265,38 @@
             jax.ShapeDtypeStruct((TB, 128, D), BF), jax.ShapeDtypeStruct((TB, 128, D + R), BF)]
 
 
-def main_chunk(j, score_scale, me, blocks, c_abs, c_t, r_abs, w_uk, w_uv, dc, dr, big, prev):
+def main_chunk(group, score_scale, me, blocks, c_abs, c_t, r_abs, w_uk, w_uv, dc, dr, big, prev_group, prev):
     per = 64 // HC
-    lead = NP if prev is not None else 0
+    j, units = group
+    j_prev, units_prev = prev_group if prev is not None else (0, 0)
+    lead = NP * units_prev
+
+    def main_unit(i):
+        return jnp.maximum(i - lead, 0) // NP
+
+    def prev_unit(i):
+        return jnp.minimum(i, lead - 1) // NP
 
     def head_block(i, m):
-        return (0, (m[0] % 2) * per + j, 0)
+        return (0, (m[0] % 2) * per + j + main_unit(i), 0)
 
     def out_block(i, m):
-        own = (m[0] % 2) * per + j
+        own = (m[0] % 2) * per + j + main_unit(i)
         if not lead:
             return (0, own, 0)
-        return (0, jnp.where(i < lead, (1 - m[0] % 2) * per + j - 2, own), 0)
+        return (0, jnp.where(i < lead, (1 - m[0] % 2) * per + j_prev + prev_unit(i), own), 0)
+
+    def par_block(i, m):
+        return (0, main_unit(i), 0)
+
+    def in_block(i, m):
+        return (0, prev_unit(i), 0)
 
     def main_step(i, m):
         return (jnp.maximum(i - lead, 0), 0, 0, 0)
 
     def prev_step(i, m):
-        return (jnp.minimum(i, NP - 1), 0, 0, 0)
+        return (jnp.minimum(i, lead - 1), 0, 0, 0)
 
     def full2(i, m):
         return (0, 0)
@@ -287,15 +309,14 @@
                 + [pl.BlockSpec((S, L), full2, pipeline_mode=once),
                    pl.BlockSpec((L, S), full2, pipeline_mode=once),
                    pl.BlockSpec((S, D), full2, pipeline_mode=once),
-                   pl.BlockSpec((L, HC, D), head_block, pipeline_mode=once),
-                   pl.BlockSpec((L, HC, D), head_block, pipeline_mode=once),
+                   pl.BlockSpec((L, HC, D), head_block),
+                   pl.BlockSpec((L, HC, D), head_block),
                    pl.BlockSpec((QB, L), full2, pipeline_mode=once),
                    pl.BlockSpec((2, QB, D), full3, pipeline_mode=once)])
     args = list(blocks) + [c_abs, c_t, r_abs, w_uk, w_uv, dc, dr]
     if prev is not None:
         in_specs += [pl.BlockSpec((1, 2, S, 2 * D), prev_step),
-                     pl.BlockSpec((TB, HC, D), full3, pipeline_mode=once),
-                     pl.BlockSpec((TB, HC, D + R), full3, pipeline_mode=once)]
+                     pl.BlockSpec((TB, HC, D), in_block), pl.BlockSpec((TB, HC, D + R), in_block)]
         args += list(prev)
     aliases = {}
     if big is not None:
@@ -304,17 +325,16 @@
         args += list(big)
     tri = QB * NQ * (NQ + 1) // 2
     outs = pl.pallas_call(
-        functools.partial(main_kernel, big is not None, prev is not None, score_scale),
+        functools.partial(main_kernel, big is not None, lead, score_scale),
         grid_spec=pltpu.PrefetchScalarGridSpec(
-            num_scalar_prefetch=1, grid=(NP + lead,),
+            num_scalar_prefetch=1, grid=(NP * units + lead,),
             in_specs=in_specs,
             out_specs=[pl.BlockSpec((L, HC, D), out_block),
                        pl.BlockSpec((L, HC, D), out_block),
                        pl.BlockSpec((TB, HC, D), out_block),
                        pl.BlockSpec((TB, HC, D + R), out_block),
                        pl.BlockSpec((1, 2, S, 2 * D), main_step),
-                       pl.BlockSpec((TB, HC, D), full3, pipeline_mode=once),
-                       pl.BlockSpec((TB, HC, D + R), full3, pipeline_mode=once),
+                       pl.BlockSpec((TB, HC, D), par_block), pl.BlockSpec((TB, HC, D + R), par_block),
                        pl.BlockSpec((QB, L), full2, pipeline_mode=once),
                        pl.BlockSpec((2, QB, D), full3, pipeline_mode=once)],
             scratch_shapes=[
@@ -329,13 +349,14 @@
                 pltpu.VMEM((2, TB * HC, D), F32),
                 pltpu.VMEM((QB, D), F32), pltpu.VMEM((QB, 2 * D), F32)]),
         out_shape=big_shapes() + [
-            jax.ShapeDtypeStruct((NP, 2, S, 2 * D), BF),
-            jax.ShapeDtypeStruct((TB, HC, D), BF), jax.ShapeDtypeStruct((TB, HC, D + R), BF),
+            jax.ShapeDtypeStruct((NP * units, 2, S, 2 * D), BF),
+            jax.ShapeDtypeStruct((TB, HC * units, D), BF),
+            jax.ShapeDtypeStruct((TB, HC * units, D + R), BF),
             jax.ShapeDtypeStruct((QB, L), F32), jax.ShapeDtypeStruct((2, QB, D), F32)],
         input_output_aliases=aliases,
         compiler_params=pltpu.CompilerParams(vmem_limit_bytes=60 * 2 ** 20),
         name="mla_chunk",
-        cost_estimate=pl.CostEstimate(flops=25 * 10 ** 9, bytes_accessed=20 * 10 ** 6, transcendentals=0),
+        cost_estimate=pl.CostEstimate(flops=units * 25 * 10 ** 9, bytes_accessed=20 * 10 ** 6, transcendentals=0),
     )(me, *args)
     return outs[:4], outs[4:7], outs[7], outs[8]
 
@@ -343,25 +364,27 @@
 def last_kernel(score_scale, core_ref, ct_ref, dkv_in, o_in, dq_in, *refs):
     dwk_big, dwv_big, o_big, dq_big = refs[4:]
     step = pl.program_id(0)
-    partner_dw(2 * step, score_scale, ct_ref, dkv_in, (dwk_big, dwv_big))
-
-    @pl.when(step == 0)
+    partner_dw(2 * (step % NP), score_scale, ct_ref, dkv_in, (dwk_big, dwv_big))
+
+    @pl.when(step % NP == 0)
     def _():
         o_big[...] = o_in[...]
         dq_big[...] = dq_in[...]
 
 
-def last_chunk(j, score_scale, core, c_t, prev, big):
+def last_chunk(group, score_scale, core, c_t, prev, big):
+    j, units = group
+
     def at(i, c):
-        return (0, (1 - c[0]) * (64 // HC) + j, 0)
+        return (0, (1 - c[0]) * (64 // HC) + j + i // NP, 0)
 
     def full3(i, c):
-        return (0, 0, 0)
+        return (0, i // NP, 0)
 
     return pl.pallas_call(
         functools.partial(last_kernel, score_scale),
         grid_spec=pltpu.PrefetchScalarGridSpec(
-            num_scalar_prefetch=1, grid=(NP,),
+            num_scalar_prefetch=1, grid=(NP * units,),
             in_specs=[pl.BlockSpec((L, S), lambda i, c: (0, 0), pipeline_mode=pl.Buffered(1)),
                       pl.BlockSpec((1, 2, S, 2 * D), lambda i, c: (i, 0, 0, 0)),
                       pl.BlockSpec((TB, HC, D), full3), pl.BlockSpec((TB, HC, D + R), full3)]
@@ -386,7 +409,8 @@
         dev = lax.axis_index("cp").astype(jnp.int32)
         me = dev[None]
         core = me % 2
-        n_chunks = queries.shape[1] // 2 // HC
+        n_chunks = len(GROUPS)
+        groups = [(sum(GROUPS[:g]), GROUPS[g]) for g in range(n_chunks)]
 
         lat = jnp.concatenate([latent, key_rope, jnp.zeros((TB, D - R), BF)], axis=1)
         lats = [lat] + [hop(lat, k) for k in range(1, ND)]
@@ -394,8 +418,9 @@
         lats[1] = lat1
         c_abs, c_t, r_abs = prep(me, lats)
 
-        packs = [pack_chunk(j, core, queries, d_out) for j in range(n_chunks)]
-        me0 = lax.optimization_barrier((me, *[own for own, _ in packs]))[0]
+        packs = []
+        for group in groups:
+            packs.append(pack_chunk(group, core, queries, d_out))
         recv = []
         for own, oth in packs:
             a1, a2, a5, a3, a4 = [hop(x, k)
@@ -408,8 +433,9 @@
         big = None
         sent = []
         for j in range(n_chunks):
-            big, send, dc, dr = main_chunk(j, score_scale, me0 if j == 0 else me, recv[j],
+            big, send, dc, dr = main_chunk(groups[j], score_scale, me, recv[j],
                                            c_abs, c_t, r_abs, w_uk, w_uv, dc, dr, big,
+                                           groups[j - 2] if j >= 2 else None,
                                            sent[j - 2] if j >= 2 else None)
             sent.append([hop(x, 1) for x in send])
         dc = dc.reshape(2, TB, L)
@@ -425,7 +451,7 @@
         d_latent = swap_sum(dc)
         d_key_rope = swap_sum(dr)
         for j in (n_chunks - 2, n_chunks - 1):
-            big = last_chunk(j, score_scale, core, c_t, sent[j], big)
+            big = last_chunk(groups[j], score_scale, core, c_t, sent[j], big)
         d_w_uk, d_w_uv, attn_out, d_query = big
         return attn_out, d_query, d_latent, d_key_rope, d_w_uk, d_w_uv
 

time: 695 us -> 724 us (1.042)
  waiting for transfers between devices: 176 us -> 211 us
  starting transfers between devices: 73.1 us -> 60.9 us
    ppermute x89 -> x69, waiting for transfers between devices: 176 us -> 211 us  [hop(): return lax.ppermute(x, 'cp', perm)]
    ppermute x89 -> x69, starting transfers between devices: 73.1 us -> 60.9 us  [hop(): return lax.ppermute(x, 'cp', perm)]
    pallas_call x8 -> x6, Pallas kernels: 23.5 us -> 19.2 us  [pack_chunk(): pl.pallas_call(pack_kernel, grid_spec=pltpu.PrefetchScalarGridSpec(num_sc...]
    unnamed x132 -> x86, local copies, waits for them, and re-layouts: 21.2 us -> 22.1 us
    pallas_call x8 -> x6, Pallas kernels: 359 us -> 359 us  [main_chunk(): pl.pallas_call(functools.partial(main_kernel, big is not None, lead, scor...]
  transfers between devices with their start and end apart: 89 -> 69, of which waited for: 22 -> 25; matrix products, arithmetic and copies ran while one was open for 2% -> 2% of each run, Pallas kernels for 57% -> 54%
where the time goes in v2:
time: 724 us; the launch traced here: 714 us
  Pallas kernels  395 us (55%)
  waiting for transfers between devices  211 us (29%)
  starting transfers between devices  60.9 us (8%)
  local copies, waits for them, and re-layouts  40.9 us (6%)
    pallas_call x6, Pallas kernels, main_chunk(): pl.pallas_call(functools.partial(main_kernel, big is not None, lead, scor...  359 us
    ppermute x69, waiting for transfers between devices, hop(): return lax.ppermute(x, 'cp', perm)  211 us
    ppermute x69, starting transfers between devices, hop(): return lax.ppermute(x, 'cp', perm)  60.9 us
    unnamed x86, local copies, waits for them, and re-layouts  22.1 us
    pallas_call x6, Pallas kernels, pack_chunk(): pl.pallas_call(pack_kernel, grid_spec=pltpu.PrefetchScalarGridSpec(num_sc...  19.2 us
  transfers between devices with their start and end apart: 69, of which 25 were waited for; matrix products, arithmetic and copies ran while one was open for 2% of the time, Pallas kernels for 54%

profile of v2, /device:TPU:0, one launch (start us, length us, event | category | flops | bytes accessed | tf_op | source)
XLA Modules:
  0.0 714.0 jit_solution(5069742485793445732)
XLA Ops:
  4.4 10.0 %copy.57.qo_ref.qp_ref = bf16[128,128,192]{2,1,0:T(8,128)(2,1)} copy(bf16[128,128,192]{1,2,0:T(8,128)(2,1)} %param.6) | data formatting | bytes 12582912 | tf_op jit(solution)/shard_map/optimization_barrier | solution.py:417
  14.4 2.9 pack.11
  17.3 2.8 collective-permute-start.43
  23.7 15.8 %collective-permute-done.1.refs_2_ = bf16[128,640]{1,0:T(8,128)(2,1)S(1)} collective-permute-done((bf16[128,640]{1,0:T(8,128)(2,1)S(1)}, bf16[128,640]{1,0:T(8,128)(2,1)S(1)}, u32[]{:S(2)}, u32[]{:S(2)}) %collective-permute-start.1) | collective-permute-done | bytes 163872 | tf_op jit(solution)/shard_map/ppermute | solution.py:405
  39.5 3.0 collective-permute-start.5
  42.5 2.9 collective-permute-start.6
  46.1 3.0 pack.10
  52.8 11.9 %collective-permute-done.46.refs_5_ = bf16[4,5,128,128]{3,2,1,0:T(8,128)(2,1)S(1)} collective-permute-done((bf16[4,5,128,128]{3,2,1,0:T(8,128)(2,1)}, bf16[4,5,128,128]{3,2,1,0:T(8,128)(2,1)S(1)}, u32[]{:S(2)}, u32[]{:S(2)}) %collective-permute-start.46) | collective-permute-done | bytes 655392 | tf_op jit(solution)/shard_map/ppermute | solution.py:405
  66.2 3.7 pack.9
  71.4 7.4 %collective-permute-done.45.refs_4_ = bf16[4,5,128,128]{3,2,1,0:T(8,128)(2,1)} collective-permute-done((bf16[4,5,128,128]{3,2,1,0:T(8,128)(2,1)}, bf16[4,5,128,128]{3,2,1,0:T(8,128)(2,1)}, u32[]{:S(2)}, u32[]{:S(2)}) %collective-permute-start.45) | collective-permute-done | bytes 655392 | tf_op jit(solution)/shard_map/ppermute | solution.py:405
  81.5 11.4 %collective-permute-done.39.refs_5_ = bf16[4,5,128,128]{3,2,1,0:T(8,128)(2,1)S(1)} collective-permute-done((bf16[4,5,128,128]{3,2,1,0:T(8,128)(2,1)}, bf16[4,5,128,128]{3,2,1,0:T(8,128)(2,1)S(1)}, u32[]{:S(2)}, u32[]{:S(2)}) %collective-permute-start.39) | collective-permute-done | bytes 655392 | tf_op jit(solution)/shard_map/ppermute | solution.py:405
  96.3 10.4 %collective-permute-done.38.refs_4_ = bf16[4,5,128,128]{3,2,1,0:T(8,128)(2,1)S(1)} collective-permute-done((bf16[4,5,128,128]{3,2,1,0:T(8,128)(2,1)S(1)}, bf16[4,5,128,128]{3,2,1,0:T(8,128)(2,1)S(1)}, u32[]{:S(2)}, u32[]{:S(2)}) %collective-permute-start.38) | collective-permute-done | bytes 655392 | tf_op jit(solution)/shard_map/ppermute | solution.py:405
  109.2 3.0 prep.1
  112.2 3.7 pack.8
  116.0 5.0 collective-permute-done.47.refs_6_
  121.5 15.7 %collective-permute-done.48.refs_7_ = bf16[4,5,128,128]{3,2,1,0:T(8,128)(2,1)} collective-permute-done((bf16[4,5,128,128]{3,2,1,0:T(8,128)(2,1)}, bf16[4,5,128,128]{3,2,1,0:T(8,128)(2,1)}, u32[]{:S(2)}, u32[]{:S(2)}) %collective-permute-start.48) | collective-permute-done | bytes 655392 | tf_op jit(solution)/shard_map/ppermute | solution.py:405
  137.9 13.2 %collective-permute-done.41.refs_7_ = bf16[4,5,128,128]{3,2,1,0:T(8,128)(2,1)S(1)} collective-permute-done((bf16[4,5,128,128]{3,2,1,0:T(8,128)(2,1)S(1)}, bf16[4,5,128,128]{3,2,1,0:T(8,128)(2,1)S(1)}, u32[]{:S(2)}, u32[]{:S(2)}) %collective-permute-start.41) | collective-permute-done | bytes 655392 | tf_op jit(solution)/shard_map/ppermute | solution.py:405
  154.8 42.5 %mla_chunk.6 = (f32[512,128,128]{2,1,0:T(8,128)}, f32[512,128,128]{2,1,0:T(8,128)}, bf16[128,128,128]{2,1,0:T(8,128)(2,1)}, bf16[128,128,192]{2,1,0:T(8,128)(2,1...) custom-call(s32[1]{0:T(128)} %bitcast.me_ref, ...), custom_call_target="tpu_custom_call" | custom-call | flops 24999999488 | bytes 20000000 | tf_op jit(solution)/shard_map/mla_chunk/pallas_call | solution.py:327
  200.0 7.3 %collective-permute-done.22.refs_2_ = bf16[8,5,128,128]{3,2,1,0:T(8,128)(2,1)S(1)} collective-permute-done((bf16[8,5,128,128]{3,2,1,0:T(8,128)(2,1)}, bf16[8,5,128,128]{3,2,1,0:T(8,128)(2,1)S(1)}, u32[]{:S(2)}, u32[]{:S(2)}) %collective-permute-start.22) | collective-permute-done | bytes 1310752 | tf_op jit(solution)/shard_map/ppermute | solution.py:405
  208.9 19.2 %collective-permute-done.25.refs_5_ = bf16[8,5,128,128]{3,2,1,0:T(8,128)(2,1)S(1)} collective-permute-done((bf16[8,5,128,128]{3,2,1,0:T(8,128)(2,1)}, bf16[8,5,128,128]{3,2,1,0:T(8,128)(2,1)S(1)}, u32[]{:S(2)}, u32[]{:S(2)}) %collective-permute-start.25) | collective-permute-done | bytes 1310752 | tf_op jit(solution)/shard_map/ppermute | solution.py:405
  229.5 5.3 collective-permute-done.23.refs_3_
  236.5 20.9 %collective-permute-done.24.refs_4_ = bf16[8,5,128,128]{3,2,1,0:T(8,128)(2,1)S(1)} collective-permute-done((bf16[8,5,128,128]{3,2,1,0:T(8,128)(2,1)S(1)}, bf16[8,5,128,128]{3,2,1,0:T(8,128)(2,1)S(1)}, u32[]{:S(2)}, u32[]{:S(2)}) %collective-permute-start.24) | collective-permute-done | bytes 1310752 | tf_op jit(solution)/shard_map/ppermute | solution.py:405
  257.4 1.9 collective-permute-start.34
  259.3 42.7 %mla_chunk.7 = (f32[512,128,128]{2,1,0:T(8,128)}, f32[512,128,128]{2,1,0:T(8,128)}, bf16[128,128,128]{2,1,0:T(8,128)(2,1)}, bf16[128,128,192]{2,1,0:T(8,128)(2,1...) custom-call(s32[1]{0:T(128)} %bitcast.me_ref, ...), custom_call_target="tpu_custom_call", output_to_operand_aliasing={{0}: (16, {}), {1}: (17, {}), {2}: (18, {}), {3}: (19, {})} | custom-call | flops 24999999488 | bytes 20000000 | tf_op jit(solution)/shard_map/mla_chunk/pallas_call | solution.py:327
  304.6 83.7 %mla_chunk.8 = (f32[512,128,128]{2,1,0:T(8,128)}, f32[512,128,128]{2,1,0:T(8,128)}, bf16[128,128,128]{2,1,0:T(8,128)(2,1)}, bf16[128,128,192]{2,1,0:T(8,128)(2,1...) custom-call(s32[1]{0:T(128)} %bitcast.me_ref, ...), custom_call_target="tpu_custom_call", output_to_operand_aliasing={{0}: (19, {}), {1}: (20, {}), {2}: (21, {}), {3}: (22, {})} | custom-call | flops 49999998976 | bytes 20000000 | tf_op jit(solution)/shard_map/mla_chunk/pallas_call | solution.py:327
  389.3 84.0 %mla_chunk.9 = (f32[512,128,128]{2,1,0:T(8,128)}, f32[512,128,128]{2,1,0:T(8,128)}, bf16[128,128,128]{2,1,0:T(8,128)(2,1)}, bf16[128,128,192]{2,1,0:T(8,128)(2,1...) custom-call(s32[1]{0:T(128)} %bitcast.me_ref, ...), custom_call_target="tpu_custom_call", output_to_operand_aliasing={{0}: (19, {}), {1}: (20, {}), {2}: (21, {}), {3}: (22, {})} | custom-call | flops 49999998976 | bytes 20000000 | tf_op jit(solution)/shard_map/mla_chunk/pallas_call | solution.py:327
  473.8 2.9 pack.7
  476.7 2.1 collective-permute-start.15
  480.6 13.4 %collective-permute-done.15.refs_2_ = bf16[4,5,128,128]{3,2,1,0:T(8,128)(2,1)} collective-permute-done((bf16[4,5,128,128]{3,2,1,0:T(8,128)(2,1)}, bf16[4,5,128,128]{3,2,1,0:T(8,128)(2,1)}, u32[]{:S(2)}, u32[]{:S(2)}) %collective-permute-start.15) | collective-permute-done | bytes 655392 | tf_op jit(solution)/shard_map/ppermute | solution.py:405
  495.9 1.9 collective-permute-start.17
  497.8 2.9 pack.6
  501.6 9.5 %collective-permute-done.16.refs_3_ = bf16[4,5,128,128]{3,2,1,0:T(8,128)(2,1)} collective-permute-done((bf16[4,5,128,128]{3,2,1,0:T(8,128)(2,1)}, bf16[4,5,128,128]{3,2,1,0:T(8,128)(2,1)}, u32[]{:S(2)}, u32[]{:S(2)}) %collective-permute-start.16) | collective-permute-done | bytes 655392 | tf_op jit(solution)/shard_map/ppermute | solution.py:405
  511.1 1.8 collective-permute-start.11
  513.0 1.7 collective-permute-start.10
  515.8 9.6 %collective-permute-done.8.refs_2_ = bf16[4,5,128,128]{3,2,1,0:T(8,128)(2,1)S(1)} collective-permute-done((bf16[4,5,128,128]{3,2,1,0:T(8,128)(2,1)}, bf16[4,5,128,128]{3,2,1,0:T(8,128)(2,1)S(1)}, u32[]{:S(2)}, u32[]{:S(2)}) %collective-permute-start.8) | collective-permute-done | bytes 655392 | tf_op jit(solution)/shard_map/ppermute | solution.py:405
  525.3 2.7 collective-permute-done.11.refs_5_
  531.0 11.5 %collective-permute-done.10.refs_4_ = bf16[4,5,128,128]{3,2,1,0:T(8,128)(2,1)} collective-permute-done((bf16[4,5,128,128]{3,2,1,0:T(8,128)(2,1)}, bf16[4,5,128,128]{3,2,1,0:T(8,128)(2,1)}, u32[]{:S(2)}, u32[]{:S(2)}) %collective-permute-start.10) | collective-permute-done | bytes 655392 | tf_op jit(solution)/shard_map/ppermute | solution.py:405
  542.5 2.2 collective-permute-start.19
  545.1 1.7 copy.70.refs_17_
  548.6 11.7 %collective-permute-done.19.refs_6_ = bf16[4,5,128,128]{3,2,1,0:T(8,128)(2,1)} collective-permute-done((bf16[4,5,128,128]{3,2,1,0:T(8,128)(2,1)}, bf16[4,5,128,128]{3,2,1,0:T(8,128)(2,1)}, u32[]{:S(2)}, u32[]{:S(2)}) %collective-permute-start.19) | collective-permute-done | bytes 655392 | tf_op jit(solution)/shard_map/ppermute | solution.py:405
  563.8 53.2 %mla_chunk.10 = (f32[512,128,128]{2,1,0:T(8,128)}, f32[512,128,128]{2,1,0:T(8,128)}, bf16[128,128,128]{2,1,0:T(8,128)(2,1)}, bf16[128,128,192]{2,1,0:T(8,128)(2,...) custom-call(s32[1]{0:T(128)} %bitcast.me_ref, ...), custom_call_target="tpu_custom_call", output_to_operand_aliasing={{0}: (19, {}), {1}: (20, {}), {2}: (21, {}), {3}: (22, {})} | custom-call | flops 24999999488 | bytes 20000000 | tf_op jit(solution)/shard_map/mla_chunk/pallas_call | solution.py:327
  618.7 53.0 %mla_chunk.11 = (f32[512,128,128]{2,1,0:T(8,128)}, f32[512,128,128]{2,1,0:T(8,128)}, bf16[128,128,128]{2,1,0:T(8,128)(2,1)}, bf16[128,128,192]{2,1,0:T(8,128)(2,...) custom-call(s32[1]{0:T(128)} %bitcast.me_ref, ...), custom_call_target="tpu_custom_call", output_to_operand_aliasing={{0}: (19, {}), {1}: (20, {}), {2}: (21, {}), {3}: (22, {})} | custom-call | flops 24999999488 | bytes 20000000 | tf_op jit(solution)/shard_map/mla_chunk/pallas_call | solution.py:327
  675.0 4.9 collective-permute-done.68
  682.9 3.4 copy-done
  686.2 7.0 last.2
  693.3 7.1 last.3
  700.4 3.4 copy-done.1
  703.7 10.1 %copy.75 = bf16[128,128,192]{1,2,0:T(8,128)(2,1)} copy(bf16[128,128,192]{2,1,0:T(8,128)(2,1)} %copy-done.1) | data formatting | bytes 12582912
  (208 shorter events, 61.9 us)
Async XLA Ops:
  17.3 34.0 %collective-permute-start.43 = (bf16[4,5,128,128]{3,2,1,0:T(8,128)(2,1)}, bf16[4,5,128,128]{3,2,1,0:T(8,128)(2,1)S(1)}, u32[]{:S(2)}, u32[]{:S(2)}) collective-permute-start(bf16[4,5,128,128]{3,2,1,0:T(8,128)(2,1)} %get-tuple-element.100.refs_0_), channel_id=1, source_target_pairs={{0,2},{1,3},{2,0},{3,1},{4,6},{5,7},{6,4},{7,5}} | collective-permute-start | bytes 1966088 | tf_op jit(solution)/shard_map/ppermute | solution.py:405
  20.2 22.3 %collective-permute-start.2 = (bf16[128,640]{1,0:T(8,128)(2,1)S(1)}, bf16[128,640]{1,0:T(8,128)(2,1)S(1)}, u32[]{:S(2)}, u32[]{:S(2)}) collective-permute-start(bf16[128,640]{1,0:T(8,128)(2,1)S(1)} %maximum_maximum_fusion.refs_0_), channel_id=1, source_target_pairs={{0,3},{1,2},{2,1},{3,0},{4,7},{5,6},{6,5},{7,4}} | collective-permute-start | bytes 491528 | tf_op jit(solution)/shard_map/ppermute | solution.py:405
  21.4 24.0 %collective-permute-start.3 = (bf16[128,640]{1,0:T(8,128)(2,1)S(1)}, bf16[128,640]{1,0:T(8,128)(2,1)S(1)}, u32[]{:S(2)}, u32[]{:S(2)}) collective-permute-start(bf16[128,640]{1,0:T(8,128)(2,1)S(1)} %maximum_maximum_fusion.refs_0_), channel_id=1, source_target_pairs={{0,4},{1,5},{2,6},{3,7},{4,0},{5,1},{6,2},{7,3}} | collective-permute-start | bytes 491528 | tf_op jit(solution)/shard_map/ppermute | solution.py:405
  22.9 26.1 %collective-permute-start.4 = (bf16[128,640]{1,0:T(8,128)(2,1)S(1)}, bf16[128,640]{1,0:T(8,128)(2,1)S(1)}, u32[]{:S(2)}, u32[]{:S(2)}) collective-permute-start(bf16[128,640]{1,0:T(8,128)(2,1)S(1)} %maximum_maximum_fusion.refs_0_), channel_id=1, source_target_pairs={{0,5},{1,4},{2,7},{3,6},{4,1},{5,0},{6,3},{7,2}} | collective-permute-start | bytes 491528 | tf_op jit(solution)/shard_map/ppermute | solution.py:405
  49.1 20.9 %collective-permute-start.42 = (bf16[4,5,128,128]{3,2,1,0:T(8,128)(2,1)S(1)}, bf16[4,5,128,128]{3,2,1,0:T(8,128)(2,1)}, u32[]{:S(2)}, u32[]{:S(2)}) collective-permute-start(bf16[4,5,128,128]{3,2,1,0:T(8,128)(2,1)S(1)} %copy-done.36), channel_id=1, source_target_pairs={{0,1},{1,0},{2,3},{3,2},{4,5},{5,4},{6,7},{7,6}} | collective-permute-start | bytes 1966088 | tf_op jit(solution)/shard_map/ppermute | solution.py:405
  49.5 20.7 %collective-permute-start.44 = (bf16[4,5,128,128]{3,2,1,0:T(8,128)(2,1)S(1)}, bf16[4,5,128,128]{3,2,1,0:T(8,128)(2,1)}, u32[]{:S(2)}, u32[]{:S(2)}) collective-permute-start(bf16[4,5,128,128]{3,2,1,0:T(8,128)(2,1)S(1)} %copy-done.36), channel_id=1, source_target_pairs={{0,3},{1,2},{2,1},{3,0},{4,7},{5,6},{6,5},{7,4}} | collective-permute-start | bytes 1966088 | tf_op jit(solution)/shard_map/ppermute | solution.py:405
  50.2 28.5 %collective-permute-start.45 = (bf16[4,5,128,128]{3,2,1,0:T(8,128)(2,1)}, bf16[4,5,128,128]{3,2,1,0:T(8,128)(2,1)}, u32[]{:S(2)}, u32[]{:S(2)}) collective-permute-start(bf16[4,5,128,128]{3,2,1,0:T(8,128)(2,1)} %get-tuple-element.100.refs_0_), channel_id=1, source_target_pairs={{0,4},{1,5},{2,6},{3,7},{4,0},{5,1},{6,2},{7,3}} | collective-permute-start | bytes 1966088 | tf_op jit(solution)/shard_map/ppermute | solution.py:405
  51.4 29.5 %collective-permute-start.36 = (bf16[4,5,128,128]{3,2,1,0:T(8,128)(2,1)}, bf16[4,5,128,128]{3,2,1,0:T(8,128)(2,1)S(1)}, u32[]{:S(2)}, u32[]{:S(2)}) collective-permute-start(bf16[4,5,128,128]{3,2,1,0:T(8,128)(2,1)} %get-tuple-element.98.refs_0_), channel_id=1, source_target_pairs={{0,2},{1,3},{2,0},{3,1},{4,6},{5,7},{6,4},{7,5}} | collective-permute-start | bytes 1966088 | tf_op jit(solution)/shard_map/ppermute | solution.py:405
  65.7 27.2 %collective-permute-start.39 = (bf16[4,5,128,128]{3,2,1,0:T(8,128)(2,1)}, bf16[4,5,128,128]{3,2,1,0:T(8,128)(2,1)S(1)}, u32[]{:S(2)}, u32[]{:S(2)}) collective-permute-start(bf16[4,5,128,128]{3,2,1,0:T(8,128)(2,1)} %get-tuple-element.99), channel_id=1, source_target_pairs={{0,5},{1,4},{2,7},{3,6},{4,1},{5,0},{6,3},{7,2}} | collective-permute-start | bytes 1966088 | tf_op jit(solution)/shard_map/ppermute | solution.py:405
  69.9 23.6 %collective-permute-start.35 = (bf16[4,5,128,128]{3,2,1,0:T(8,128)(2,1)}, bf16[4,5,128,128]{3,2,1,0:T(8,128)(2,1)S(1)}, u32[]{:S(2)}, u32[]{:S(2)}) collective-permute-start(bf16[4,5,128,128]{3,2,1,0:T(8,128)(2,1)} %get-tuple-element.99), channel_id=1, source_target_pairs={{0,1},{1,0},{2,3},{3,2},{4,5},{5,4},{6,7},{7,6}} | collective-permute-start | bytes 1966088 | tf_op jit(solution)/shard_map/ppermute | solution.py:405
  70.2 24.6 %collective-permute-start.37 = (bf16[4,5,128,128]{3,2,1,0:T(8,128)(2,1)}, bf16[4,5,128,128]{3,2,1,0:T(8,128)(2,1)S(1)}, u32[]{:S(2)}, u32[]{:S(2)}) collective-permute-start(bf16[4,5,128,128]{3,2,1,0:T(8,128)(2,1)} %get-tuple-element.99), channel_id=1, source_target_pairs={{0,3},{1,2},{2,1},{3,0},{4,7},{5,6},{6,5},{7,4}} | collective-permute-start | bytes 1966088 | tf_op jit(solution)/shard_map/ppermute | solution.py:405
  78.8 28.0 %collective-permute-start.38 = (bf16[4,5,128,128]{3,2,1,0:T(8,128)(2,1)S(1)}, bf16[4,5,128,128]{3,2,1,0:T(8,128)(2,1)S(1)}, u32[]{:S(2)}, u32[]{:S(2)}) collective-permute-start(bf16[4,5,128,128]{3,2,1,0:T(8,128)(2,1)S(1)} %copy-done.5), channel_id=1, source_target_pairs={{0,4},{1,5},{2,6},{3,7},{4,0},{5,1},{6,2},{7,3}} | collective-permute-start | bytes 1966088 | tf_op jit(solution)/shard_map/ppermute | solution.py:405
  80.8 71.8 %collective-permute-start.29 = (bf16[8,5,128,128]{3,2,1,0:T(8,128)(2,1)}, bf16[8,5,128,128]{3,2,1,0:T(8,128)(2,1)}, u32[]{:S(2)}, u32[]{:S(2)}) collective-permute-start(bf16[8,5,128,128]{3,2,1,0:T(8,128)(2,1)} %get-tuple-element.96.refs_0_), channel_id=1, source_target_pairs={{0,2},{1,3},{2,0},{3,1},{4,6},{5,7},{6,4},{7,5}} | collective-permute-start | bytes 3932168 | tf_op jit(solution)/shard_map/ppermute | solution.py:405
  92.9 28.0 %collective-permute-start.47 = (bf16[4,5,128,128]{3,2,1,0:T(8,128)(2,1)}, bf16[4,5,128,128]{3,2,1,0:T(8,128)(2,1)}, u32[]{:S(2)}, u32[]{:S(2)}) collective-permute-start(bf16[4,5,128,128]{3,2,1,0:T(8,128)(2,1)} %copy-done.34), channel_id=1, source_target_pairs={{0,4},{1,5},{2,6},{3,7},{4,0},{5,1},{6,2},{7,3}} | collective-permute-start | bytes 1966088 | tf_op jit(solution)/shard_map/ppermute | solution.py:405
  93.6 43.6 %collective-permute-start.48 = (bf16[4,5,128,128]{3,2,1,0:T(8,128)(2,1)}, bf16[4,5,128,128]{3,2,1,0:T(8,128)(2,1)}, u32[]{:S(2)}, u32[]{:S(2)}) collective-permute-start(bf16[4,5,128,128]{3,2,1,0:T(8,128)(2,1)} %copy-done.35), channel_id=1, source_target_pairs={{0,2},{1,3},{2,0},{3,1},{4,6},{5,7},{6,4},{7,5}} | collective-permute-start | bytes 1966088 | tf_op jit(solution)/shard_map/ppermute | solution.py:405
  94.8 42.3 %collective-permute-start.40 = (bf16[4,5,128,128]{3,2,1,0:T(8,128)(2,1)S(1)}, bf16[4,5,128,128]{3,2,1,0:T(8,128)(2,1)}, u32[]{:S(2)}, u32[]{:S(2)}) collective-permute-start(bf16[4,5,128,128]{3,2,1,0:T(8,128)(2,1)S(1)} %collective-permute-done.36.refs_2_), channel_id=1, source_target_pairs={{0,4},{1,5},{2,6},{3,7},{4,0},{5,1},{6,2},{7,3}} | collective-permute-start | bytes 1966088 | tf_op jit(solution)/shard_map/ppermute | solution.py:405
  107.6 43.5 %collective-permute-start.41 = (bf16[4,5,128,128]{3,2,1,0:T(8,128)(2,1)S(1)}, bf16[4,5,128,128]{3,2,1,0:T(8,128)(2,1)S(1)}, u32[]{:S(2)}, u32[]{:S(2)}) collective-permute-start(bf16[4,5,128,128]{3,2,1,0:T(8,128)(2,1)S(1)} %collective-permute-done.39.refs_5_), channel_id=1, source_target_pairs={{0,2},{1,3},{2,0},{3,1},{4,6},{5,7},{6,4},{7,5}} | collective-permute-start | bytes 1966088 | tf_op jit(solution)/shard_map/ppermute | solution.py:405
  120.9 76.4 %collective-permute-start.32 = (bf16[8,5,128,128]{3,2,1,0:T(8,128)(2,1)}, bf16[8,5,128,128]{3,2,1,0:T(8,128)(2,1)}, u32[]{:S(2)}, u32[]{:S(2)}) collective-permute-start(bf16[8,5,128,128]{3,2,1,0:T(8,128)(2,1)} %get-tuple-element.97), channel_id=1, source_target_pairs={{0,5},{1,4},{2,7},{3,6},{4,1},{5,0},{6,3},{7,2}} | collective-permute-start | bytes 3932168 | tf_op jit(solution)/shard_map/ppermute | solution.py:405
  137.1 60.2 %collective-permute-start.28 = (bf16[8,5,128,128]{3,2,1,0:T(8,128)(2,1)}, bf16[8,5,128,128]{3,2,1,0:T(8,128)(2,1)}, u32[]{:S(2)}, u32[]{:S(2)}) collective-permute-start(bf16[8,5,128,128]{3,2,1,0:T(8,128)(2,1)} %get-tuple-element.97), channel_id=1, source_target_pairs={{0,1},{1,0},{2,3},{3,2},{4,5},{5,4},{6,7},{7,6}} | collective-permute-start | bytes 3932168 | tf_op jit(solution)/shard_map/ppermute | solution.py:405
  137.1 61.2 %collective-permute-start.30 = (bf16[8,5,128,128]{3,2,1,0:T(8,128)(2,1)}, bf16[8,5,128,128]{3,2,1,0:T(8,128)(2,1)}, u32[]{:S(2)}, u32[]{:S(2)}) collective-permute-start(bf16[8,5,128,128]{3,2,1,0:T(8,128)(2,1)} %get-tuple-element.97), channel_id=1, source_target_pairs={{0,3},{1,2},{2,1},{3,0},{4,7},{5,6},{6,5},{7,4}} | collective-permute-start | bytes 3932168 | tf_op jit(solution)/shard_map/ppermute | solution.py:405
  151.1 47.3 %collective-permute-start.31 = (bf16[8,5,128,128]{3,2,1,0:T(8,128)(2,1)}, bf16[8,5,128,128]{3,2,1,0:T(8,128)(2,1)}, u32[]{:S(2)}, u32[]{:S(2)}) collective-permute-start(bf16[8,5,128,128]{3,2,1,0:T(8,128)(2,1)} %get-tuple-element.96.refs_0_), channel_id=1, source_target_pairs={{0,4},{1,5},{2,6},{3,7},{4,0},{5,1},{6,2},{7,3}} | collective-permute-start | bytes 3932168 | tf_op jit(solution)/shard_map/ppermute | solution.py:405
  152.7 54.6 %collective-permute-start.22 = (bf16[8,5,128,128]{3,2,1,0:T(8,128)(2,1)}, bf16[8,5,128,128]{3,2,1,0:T(8,128)(2,1)S(1)}, u32[]{:S(2)}, u32[]{:S(2)}) collective-permute-start(bf16[8,5,128,128]{3,2,1,0:T(8,128)(2,1)} %get-tuple-element.94.refs_0_), channel_id=1, source_target_pairs={{0,2},{1,3},{2,0},{3,1},{4,6},{5,7},{6,4},{7,5}} | collective-permute-start | bytes 3932168 | tf_op jit(solution)/shard_map/ppermute | solution.py:405
  197.3 106.1 %collective-permute-start.49 = (bf16[4,2,1024,256]{3,2,1,0:T(8,128)(2,1)}, bf16[4,2,1024,256]{3,2,1,0:T(8,128)(2,1)}, u32[]{:S(2)}, u32[]{:S(2)}) collective-permute-start(bf16[4,2,1024,256]{3,2,1,0:T(8,128)(2,1)} %get-tuple-element.110), channel_id=1, source_target_pairs={{0,1},{1,0},{2,3},{3,2},{4,5},{5,4},{6,7},{7,6}} | collective-permute-start | bytes 12582920 | tf_op jit(solution)/shard_map/ppermute | solution.py:405
  197.4 30.7 %collective-permute-start.25 = (bf16[8,5,128,128]{3,2,1,0:T(8,128)(2,1)}, bf16[8,5,128,128]{3,2,1,0:T(8,128)(2,1)S(1)}, u32[]{:S(2)}, u32[]{:S(2)}) collective-permute-start(bf16[8,5,128,128]{3,2,1,0:T(8,128)(2,1)} %get-tuple-element.95), channel_id=1, source_target_pairs={{0,5},{1,4},{2,7},{3,6},{4,1},{5,0},{6,3},{7,2}} | collective-permute-start | bytes 3932168 | tf_op jit(solution)/shard_map/ppermute | solution.py:405
  198.3 31.1 %collective-permute-start.21 = (bf16[8,5,128,128]{3,2,1,0:T(8,128)(2,1)}, bf16[8,5,128,128]{3,2,1,0:T(8,128)(2,1)S(1)}, u32[]{:S(2)}, u32[]{:S(2)}) collective-permute-start(bf16[8,5,128,128]{3,2,1,0:T(8,128)(2,1)} %get-tuple-element.95), channel_id=1, source_target_pairs={{0,1},{1,0},{2,3},{3,2},{4,5},{5,4},{6,7},{7,6}} | collective-permute-start | bytes 3932168 | tf_op jit(solution)/shard_map/ppermute | solution.py:405
  198.4 36.4 %collective-permute-start.23 = (bf16[8,5,128,128]{3,2,1,0:T(8,128)(2,1)}, bf16[8,5,128,128]{3,2,1,0:T(8,128)(2,1)S(1)}, u32[]{:S(2)}, u32[]{:S(2)}) collective-permute-start(bf16[8,5,128,128]{3,2,1,0:T(8,128)(2,1)} %get-tuple-element.95), channel_id=1, source_target_pairs={{0,3},{1,2},{2,1},{3,0},{4,7},{5,6},{6,5},{7,4}} | collective-permute-start | bytes 3932168 | tf_op jit(solution)/shard_map/ppermute | solution.py:405
  207.2 50.2 %collective-permute-start.24 = (bf16[8,5,128,128]{3,2,1,0:T(8,128)(2,1)S(1)}, bf16[8,5,128,128]{3,2,1,0:T(8,128)(2,1)S(1)}, u32[]{:S(2)}, u32[]{:S(2)}) collective-permute-start(bf16[8,5,128,128]{3,2,1,0:T(8,128)(2,1)S(1)} %copy-done.27), channel_id=1, source_target_pairs={{0,4},{1,5},{2,6},{3,7},{4,0},{5,1},{6,2},{7,3}} | collective-permute-start | bytes 3932168 | tf_op jit(solution)/shard_map/ppermute | solution.py:405
  228.0 74.0 %collective-permute-start.51 = (bf16[128,8,192]{2,1,0:T(8,128)(2,1)}, bf16[128,8,192]{2,1,0:T(8,128)(2,1)S(1)}, u32[]{:S(2)}, u32[]{:S(2)}) collective-permute-start(bf16[128,8,192]{2,1,0:T(8,128)(2,1)} %get-tuple-element.112), channel_id=1, source_target_pairs={{0,1},{1,0},{2,3},{3,2},{4,5},{5,4},{6,7},{7,6}} | collective-permute-start | bytes 1179656 | tf_op jit(solution)/shard_map/ppermute | solution.py:405
  229.4 72.5 %collective-permute-start.50 = (bf16[128,8,128]{2,1,0:T(8,128)(2,1)}, bf16[128,8,128]{2,1,0:T(8,128)(2,1)S(1)}, u32[]{:S(2)}, u32[]{:S(2)}) collective-permute-start(bf16[128,8,128]{2,1,0:T(8,128)(2,1)} %get-tuple-element.111), channel_id=1, source_target_pairs={{0,1},{1,0},{2,3},{3,2},{4,5},{5,4},{6,7},{7,6}} | collective-permute-start | bytes 786440 | tf_op jit(solution)/shard_map/ppermute | solution.py:405
  234.8 67.8 %collective-permute-start.33 = (bf16[8,5,128,128]{3,2,1,0:T(8,128)(2,1)}, bf16[8,5,128,128]{3,2,1,0:T(8,128)(2,1)}, u32[]{:S(2)}, u32[]{:S(2)}) collective-permute-start(bf16[8,5,128,128]{3,2,1,0:T(8,128)(2,1)} %collective-permute-done.29.refs_2_), channel_id=1, source_target_pairs={{0,4},{1,5},{2,6},{3,7},{4,0},{5,1},{6,2},{7,3}} | collective-permute-start | bytes 3932168 | tf_op jit(solution)/shard_map/ppermute | solution.py:405
  257.4 45.2 %collective-permute-start.34 = (bf16[8,5,128,128]{3,2,1,0:T(8,128)(2,1)}, bf16[8,5,128,128]{3,2,1,0:T(8,128)(2,1)}, u32[]{:S(2)}, u32[]{:S(2)}) collective-permute-start(bf16[8,5,128,128]{3,2,1,0:T(8,128)(2,1)} %collective-permute-done.32.refs_5_), channel_id=1, source_target_pairs={{0,2},{1,3},{2,0},{3,1},{4,6},{5,7},{6,4},{7,5}} | collective-permute-start | bytes 3932168 | tf_op jit(solution)/shard_map/ppermute | solution.py:405
  302.0 86.5 %collective-permute-start.52 = (bf16[4,2,1024,256]{3,2,1,0:T(8,128)(2,1)}, bf16[4,2,1024,256]{3,2,1,0:T(8,128)(2,1)}, u32[]{:S(2)}, u32[]{:S(2)}) collective-permute-start(bf16[4,2,1024,256]{3,2,1,0:T(8,128)(2,1)} %get-tuple-element.119), channel_id=1, source_target_pairs={{0,1},{1,0},{2,3},{3,2},{4,5},{5,4},{6,7},{7,6}} | collective-permute-start | bytes 12582920 | tf_op jit(solution)/shard_map/ppermute | solution.py:405
  302.0 86.4 %collective-permute-start.54 = (bf16[128,8,192]{2,1,0:T(8,128)(2,1)}, bf16[128,8,192]{2,1,0:T(8,128)(2,1)S(1)}, u32[]{:S(2)}, u32[]{:S(2)}) collective-permute-start(bf16[128,8,192]{2,1,0:T(8,128)(2,1)} %get-tuple-element.121), channel_id=1, source_target_pairs={{0,1},{1,0},{2,3},{3,2},{4,5},{5,4},{6,7},{7,6}} | collective-permute-start | bytes 1179656 | tf_op jit(solution)/shard_map/ppermute | solution.py:405
  302.5 85.9 %collective-permute-start.53 = (bf16[128,8,128]{2,1,0:T(8,128)(2,1)}, bf16[128,8,128]{2,1,0:T(8,128)(2,1)}, u32[]{:S(2)}, u32[]{:S(2)}) collective-permute-start(bf16[128,8,128]{2,1,0:T(8,128)(2,1)} %get-tuple-element.120), channel_id=1, source_target_pairs={{0,1},{1,0},{2,3},{3,2},{4,5},{5,4},{6,7},{7,6}} | collective-permute-start | bytes 786440 | tf_op jit(solution)/shard_map/ppermute | solution.py:405
  302.6 85.9 %collective-permute-start.26 = (bf16[8,5,128,128]{3,2,1,0:T(8,128)(2,1)S(1)}, bf16[8,5,128,128]{3,2,1,0:T(8,128)(2,1)}, u32[]{:S(2)}, u32[]{:S(2)}) collective-permute-start(bf16[8,5,128,128]{3,2,1,0:T(8,128)(2,1)S(1)} %collective-permute-done.22.refs_2_), channel_id=1, source_target_pairs={{0,4},{1,5},{2,6},{3,7},{4,0},{5,1},{6,2},{7,3}} | collective-permute-start | bytes 3932168 | tf_op jit(solution)/shard_map/ppermute | solution.py:405
  303.4 85.0 %collective-permute-start.27 = (bf16[8,5,128,128]{3,2,1,0:T(8,128)(2,1)S(1)}, bf16[8,5,128,128]{3,2,1,0:T(8,128)(2,1)}, u32[]{:S(2)}, u32[]{:S(2)}) collective-permute-start(bf16[8,5,128,128]{3,2,1,0:T(8,128)(2,1)S(1)} %copy-done.30), channel_id=1, source_target_pairs={{0,2},{1,3},{2,0},{3,1},{4,6},{5,7},{6,4},{7,5}} | collective-permute-start | bytes 3932168 | tf_op jit(solution)/shard_map/ppermute | solution.py:405
  388.4 175.4 %collective-permute-start.55 = (bf16[8,2,1024,256]{3,2,1,0:T(8,128)(2,1)}, bf16[8,2,1024,256]{3,2,1,0:T(8,128)(2,1)}, u32[]{:S(2)}, u32[]{:S(2)}) collective-permute-start(bf16[8,2,1024,256]{3,2,1,0:T(8,128)(2,1)} %get-tuple-element.128), channel_id=1, source_target_pairs={{0,1},{1,0},{2,3},{3,2},{4,5},{5,4},{6,7},{7,6}} | collective-permute-start | bytes 25165832 | tf_op jit(solution)/shard_map/ppermute | solution.py:405
  473.2 144.3 %collective-permute-start.58 = (bf16[8,2,1024,256]{3,2,1,0:T(8,128)(2,1)}, bf16[8,2,1024,256]{3,2,1,0:T(8,128)(2,1)}, u32[]{:S(2)}, u32[]{:S(2)}) collective-permute-start(bf16[8,2,1024,256]{3,2,1,0:T(8,128)(2,1)} %get-tuple-element.137), channel_id=1, source_target_pairs={{0,1},{1,0},{2,3},{3,2},{4,5},{5,4},{6,7},{7,6}} | collective-permute-start | bytes 25165832 | tf_op jit(solution)/shard_map/ppermute | solution.py:405
  479.9 20.9 %collective-permute-start.14 = (bf16[4,5,128,128]{3,2,1,0:T(8,128)(2,1)}, bf16[4,5,128,128]{3,2,1,0:T(8,128)(2,1)S(1)}, u32[]{:S(2)}, u32[]{:S(2)}) collective-permute-start(bf16[4,5,128,128]{3,2,1,0:T(8,128)(2,1)} %get-tuple-element.93), channel_id=1, source_target_pairs={{0,1},{1,0},{2,3},{3,2},{4,5},{5,4},{6,7},{7,6}} | collective-permute-start | bytes 1966088 | tf_op jit(solution)/shard_map/ppermute | solution.py:405
  500.7 24.6 %collective-permute-start.8 = (bf16[4,5,128,128]{3,2,1,0:T(8,128)(2,1)}, bf16[4,5,128,128]{3,2,1,0:T(8,128)(2,1)S(1)}, u32[]{:S(2)}, u32[]{:S(2)}) collective-permute-start(bf16[4,5,128,128]{3,2,1,0:T(8,128)(2,1)} %get-tuple-element.88.refs_0_), channel_id=1, source_target_pairs={{0,2},{1,3},{2,0},{3,1},{4,6},{5,7},{6,4},{7,5}} | collective-permute-start | bytes 1966088 | tf_op jit(solution)/shard_map/ppermute | solution.py:405
  513.0 29.5 %collective-permute-start.10 = (bf16[4,5,128,128]{3,2,1,0:T(8,128)(2,1)}, bf16[4,5,128,128]{3,2,1,0:T(8,128)(2,1)}, u32[]{:S(2)}, u32[]{:S(2)}) collective-permute-start(bf16[4,5,128,128]{3,2,1,0:T(8,128)(2,1)} %get-tuple-element.88.refs_0_), channel_id=1, source_target_pairs={{0,4},{1,5},{2,6},{3,7},{4,0},{5,1},{6,2},{7,3}} | collective-permute-start | bytes 1966088 | tf_op jit(solution)/shard_map/ppermute | solution.py:405
  525.3 19.4 %collective-permute-start.57 = (bf16[128,16,192]{0,2,1:T(8,128)(2,1)S(1)}, bf16[128,16,192]{0,2,1:T(8,128)(2,1)S(1)}, u32[]{:S(2)}, u32[]{:S(2)}) collective-permute-start(bf16[128,16,192]{0,2,1:T(8,128)(2,1)S(1)} %copy.69), channel_id=1, source_target_pairs={{0,1},{1,0},{2,3},{3,2},{4,5},{5,4},{6,7},{7,6}} | collective-permute-start | bytes 2359304 | tf_op jit(solution)/shard_map/ppermute | solution.py:405
  560.3 56.7 %collective-permute-start.9 = (bf16[4,5,128,128]{3,2,1,0:T(8,128)(2,1)}, bf16[4,5,128,128]{3,2,1,0:T(8,128)(2,1)S(1)}, u32[]{:S(2)}, u32[]{:S(2)}) collective-permute-start(bf16[4,5,128,128]{3,2,1,0:T(8,128)(2,1)} %get-tuple-element.89), channel_id=1, source_target_pairs={{0,3},{1,2},{2,1},{3,0},{4,7},{5,6},{6,5},{7,4}} | collective-permute-start | bytes 1966088 | tf_op jit(solution)/shard_map/ppermute | solution.py:405
  561.8 55.7 %collective-permute-start.12 = (bf16[4,5,128,128]{3,2,1,0:T(8,128)(2,1)S(1)}, bf16[4,5,128,128]{3,2,1,0:T(8,128)(2,1)S(1)}, u32[]{:S(2)}, u32[]{:S(2)}) collective-permute-start(bf16[4,5,128,128]{3,2,1,0:T(8,128)(2,1)S(1)} %collective-permute-done.8.refs_2_), channel_id=1, source_target_pairs={{0,4},{1,5},{2,6},{3,7},{4,0},{5,1},{6,2},{7,3}} | collective-permute-start | bytes 1966088 | tf_op jit(solution)/shard_map/ppermute | solution.py:405
  562.1 55.4 %collective-permute-start.13 = (bf16[4,5,128,128]{3,2,1,0:T(8,128)(2,1)}, bf16[4,5,128,128]{3,2,1,0:T(8,128)(2,1)S(1)}, u32[]{:S(2)}, u32[]{:S(2)}) collective-permute-start(bf16[4,5,128,128]{3,2,1,0:T(8,128)(2,1)} %collective-permute-done.11.refs_5_), channel_id=1, source_target_pairs={{0,2},{1,3},{2,0},{3,1},{4,6},{5,7},{6,4},{7,5}} | collective-permute-start | bytes 1966088 | tf_op jit(solution)/shard_map/ppermute | solution.py:405
  563.8 53.8 %collective-permute-start.59 = (bf16[128,16,128]{2,1,0:T(8,128)(2,1)}, bf16[128,16,128]{2,1,0:T(8,128)(2,1)S(1)}, u32[]{:S(2)}, u32[]{:S(2)}) collective-permute-start(bf16[128,16,128]{2,1,0:T(8,128)(2,1)} %get-tuple-element.138), channel_id=1, source_target_pairs={{0,1},{1,0},{2,3},{3,2},{4,5},{5,4},{6,7},{7,6}} | collective-permute-start | bytes 1572872 | tf_op jit(solution)/shard_map/ppermute | solution.py:405
  617.0 65.9 %collective-permute-start.64 = (bf16[4,2,1024,256]{3,2,1,0:T(8,128)(2,1)}, bf16[4,2,1024,256]{3,2,1,0:T(8,128)(2,1)}, u32[]{:S(2)}, u32[]{:S(2)}) collective-permute-start(bf16[4,2,1024,256]{3,2,1,0:T(8,128)(2,1)} %get-tuple-element.147), channel_id=1, source_target_pairs={{0,1},{1,0},{2,3},{3,2},{4,5},{5,4},{6,7},{7,6}} | collective-permute-start | bytes 12582920 | tf_op jit(solution)/shard_map/ppermute | solution.py:405
  671.7 21.6 %collective-permute-start.61 = (bf16[4,2,1024,256]{3,2,1,0:T(8,128)(2,1)}, bf16[4,2,1024,256]{3,2,1,0:T(8,128)(2,1)}, u32[]{:S(2)}, u32[]{:S(2)}) collective-permute-start(bf16[4,2,1024,256]{3,2,1,0:T(8,128)(2,1)} %get-tuple-element.144), channel_id=1, source_target_pairs={{0,1},{1,0},{2,3},{3,2},{4,5},{5,4},{6,7},{7,6}} | collective-permute-start | bytes 12582920 | tf_op jit(solution)/shard_map/ppermute | solution.py:405
  (63 other events, 1213.9 us)

commit v3 on v2

--- a/solution.py
+++ b/solution.py
@@ -21,7 +21,7 @@
 ROWS = 32
 NEG = -1e30
 BF = jnp.bfloat16
-GROUPS = (1, 1, 2, 2, 1, 1)
+GROUPS = (1, 1, 1, 1, 1, 2, 1)
 F32 = jnp.float32
 
 
@@ -176,8 +176,7 @@
         kr[k, :, :D] = keys[:, k * D:(k + 1) * D]
         vs[k] = vals[:, k * D:(k + 1) * D]
 
-    low = lax.broadcasted_iota(jnp.int32, (8, QB), 0)
-    col = lax.broadcasted_iota(jnp.int32, (8, QB), 1)
+    upper = lax.broadcasted_iota(jnp.int32, (QB, QB), 0) <= lax.broadcasted_iota(jnp.int32, (QB, QB), 1)
 
     @pl.loop(0, 2)
     def _(k):
@@ -185,22 +184,20 @@
             q_i = qa[k, i * QB:(i + 1) * QB, :]
             d_i = do[k, i * QB:(i + 1) * QB, :]
             base = QB * (i * (i + 1) // 2)
-            rows = slice(0, (i + 1) * QB)
-            out = slice(base, base + (i + 1) * QB)
-            st[out, :] = dot(kr[k, rows, :], q_i, 1, 1)
-            dp[out, :] = dot(vs[k, rows, :], d_i, 1, 1)
+            for t in range(i + 1):
+                rows = slice(t * QB, (t + 1) * QB)
+                out = slice(base + t * QB, base + (t + 1) * QB)
+                sc = dot(kr[k, rows, :], q_i, 1, 1)
+                st[out, :] = jnp.where(upper, sc, NEG) if t == i else sc
+                dp[out, :] = dot(vs[k, rows, :], d_i, 1, 1)
 
         def soften(i):
             n = (i + 1) * QB
             base = QB * (i * (i + 1) // 2)
-            mxs = [None] * 4
-            for r0 in range(0, n, 8):
-                x = st[base + r0:base + r0 + 8, :]
-                if r0 >= i * QB:
-                    x = jnp.where(low + (r0 - i * QB) <= col, x, NEG)
-                    st[base + r0:base + r0 + 8, :] = x
-                a = r0 // 8 % 4
-                mxs[a] = x if mxs[a] is None else jnp.maximum(mxs[a], x)
+            mxs = [st[base + 8 * a:base + 8 * a + 8, :] for a in range(4)]
+            for r0 in range(32, n, 32):
+                for a in range(4):
+                    mxs[a] = jnp.maximum(mxs[a], st[base + r0 + 8 * a:base + r0 + 8 * a + 8, :])
             mx = jnp.maximum(jnp.maximum(mxs[0], mxs[1]), jnp.maximum(mxs[2], mxs[3]))
             mx = jnp.max(mx, axis=0, keepdims=True)
             ls = jnp.zeros((8, QB), F32)
@@ -393,7 +390,7 @@
                        pl.BlockSpec((TB, HC, D), at), pl.BlockSpec((TB, HC, D + R), at)]),
         out_shape=big_shapes(),
         input_output_aliases={5 + b: b for b in range(4)},
-        compiler_params=pltpu.CompilerParams(vmem_limit_bytes=40 * 2 ** 20),
+        compiler_params=pltpu.CompilerParams(vmem_limit_bytes=60 * 2 ** 20),
         name="last",
         cost_estimate=pl.CostEstimate(flops=2 * 10 ** 9, bytes_accessed=10 ** 7, transcendentals=0),
     )(core, c_t, *prev, *big)

time: 724 us -> 706 us (0.975)
  waiting for transfers between devices: 211 us -> 199 us
    ppermute x69 -> x79, waiting for transfers between devices: 211 us -> 199 us  [hop(): return lax.ppermute(x, 'cp', perm)]
    pallas_call x6 -> x7, Pallas kernels: 359 us -> 349 us  [main_chunk(): pl.pallas_call(functools.partial(main_kernel, big is not None, lead, scor...]
    unnamed x86 -> x116, local copies, waits for them, and re-layouts: 22.1 us -> 18.8 us
    pallas_call x6 -> x7, Pallas kernels: 19.2 us -> 21.4 us  [pack_chunk(): pl.pallas_call(pack_kernel, grid_spec=pltpu.PrefetchScalarGridSpec(num_sc...]
    ppermute x69 -> x79, starting transfers between devices: 60.9 us -> 62 us  [hop(): return lax.ppermute(x, 'cp', perm)]
  transfers between devices with their start and end apart: 69 -> 79, of which waited for: 25 -> 24; matrix products, arithmetic and copies ran while one was open for 2% -> 1% of each run, Pallas kernels for 54% -> 55%
where the time goes in v3:
time: 706 us; the launch traced here: 696 us
  Pallas kernels  395 us (56%)
  waiting for transfers between devices  199 us (28%)
  starting transfers between devices  62 us (9%)
  local copies, waits for them, and re-layouts  34.3 us (5%)
    pallas_call x7, Pallas kernels, main_chunk(): pl.pallas_call(functools.partial(main_kernel, big is not None, lead, scor...  349 us
    ppermute x79, waiting for transfers between devices, hop(): return lax.ppermute(x, 'cp', perm)  199 us
    ppermute x79, starting transfers between devices, hop(): return lax.ppermute(x, 'cp', perm)  62 us
    pallas_call x7, Pallas kernels, pack_chunk(): pl.pallas_call(pack_kernel, grid_spec=pltpu.PrefetchScalarGridSpec(num_sc...  21.4 us
    pallas_call x2, Pallas kernels, last_chunk(): pl.pallas_call(functools.partial(last_kernel, score_scale), grid_spec=plt...  20.9 us
    unnamed x116, local copies, waits for them, and re-layouts  18.8 us
  transfers between devices with their start and end apart: 79, of which 24 were waited for; matrix products, arithmetic and copies ran while one was open for 1% of the time, Pallas kernels for 55%

profile of v3, /device:TPU:0, one launch (start us, length us, event | category | flops | bytes accessed | tf_op | source)
XLA Modules:
  0.0 696.2 jit_solution(3679635412757085791)
XLA Ops:
  4.4 10.0 %copy.63.qo_ref.qp_ref = bf16[128,128,192]{2,1,0:T(8,128)(2,1)} copy(bf16[128,128,192]{1,2,0:T(8,128)(2,1)} %param.6) | data formatting | bytes 12582912 | tf_op jit(solution)/shard_map/optimization_barrier | solution.py:414
  14.4 2.9 pack.13
  17.3 2.8 collective-permute-start.50
  23.7 15.8 %collective-permute-done.1.refs_2_ = bf16[128,640]{1,0:T(8,128)(2,1)S(1)} collective-permute-done((bf16[128,640]{1,0:T(8,128)(2,1)S(1)}, bf16[128,640]{1,0:T(8,128)(2,1)S(1)}, u32[]{:S(2)}, u32[]{:S(2)}) %collective-permute-start.1) | collective-permute-done | bytes 163872 | tf_op jit(solution)/shard_map/ppermute | solution.py:402
  39.5 3.0 collective-permute-start.5
  42.5 2.9 collective-permute-start.6
  46.7 2.9 pack.12
  52.8 12.0 %collective-permute-done.53.refs_5_ = bf16[4,5,128,128]{3,2,1,0:T(8,128)(2,1)S(1)} collective-permute-done((bf16[4,5,128,128]{3,2,1,0:T(8,128)(2,1)}, bf16[4,5,128,128]{3,2,1,0:T(8,128)(2,1)S(1)}, u32[]{:S(2)}, u32[]{:S(2)}) %collective-permute-start.53) | collective-permute-done | bytes 655392 | tf_op jit(solution)/shard_map/ppermute | solution.py:402
  65.6 2.9 pack.11
  69.8 9.0 %collective-permute-done.52.refs_4_ = bf16[4,5,128,128]{3,2,1,0:T(8,128)(2,1)} collective-permute-done((bf16[4,5,128,128]{3,2,1,0:T(8,128)(2,1)S(1)}, bf16[4,5,128,128]{3,2,1,0:T(8,128)(2,1)}, u32[]{:S(2)}, u32[]{:S(2)}) %collective-permute-start.52) | collective-permute-done | bytes 655392 | tf_op jit(solution)/shard_map/ppermute | solution.py:402
  79.7 2.1 collective-permute-done.43.refs_2_
  82.3 10.6 %collective-permute-done.46.refs_5_ = bf16[4,5,128,128]{3,2,1,0:T(8,128)(2,1)S(1)} collective-permute-done((bf16[4,5,128,128]{3,2,1,0:T(8,128)(2,1)}, bf16[4,5,128,128]{3,2,1,0:T(8,128)(2,1)S(1)}, u32[]{:S(2)}, u32[]{:S(2)}) %collective-permute-start.46) | collective-permute-done | bytes 655392 | tf_op jit(solution)/shard_map/ppermute | solution.py:402
  95.9 10.8 %collective-permute-done.45.refs_4_ = bf16[4,5,128,128]{3,2,1,0:T(8,128)(2,1)S(1)} collective-permute-done((bf16[4,5,128,128]{3,2,1,0:T(8,128)(2,1)S(1)}, bf16[4,5,128,128]{3,2,1,0:T(8,128)(2,1)S(1)}, u32[]{:S(2)}, u32[]{:S(2)}) %collective-permute-start.45) | collective-permute-done | bytes 655392 | tf_op jit(solution)/shard_map/ppermute | solution.py:402
  107.6 2.1 collective-permute-done.36.refs_2_
  110.3 3.0 prep.1
  113.3 3.0 pack.10
  116.3 4.7 collective-permute-done.39.refs_5_
  125.5 9.5 %collective-permute-done.54.refs_6_ = bf16[4,5,128,128]{3,2,1,0:T(8,128)(2,1)} collective-permute-done((bf16[4,5,128,128]{3,2,1,0:T(8,128)(2,1)}, bf16[4,5,128,128]{3,2,1,0:T(8,128)(2,1)}, u32[]{:S(2)}, u32[]{:S(2)}) %collective-permute-start.54) | collective-permute-done | bytes 655392 | tf_op jit(solution)/shard_map/ppermute | solution.py:402
  135.8 2.1 collective-permute-done.55.refs_7_
  140.1 41.2 %mla_chunk.7 = (f32[512,128,128]{2,1,0:T(8,128)}, f32[512,128,128]{2,1,0:T(8,128)}, bf16[128,128,128]{2,1,0:T(8,128)(2,1)}, bf16[128,128,192]{2,1,0:T(8,128)(2,1...) custom-call(s32[1]{0:T(128)} %bitcast.me_ref, ...), custom_call_target="tpu_custom_call" | custom-call | flops 24999999488 | bytes 20000000 | tf_op jit(solution)/shard_map/mla_chunk/pallas_call | solution.py:324
  181.3 3.0 pack.9
  187.9 41.4 %mla_chunk.8 = (f32[512,128,128]{2,1,0:T(8,128)}, f32[512,128,128]{2,1,0:T(8,128)}, bf16[128,128,128]{2,1,0:T(8,128)(2,1)}, bf16[128,128,192]{2,1,0:T(8,128)(2,1...) custom-call(s32[1]{0:T(128)} %bitcast.me_ref, ...), custom_call_target="tpu_custom_call", output_to_operand_aliasing={{0}: (16, {}), {1}: (17, {}), {2}: (18, {}), {3}: (19, {})} | custom-call | flops 24999999488 | bytes 20000000 | tf_op jit(solution)/shard_map/mla_chunk/pallas_call | solution.py:324
  230.7 1.9 collective-permute-start.23
  232.6 13.4 %collective-permute-done.25.refs_5_ = bf16[4,5,128,128]{3,2,1,0:T(8,128)(2,1)S(1)} collective-permute-done((bf16[4,5,128,128]{3,2,1,0:T(8,128)(2,1)}, bf16[4,5,128,128]{3,2,1,0:T(8,128)(2,1)S(1)}, u32[]{:S(2)}, u32[]{:S(2)}) %collective-permute-start.25) | collective-permute-done | bytes 655392 | tf_op jit(solution)/shard_map/ppermute | solution.py:402
  248.0 2.0 collective-permute-start.41
  250.0 13.6 %collective-permute-done.24.refs_4_ = bf16[4,5,128,128]{3,2,1,0:T(8,128)(2,1)S(1)} collective-permute-done((bf16[4,5,128,128]{3,2,1,0:T(8,128)(2,1)S(1)}, bf16[4,5,128,128]{3,2,1,0:T(8,128)(2,1)S(1)}, u32[]{:S(2)}, u32[]{:S(2)}) %collective-permute-start.24) | collective-permute-done | bytes 655392 | tf_op jit(solution)/shard_map/ppermute | solution.py:402
  263.6 13.8 %collective-permute-done.40.refs_6_ = bf16[4,5,128,128]{3,2,1,0:T(8,128)(2,1)S(1)} collective-permute-done((bf16[4,5,128,128]{3,2,1,0:T(8,128)(2,1)S(1)}, bf16[4,5,128,128]{3,2,1,0:T(8,128)(2,1)S(1)}, u32[]{:S(2)}, u32[]{:S(2)}) %collective-permute-start.40) | collective-permute-done | bytes 655392 | tf_op jit(solution)/shard_map/ppermute | solution.py:402
  278.3 3.8 pack.8
  283.3 1.9 collective-permute-start.34
  285.7 46.3 %mla_chunk.9 = (f32[512,128,128]{2,1,0:T(8,128)}, f32[512,128,128]{2,1,0:T(8,128)}, bf16[128,128,128]{2,1,0:T(8,128)(2,1)}, bf16[128,128,192]{2,1,0:T(8,128)(2,1...) custom-call(s32[1]{0:T(128)} %bitcast.me_ref, ...), custom_call_target="tpu_custom_call", output_to_operand_aliasing={{0}: (19, {}), {1}: (20, {}), {2}: (21, {}), {3}: (22, {})} | custom-call | flops 24999999488 | bytes 20000000 | tf_op jit(solution)/shard_map/mla_chunk/pallas_call | solution.py:324
  336.3 46.5 %mla_chunk.10 = (f32[512,128,128]{2,1,0:T(8,128)}, f32[512,128,128]{2,1,0:T(8,128)}, bf16[128,128,128]{2,1,0:T(8,128)(2,1)}, bf16[128,128,192]{2,1,0:T(8,128)(2,...) custom-call(s32[1]{0:T(128)} %bitcast.me_ref, ...), custom_call_target="tpu_custom_call", output_to_operand_aliasing={{0}: (19, {}), {1}: (20, {}), {2}: (21, {}), {3}: (22, {})} | custom-call | flops 24999999488 | bytes 20000000 | tf_op jit(solution)/shard_map/mla_chunk/pallas_call | solution.py:324
  385.6 6.6 collective-permute-done.14.refs_1_
  392.3 22.2 %collective-permute-done.16.refs_3_ = bf16[8,5,128,128]{3,2,1,0:T(8,128)(2,1)S(1)} collective-permute-done((bf16[8,5,128,128]{3,2,1,0:T(8,128)(2,1)}, bf16[8,5,128,128]{3,2,1,0:T(8,128)(2,1)S(1)}, u32[]{:S(2)}, u32[]{:S(2)}) %collective-permute-start.16) | collective-permute-done | bytes 1310752 | tf_op jit(solution)/shard_map/ppermute | solution.py:402
  419.0 46.2 %mla_chunk.11 = (f32[512,128,128]{2,1,0:T(8,128)}, f32[512,128,128]{2,1,0:T(8,128)}, bf16[128,128,128]{2,1,0:T(8,128)(2,1)}, bf16[128,128,192]{2,1,0:T(8,128)(2,...) custom-call(s32[1]{0:T(128)} %bitcast.me_ref, ...), custom_call_target="tpu_custom_call", output_to_operand_aliasing={{0}: (19, {}), {1}: (20, {}), {2}: (21, {}), {3}: (22, {})} | custom-call | flops 24999999488 | bytes 20000000 | tf_op jit(solution)/shard_map/mla_chunk/pallas_call | solution.py:324
  466.1 81.4 %mla_chunk.12 = (f32[512,128,128]{2,1,0:T(8,128)}, f32[512,128,128]{2,1,0:T(8,128)}, bf16[128,128,128]{2,1,0:T(8,128)(2,1)}, bf16[128,128,192]{2,1,0:T(8,128)(2,...) custom-call(s32[1]{0:T(128)} %bitcast.me_ref, ...), custom_call_target="tpu_custom_call", output_to_operand_aliasing={{0}: (19, {}), {1}: (20, {}), {2}: (21, {}), {3}: (22, {})} | custom-call | flops 49999998976 | bytes 20000000 | tf_op jit(solution)/shard_map/mla_chunk/pallas_call | solution.py:324
  548.0 2.9 pack.7
  550.9 1.8 collective-permute-start.8
  554.5 13.3 %collective-permute-done.8.refs_2_ = bf16[4,5,128,128]{3,2,1,0:T(8,128)(2,1)S(1)} collective-permute-done((bf16[4,5,128,128]{3,2,1,0:T(8,128)(2,1)}, bf16[4,5,128,128]{3,2,1,0:T(8,128)(2,1)S(1)}, u32[]{:S(2)}, u32[]{:S(2)}) %collective-permute-start.8) | collective-permute-done | bytes 655392 | tf_op jit(solution)/shard_map/ppermute | solution.py:402
  567.8 1.7 collective-permute-done.11.refs_5_
  569.8 14.1 %collective-permute-done.10.refs_4_ = bf16[4,5,128,128]{3,2,1,0:T(8,128)(2,1)S(1)} collective-permute-done((bf16[4,5,128,128]{3,2,1,0:T(8,128)(2,1)}, bf16[4,5,128,128]{3,2,1,0:T(8,128)(2,1)S(1)}, u32[]{:S(2)}, u32[]{:S(2)}) %collective-permute-start.10) | collective-permute-done | bytes 655392 | tf_op jit(solution)/shard_map/ppermute | solution.py:402
  584.0 1.8 collective-permute-start.12
  586.6 14.2 %collective-permute-done.12.refs_6_ = bf16[4,5,128,128]{3,2,1,0:T(8,128)(2,1)S(1)} collective-permute-done((bf16[4,5,128,128]{3,2,1,0:T(8,128)(2,1)S(1)}, bf16[4,5,128,128]{3,2,1,0:T(8,128)(2,1)S(1)}, u32[]{:S(2)}, u32[]{:S(2)}) %collective-permute-start.12) | collective-permute-done | bytes 655392 | tf_op jit(solution)/shard_map/ppermute | solution.py:402
  603.4 46.4 %mla_chunk.13 = (f32[512,128,128]{2,1,0:T(8,128)}, f32[512,128,128]{2,1,0:T(8,128)}, bf16[128,128,128]{2,1,0:T(8,128)(2,1)}, bf16[128,128,192]{2,1,0:T(8,128)(2,...) custom-call(s32[1]{0:T(128)} %bitcast.me_ref, ...), custom_call_target="tpu_custom_call", output_to_operand_aliasing={{0}: (19, {}), {1}: (20, {}), {2}: (21, {}), {3}: (22, {})} | custom-call | flops 24999999488 | bytes 20000000 | tf_op jit(solution)/shard_map/mla_chunk/pallas_call | solution.py:324
  654.0 4.3 collective-permute-done.76
  658.5 1.7 copy.78.dq_in
  663.9 13.0 %last.2 = (f32[512,128,128]{2,1,0:T(8,128)}, f32[512,128,128]{2,1,0:T(8,128)}, bf16[128,128,128]{2,1,0:T(8,128)(2,1)}, bf16[128,128,192]{2,1,0:T(8,128)(2,1)}) custom-call(s32[1]{0:T(128)} %select_n.17.core_ref, bf16[512,1024]{1,0:T(8,128)(2,1)} %get-tuple-element.97.refs_9_.ct_ref, ...), custom_call_target="tpu_custom_call", output_to_operand_aliasing={{0}: (5, {}), {1}: (6, {}), {2}: (7, {}), {3}: (8, {})} | custom-call | flops 2000000000 | bytes 10000000 | tf_op jit(solution)/shard_map/last/pallas_call | solution.py:381
  677.8 7.9 %last.3 = (f32[512,128,128]{2,1,0:T(8,128)}, f32[512,128,128]{2,1,0:T(8,128)}, bf16[128,128,128]{2,1,0:T(8,128)(2,1)}, bf16[128,128,192]{2,1,0:T(8,128)(2,1)}) custom-call(s32[1]{0:T(128)} %select_n.17.core_ref, bf16[512,1024]{1,0:T(8,128)(2,1)} %get-tuple-element.97.refs_9_.ct_ref, ...), custom_call_target="tpu_custom_call", output_to_operand_aliasing={{0}: (5, {}), {1}: (6, {}), {2}: (7, {}), {3}: (8, {})} | custom-call | flops 2000000000 | bytes 10000000 | tf_op jit(solution)/shard_map/last/pallas_call | solution.py:381
  685.7 10.1 %copy.81 = bf16[128,128,192]{1,2,0:T(8,128)(2,1)} copy(bf16[128,128,192]{2,1,0:T(8,128)(2,1)} %get-tuple-element.193) | data formatting | bytes 12582912
  (258 shorter events, 64.1 us)
Async XLA Ops:
  17.3 34.0 %collective-permute-start.50 = (bf16[4,5,128,128]{3,2,1,0:T(8,128)(2,1)}, bf16[4,5,128,128]{3,2,1,0:T(8,128)(2,1)S(1)}, u32[]{:S(2)}, u32[]{:S(2)}) collective-permute-start(bf16[4,5,128,128]{3,2,1,0:T(8,128)(2,1)} %get-tuple-element.113.refs_0_), channel_id=1, source_target_pairs={{0,2},{1,3},{2,0},{3,1},{4,6},{5,7},{6,4},{7,5}} | collective-permute-start | bytes 1966088 | tf_op jit(solution)/shard_map/ppermute | solution.py:402
  21.4 24.0 %collective-permute-start.3 = (bf16[128,640]{1,0:T(8,128)(2,1)S(1)}, bf16[128,640]{1,0:T(8,128)(2,1)S(1)}, u32[]{:S(2)}, u32[]{:S(2)}) collective-permute-start(bf16[128,640]{1,0:T(8,128)(2,1)S(1)} %maximum_maximum_fusion.refs_0_), channel_id=1, source_target_pairs={{0,4},{1,5},{2,6},{3,7},{4,0},{5,1},{6,2},{7,3}} | collective-permute-start | bytes 491528 | tf_op jit(solution)/shard_map/ppermute | solution.py:402
  50.3 28.5 %collective-permute-start.52 = (bf16[4,5,128,128]{3,2,1,0:T(8,128)(2,1)S(1)}, bf16[4,5,128,128]{3,2,1,0:T(8,128)(2,1)}, u32[]{:S(2)}, u32[]{:S(2)}) collective-permute-start(bf16[4,5,128,128]{3,2,1,0:T(8,128)(2,1)S(1)} %copy-done.52), channel_id=1, source_target_pairs={{0,4},{1,5},{2,6},{3,7},{4,0},{5,1},{6,2},{7,3}} | collective-permute-start | bytes 1966088 | tf_op jit(solution)/shard_map/ppermute | solution.py:402
  51.3 30.4 %collective-permute-start.43 = (bf16[4,5,128,128]{3,2,1,0:T(8,128)(2,1)}, bf16[4,5,128,128]{3,2,1,0:T(8,128)(2,1)}, u32[]{:S(2)}, u32[]{:S(2)}) collective-permute-start(bf16[4,5,128,128]{3,2,1,0:T(8,128)(2,1)} %get-tuple-element.111.refs_0_), channel_id=1, source_target_pairs={{0,2},{1,3},{2,0},{3,1},{4,6},{5,7},{6,4},{7,5}} | collective-permute-start | bytes 1966088 | tf_op jit(solution)/shard_map/ppermute | solution.py:402
  64.8 28.1 %collective-permute-start.46 = (bf16[4,5,128,128]{3,2,1,0:T(8,128)(2,1)}, bf16[4,5,128,128]{3,2,1,0:T(8,128)(2,1)S(1)}, u32[]{:S(2)}, u32[]{:S(2)}) collective-permute-start(bf16[4,5,128,128]{3,2,1,0:T(8,128)(2,1)} %get-tuple-element.112), channel_id=1, source_target_pairs={{0,5},{1,4},{2,7},{3,6},{4,1},{5,0},{6,3},{7,2}} | collective-permute-start | bytes 1966088 | tf_op jit(solution)/shard_map/ppermute | solution.py:402
  65.4 28.8 %collective-permute-start.42 = (bf16[4,5,128,128]{3,2,1,0:T(8,128)(2,1)}, bf16[4,5,128,128]{3,2,1,0:T(8,128)(2,1)}, u32[]{:S(2)}, u32[]{:S(2)}) collective-permute-start(bf16[4,5,128,128]{3,2,1,0:T(8,128)(2,1)} %get-tuple-element.112), channel_id=1, source_target_pairs={{0,1},{1,0},{2,3},{3,2},{4,5},{5,4},{6,7},{7,6}} | collective-permute-start | bytes 1966088 | tf_op jit(solution)/shard_map/ppermute | solution.py:402
  68.6 26.0 %collective-permute-start.44 = (bf16[4,5,128,128]{3,2,1,0:T(8,128)(2,1)}, bf16[4,5,128,128]{3,2,1,0:T(8,128)(2,1)S(1)}, u32[]{:S(2)}, u32[]{:S(2)}) collective-permute-start(bf16[4,5,128,128]{3,2,1,0:T(8,128)(2,1)} %get-tuple-element.112), channel_id=1, source_target_pairs={{0,3},{1,2},{2,1},{3,0},{4,7},{5,6},{6,5},{7,4}} | collective-permute-start | bytes 1966088 | tf_op jit(solution)/shard_map/ppermute | solution.py:402
  78.8 28.0 %collective-permute-start.45 = (bf16[4,5,128,128]{3,2,1,0:T(8,128)(2,1)S(1)}, bf16[4,5,128,128]{3,2,1,0:T(8,128)(2,1)S(1)}, u32[]{:S(2)}, u32[]{:S(2)}) collective-permute-start(bf16[4,5,128,128]{3,2,1,0:T(8,128)(2,1)S(1)} %copy-done.17), channel_id=1, source_target_pairs={{0,4},{1,5},{2,6},{3,7},{4,0},{5,1},{6,2},{7,3}} | collective-permute-start | bytes 1966088 | tf_op jit(solution)/shard_map/ppermute | solution.py:402
  81.7 28.0 %collective-permute-start.36 = (bf16[4,5,128,128]{3,2,1,0:T(8,128)(2,1)}, bf16[4,5,128,128]{3,2,1,0:T(8,128)(2,1)S(1)}, u32[]{:S(2)}, u32[]{:S(2)}) collective-permute-start(bf16[4,5,128,128]{3,2,1,0:T(8,128)(2,1)} %get-tuple-element.109.refs_0_), channel_id=1, source_target_pairs={{0,2},{1,3},{2,0},{3,1},{4,6},{5,7},{6,4},{7,5}} | collective-permute-start | bytes 1966088 | tf_op jit(solution)/shard_map/ppermute | solution.py:402
  93.7 27.2 %collective-permute-start.39 = (bf16[4,5,128,128]{3,2,1,0:T(8,128)(2,1)}, bf16[4,5,128,128]{3,2,1,0:T(8,128)(2,1)S(1)}, u32[]{:S(2)}, u32[]{:S(2)}) collective-permute-start(bf16[4,5,128,128]{3,2,1,0:T(8,128)(2,1)} %get-tuple-element.110), channel_id=1, source_target_pairs={{0,5},{1,4},{2,7},{3,6},{4,1},{5,0},{6,3},{7,2}} | collective-permute-start | bytes 1966088 | tf_op jit(solution)/shard_map/ppermute | solution.py:402
  94.2 27.5 %collective-permute-start.35 = (bf16[4,5,128,128]{3,2,1,0:T(8,128)(2,1)}, bf16[4,5,128,128]{3,2,1,0:T(8,128)(2,1)S(1)}, u32[]{:S(2)}, u32[]{:S(2)}) collective-permute-start(bf16[4,5,128,128]{3,2,1,0:T(8,128)(2,1)} %get-tuple-element.110), channel_id=1, source_target_pairs={{0,1},{1,0},{2,3},{3,2},{4,5},{5,4},{6,7},{7,6}} | collective-permute-start | bytes 1966088 | tf_op jit(solution)/shard_map/ppermute | solution.py:402
  94.5 28.7 %collective-permute-start.37 = (bf16[4,5,128,128]{3,2,1,0:T(8,128)(2,1)}, bf16[4,5,128,128]{3,2,1,0:T(8,128)(2,1)S(1)}, u32[]{:S(2)}, u32[]{:S(2)}) collective-permute-start(bf16[4,5,128,128]{3,2,1,0:T(8,128)(2,1)} %get-tuple-element.110), channel_id=1, source_target_pairs={{0,3},{1,2},{2,1},{3,0},{4,7},{5,6},{6,5},{7,4}} | collective-permute-start | bytes 1966088 | tf_op jit(solution)/shard_map/ppermute | solution.py:402
  106.8 28.2 %collective-permute-start.54 = (bf16[4,5,128,128]{3,2,1,0:T(8,128)(2,1)}, bf16[4,5,128,128]{3,2,1,0:T(8,128)(2,1)}, u32[]{:S(2)}, u32[]{:S(2)}) collective-permute-start(bf16[4,5,128,128]{3,2,1,0:T(8,128)(2,1)} %copy-done.53), channel_id=1, source_target_pairs={{0,4},{1,5},{2,6},{3,7},{4,0},{5,1},{6,2},{7,3}} | collective-permute-start | bytes 1966088 | tf_op jit(solution)/shard_map/ppermute | solution.py:402
  109.7 28.2 %collective-permute-start.55 = (bf16[4,5,128,128]{3,2,1,0:T(8,128)(2,1)}, bf16[4,5,128,128]{3,2,1,0:T(8,128)(2,1)}, u32[]{:S(2)}, u32[]{:S(2)}) collective-permute-start(bf16[4,5,128,128]{3,2,1,0:T(8,128)(2,1)} %copy-done.54), channel_id=1, source_target_pairs={{0,2},{1,3},{2,0},{3,1},{4,6},{5,7},{6,4},{7,5}} | collective-permute-start | bytes 1966088 | tf_op jit(solution)/shard_map/ppermute | solution.py:402
  121.0 60.3 %collective-permute-start.38 = (bf16[4,5,128,128]{3,2,1,0:T(8,128)(2,1)S(1)}, bf16[4,5,128,128]{3,2,1,0:T(8,128)(2,1)}, u32[]{:S(2)}, u32[]{:S(2)}) collective-permute-start(bf16[4,5,128,128]{3,2,1,0:T(8,128)(2,1)S(1)} %copy-done.2), channel_id=1, source_target_pairs={{0,4},{1,5},{2,6},{3,7},{4,0},{5,1},{6,2},{7,3}} | collective-permute-start | bytes 1966088 | tf_op jit(solution)/shard_map/ppermute | solution.py:402
  121.8 62.5 %collective-permute-start.29 = (bf16[4,5,128,128]{3,2,1,0:T(8,128)(2,1)}, bf16[4,5,128,128]{3,2,1,0:T(8,128)(2,1)S(1)}, u32[]{:S(2)}, u32[]{:S(2)}) collective-permute-start(bf16[4,5,128,128]{3,2,1,0:T(8,128)(2,1)} %get-tuple-element.107.refs_0_), channel_id=1, source_target_pairs={{0,2},{1,3},{2,0},{3,1},{4,6},{5,7},{6,4},{7,5}} | collective-permute-start | bytes 1966088 | tf_op jit(solution)/shard_map/ppermute | solution.py:402
  124.2 60.6 %collective-permute-start.32 = (bf16[4,5,128,128]{3,2,1,0:T(8,128)(2,1)}, bf16[4,5,128,128]{3,2,1,0:T(8,128)(2,1)S(1)}, u32[]{:S(2)}, u32[]{:S(2)}) collective-permute-start(bf16[4,5,128,128]{3,2,1,0:T(8,128)(2,1)} %get-tuple-element.108), channel_id=1, source_target_pairs={{0,5},{1,4},{2,7},{3,6},{4,1},{5,0},{6,3},{7,2}} | collective-permute-start | bytes 1966088 | tf_op jit(solution)/shard_map/ppermute | solution.py:402
  135.0 51.3 %collective-permute-start.47 = (bf16[4,5,128,128]{3,2,1,0:T(8,128)(2,1)}, bf16[4,5,128,128]{3,2,1,0:T(8,128)(2,1)}, u32[]{:S(2)}, u32[]{:S(2)}) collective-permute-start(bf16[4,5,128,128]{3,2,1,0:T(8,128)(2,1)} %collective-permute-done.43.refs_2_), channel_id=1, source_target_pairs={{0,4},{1,5},{2,6},{3,7},{4,0},{5,1},{6,2},{7,3}} | collective-permute-start | bytes 1966088 | tf_op jit(solution)/shard_map/ppermute | solution.py:402
  137.9 49.6 %collective-permute-start.48 = (bf16[4,5,128,128]{3,2,1,0:T(8,128)(2,1)}, bf16[4,5,128,128]{3,2,1,0:T(8,128)(2,1)}, u32[]{:S(2)}, u32[]{:S(2)}) collective-permute-start(bf16[4,5,128,128]{3,2,1,0:T(8,128)(2,1)} %copy-done.18), channel_id=1, source_target_pairs={{0,2},{1,3},{2,0},{3,1},{4,6},{5,7},{6,4},{7,5}} | collective-permute-start | bytes 1966088 | tf_op jit(solution)/shard_map/ppermute | solution.py:402
  181.3 104.0 %collective-permute-start.56 = (bf16[4,2,1024,256]{3,2,1,0:T(8,128)(2,1)}, bf16[4,2,1024,256]{3,2,1,0:T(8,128)(2,1)}, u32[]{:S(2)}, u32[]{:S(2)}) collective-permute-start(bf16[4,2,1024,256]{3,2,1,0:T(8,128)(2,1)} %get-tuple-element.123), channel_id=1, source_target_pairs={{0,1},{1,0},{2,3},{3,2},{4,5},{5,4},{6,7},{7,6}} | collective-permute-start | bytes 12582920 | tf_op jit(solution)/shard_map/ppermute | solution.py:402
  184.3 45.0 %collective-permute-start.28 = (bf16[4,5,128,128]{3,2,1,0:T(8,128)(2,1)}, bf16[4,5,128,128]{3,2,1,0:T(8,128)(2,1)}, u32[]{:S(2)}, u32[]{:S(2)}) collective-permute-start(bf16[4,5,128,128]{3,2,1,0:T(8,128)(2,1)} %get-tuple-element.108), channel_id=1, source_target_pairs={{0,1},{1,0},{2,3},{3,2},{4,5},{5,4},{6,7},{7,6}} | collective-permute-start | bytes 1966088 | tf_op jit(solution)/shard_map/ppermute | solution.py:402
  184.7 44.6 %collective-permute-start.30 = (bf16[4,5,128,128]{3,2,1,0:T(8,128)(2,1)}, bf16[4,5,128,128]{3,2,1,0:T(8,128)(2,1)}, u32[]{:S(2)}, u32[]{:S(2)}) collective-permute-start(bf16[4,5,128,128]{3,2,1,0:T(8,128)(2,1)} %get-tuple-element.108), channel_id=1, source_target_pairs={{0,3},{1,2},{2,1},{3,0},{4,7},{5,6},{6,5},{7,4}} | collective-permute-start | bytes 1966088 | tf_op jit(solution)/shard_map/ppermute | solution.py:402
  186.3 44.4 %collective-permute-start.31 = (bf16[4,5,128,128]{3,2,1,0:T(8,128)(2,1)S(1)}, bf16[4,5,128,128]{3,2,1,0:T(8,128)(2,1)}, u32[]{:S(2)}, u32[]{:S(2)}) collective-permute-start(bf16[4,5,128,128]{3,2,1,0:T(8,128)(2,1)S(1)} %copy-done.4), channel_id=1, source_target_pairs={{0,4},{1,5},{2,6},{3,7},{4,0},{5,1},{6,2},{7,3}} | collective-permute-start | bytes 1966088 | tf_op jit(solution)/shard_map/ppermute | solution.py:402
  187.6 43.1 %collective-permute-start.22 = (bf16[4,5,128,128]{3,2,1,0:T(8,128)(2,1)}, bf16[4,5,128,128]{3,2,1,0:T(8,128)(2,1)S(1)}, u32[]{:S(2)}, u32[]{:S(2)}) collective-permute-start(bf16[4,5,128,128]{3,2,1,0:T(8,128)(2,1)} %get-tuple-element.105.refs_0_), channel_id=1, source_target_pairs={{0,2},{1,3},{2,0},{3,1},{4,6},{5,7},{6,4},{7,5}} | collective-permute-start | bytes 1966088 | tf_op jit(solution)/shard_map/ppermute | solution.py:402
  229.3 105.6 %collective-permute-start.59 = (bf16[4,2,1024,256]{3,2,1,0:T(8,128)(2,1)}, bf16[4,2,1024,256]{3,2,1,0:T(8,128)(2,1)}, u32[]{:S(2)}, u32[]{:S(2)}) collective-permute-start(bf16[4,2,1024,256]{3,2,1,0:T(8,128)(2,1)} %get-tuple-element.132), channel_id=1, source_target_pairs={{0,1},{1,0},{2,3},{3,2},{4,5},{5,4},{6,7},{7,6}} | collective-permute-start | bytes 12582920 | tf_op jit(solution)/shard_map/ppermute | solution.py:402
  247.2 30.3 %collective-permute-start.40 = (bf16[4,5,128,128]{3,2,1,0:T(8,128)(2,1)S(1)}, bf16[4,5,128,128]{3,2,1,0:T(8,128)(2,1)S(1)}, u32[]{:S(2)}, u32[]{:S(2)}) collective-permute-start(bf16[4,5,128,128]{3,2,1,0:T(8,128)(2,1)S(1)} %collective-permute-done.36.refs_2_), channel_id=1, source_target_pairs={{0,4},{1,5},{2,6},{3,7},{4,0},{5,1},{6,2},{7,3}} | collective-permute-start | bytes 1966088 | tf_op jit(solution)/shard_map/ppermute | solution.py:402
  248.0 34.1 %collective-permute-start.41 = (bf16[4,5,128,128]{3,2,1,0:T(8,128)(2,1)}, bf16[4,5,128,128]{3,2,1,0:T(8,128)(2,1)}, u32[]{:S(2)}, u32[]{:S(2)}) collective-permute-start(bf16[4,5,128,128]{3,2,1,0:T(8,128)(2,1)} %copy-done.7), channel_id=1, source_target_pairs={{0,2},{1,3},{2,0},{3,1},{4,6},{5,7},{6,4},{7,5}} | collective-permute-start | bytes 1966088 | tf_op jit(solution)/shard_map/ppermute | solution.py:402
  282.1 49.9 %collective-permute-start.33 = (bf16[4,5,128,128]{3,2,1,0:T(8,128)(2,1)S(1)}, bf16[4,5,128,128]{3,2,1,0:T(8,128)(2,1)S(1)}, u32[]{:S(2)}, u32[]{:S(2)}) collective-permute-start(bf16[4,5,128,128]{3,2,1,0:T(8,128)(2,1)S(1)} %collective-permute-done.29.refs_2_), channel_id=1, source_target_pairs={{0,4},{1,5},{2,6},{3,7},{4,0},{5,1},{6,2},{7,3}} | collective-permute-start | bytes 1966088 | tf_op jit(solution)/shard_map/ppermute | solution.py:402
  283.3 49.4 %collective-permute-start.34 = (bf16[4,5,128,128]{3,2,1,0:T(8,128)(2,1)S(1)}, bf16[4,5,128,128]{3,2,1,0:T(8,128)(2,1)}, u32[]{:S(2)}, u32[]{:S(2)}) collective-permute-start(bf16[4,5,128,128]{3,2,1,0:T(8,128)(2,1)S(1)} %copy-done.9), channel_id=1, source_target_pairs={{0,2},{1,3},{2,0},{3,1},{4,6},{5,7},{6,4},{7,5}} | collective-permute-start | bytes 1966088 | tf_op jit(solution)/shard_map/ppermute | solution.py:402
  285.2 48.9 %collective-permute-start.61 = (bf16[128,8,192]{2,1,0:T(8,128)(2,1)}, bf16[128,8,192]{2,1,0:T(8,128)(2,1)}, u32[]{:S(2)}, u32[]{:S(2)}) collective-permute-start(bf16[128,8,192]{2,1,0:T(8,128)(2,1)} %get-tuple-element.134), channel_id=1, source_target_pairs={{0,1},{1,0},{2,3},{3,2},{4,5},{5,4},{6,7},{7,6}} | collective-permute-start | bytes 1179656 | tf_op jit(solution)/shard_map/ppermute | solution.py:402
  285.2 47.6 %collective-permute-start.60 = (bf16[128,8,128]{2,1,0:T(8,128)(2,1)}, bf16[128,8,128]{2,1,0:T(8,128)(2,1)S(1)}, u32[]{:S(2)}, u32[]{:S(2)}) collective-permute-start(bf16[128,8,128]{2,1,0:T(8,128)(2,1)} %get-tuple-element.133), channel_id=1, source_target_pairs={{0,1},{1,0},{2,3},{3,2},{4,5},{5,4},{6,7},{7,6}} | collective-permute-start | bytes 786440 | tf_op jit(solution)/shard_map/ppermute | solution.py:402
  332.1 51.3 %collective-permute-start.15 = (bf16[8,5,128,128]{3,2,1,0:T(8,128)(2,1)}, bf16[8,5,128,128]{3,2,1,0:T(8,128)(2,1)}, u32[]{:S(2)}, u32[]{:S(2)}) collective-permute-start(bf16[8,5,128,128]{3,2,1,0:T(8,128)(2,1)} %get-tuple-element.103.refs_0_), channel_id=1, source_target_pairs={{0,2},{1,3},{2,0},{3,1},{4,6},{5,7},{6,4},{7,5}} | collective-permute-start | bytes 3932168 | tf_op jit(solution)/shard_map/ppermute | solution.py:402
  332.7 85.5 %collective-permute-start.62 = (bf16[4,2,1024,256]{3,2,1,0:T(8,128)(2,1)}, bf16[4,2,1024,256]{3,2,1,0:T(8,128)(2,1)}, u32[]{:S(2)}, u32[]{:S(2)}) collective-permute-start(bf16[4,2,1024,256]{3,2,1,0:T(8,128)(2,1)} %get-tuple-element.141), channel_id=1, source_target_pairs={{0,1},{1,0},{2,3},{3,2},{4,5},{5,4},{6,7},{7,6}} | collective-permute-start | bytes 12582920 | tf_op jit(solution)/shard_map/ppermute | solution.py:402
  332.8 51.2 %collective-permute-start.18 = (bf16[8,5,128,128]{3,2,1,0:T(8,128)(2,1)}, bf16[8,5,128,128]{3,2,1,0:T(8,128)(2,1)}, u32[]{:S(2)}, u32[]{:S(2)}) collective-permute-start(bf16[8,5,128,128]{3,2,1,0:T(8,128)(2,1)} %get-tuple-element.104), channel_id=1, source_target_pairs={{0,5},{1,4},{2,7},{3,6},{4,1},{5,0},{6,3},{7,2}} | collective-permute-start | bytes 3932168 | tf_op jit(solution)/shard_map/ppermute | solution.py:402
  334.1 48.7 %collective-permute-start.26 = (bf16[4,5,128,128]{3,2,1,0:T(8,128)(2,1)S(1)}, bf16[4,5,128,128]{3,2,1,0:T(8,128)(2,1)S(1)}, u32[]{:S(2)}, u32[]{:S(2)}) collective-permute-start(bf16[4,5,128,128]{3,2,1,0:T(8,128)(2,1)S(1)} %collective-permute-done.22.refs_2_), channel_id=1, source_target_pairs={{0,4},{1,5},{2,6},{3,7},{4,0},{5,1},{6,2},{7,3}} | collective-permute-start | bytes 1966088 | tf_op jit(solution)/shard_map/ppermute | solution.py:402
  334.9 48.0 %collective-permute-start.27 = (bf16[4,5,128,128]{3,2,1,0:T(8,128)(2,1)S(1)}, bf16[4,5,128,128]{3,2,1,0:T(8,128)(2,1)S(1)}, u32[]{:S(2)}, u32[]{:S(2)}) collective-permute-start(bf16[4,5,128,128]{3,2,1,0:T(8,128)(2,1)S(1)} %copy-done.13), channel_id=1, source_target_pairs={{0,2},{1,3},{2,0},{3,1},{4,6},{5,7},{6,4},{7,5}} | collective-permute-start | bytes 1966088 | tf_op jit(solution)/shard_map/ppermute | solution.py:402
  382.9 82.4 %collective-permute-start.65 = (bf16[4,2,1024,256]{3,2,1,0:T(8,128)(2,1)}, bf16[4,2,1024,256]{3,2,1,0:T(8,128)(2,1)}, u32[]{:S(2)}, u32[]{:S(2)}) collective-permute-start(bf16[4,2,1024,256]{3,2,1,0:T(8,128)(2,1)} %get-tuple-element.150), channel_id=1, source_target_pairs={{0,1},{1,0},{2,3},{3,2},{4,5},{5,4},{6,7},{7,6}} | collective-permute-start | bytes 12582920 | tf_op jit(solution)/shard_map/ppermute | solution.py:402
  383.4 31.1 %collective-permute-start.16 = (bf16[8,5,128,128]{3,2,1,0:T(8,128)(2,1)}, bf16[8,5,128,128]{3,2,1,0:T(8,128)(2,1)S(1)}, u32[]{:S(2)}, u32[]{:S(2)}) collective-permute-start(bf16[8,5,128,128]{3,2,1,0:T(8,128)(2,1)} %get-tuple-element.104), channel_id=1, source_target_pairs={{0,3},{1,2},{2,1},{3,0},{4,7},{5,6},{6,5},{7,4}} | collective-permute-start | bytes 3932168 | tf_op jit(solution)/shard_map/ppermute | solution.py:402
  384.0 31.4 %collective-permute-start.17 = (bf16[8,5,128,128]{3,2,1,0:T(8,128)(2,1)}, bf16[8,5,128,128]{3,2,1,0:T(8,128)(2,1)S(1)}, u32[]{:S(2)}, u32[]{:S(2)}) collective-permute-start(bf16[8,5,128,128]{3,2,1,0:T(8,128)(2,1)} %get-tuple-element.103.refs_0_), channel_id=1, source_target_pairs={{0,4},{1,5},{2,6},{3,7},{4,0},{5,1},{6,2},{7,3}} | collective-permute-start | bytes 3932168 | tf_op jit(solution)/shard_map/ppermute | solution.py:402
  392.2 26.0 %collective-permute-start.64 = (bf16[128,8,192]{2,1,0:T(8,128)(2,1)}, bf16[128,8,192]{2,1,0:T(8,128)(2,1)S(1)}, u32[]{:S(2)}, u32[]{:S(2)}) collective-permute-start(bf16[128,8,192]{2,1,0:T(8,128)(2,1)} %get-tuple-element.143), channel_id=1, source_target_pairs={{0,1},{1,0},{2,3},{3,2},{4,5},{5,4},{6,7},{7,6}} | collective-permute-start | bytes 1179656 | tf_op jit(solution)/shard_map/ppermute | solution.py:402
  415.4 49.9 %collective-permute-start.19 = (bf16[8,5,128,128]{3,2,1,0:T(8,128)(2,1)}, bf16[8,5,128,128]{3,2,1,0:T(8,128)(2,1)}, u32[]{:S(2)}, u32[]{:S(2)}) collective-permute-start(bf16[8,5,128,128]{3,2,1,0:T(8,128)(2,1)} %collective-permute-done.15.refs_2_), channel_id=1, source_target_pairs={{0,4},{1,5},{2,6},{3,7},{4,0},{5,1},{6,2},{7,3}} | collective-permute-start | bytes 3932168 | tf_op jit(solution)/shard_map/ppermute | solution.py:402
  417.0 48.3 %collective-permute-start.20 = (bf16[8,5,128,128]{3,2,1,0:T(8,128)(2,1)}, bf16[8,5,128,128]{3,2,1,0:T(8,128)(2,1)}, u32[]{:S(2)}, u32[]{:S(2)}) collective-permute-start(bf16[8,5,128,128]{3,2,1,0:T(8,128)(2,1)} %collective-permute-done.18.refs_5_), channel_id=1, source_target_pairs={{0,2},{1,3},{2,0},{3,1},{4,6},{5,7},{6,4},{7,5}} | collective-permute-start | bytes 3932168 | tf_op jit(solution)/shard_map/ppermute | solution.py:402
  418.2 47.2 %collective-permute-start.67 = (bf16[128,8,192]{2,1,0:T(8,128)(2,1)}, bf16[128,8,192]{2,1,0:T(8,128)(2,1)S(1)}, u32[]{:S(2)}, u32[]{:S(2)}) collective-permute-start(bf16[128,8,192]{2,1,0:T(8,128)(2,1)} %get-tuple-element.152), channel_id=1, source_target_pairs={{0,1},{1,0},{2,3},{3,2},{4,5},{5,4},{6,7},{7,6}} | collective-permute-start | bytes 1179656 | tf_op jit(solution)/shard_map/ppermute | solution.py:402
  418.2 47.1 %collective-permute-start.66 = (bf16[128,8,128]{2,1,0:T(8,128)(2,1)}, bf16[128,8,128]{2,1,0:T(8,128)(2,1)}, u32[]{:S(2)}, u32[]{:S(2)}) collective-permute-start(bf16[128,8,128]{2,1,0:T(8,128)(2,1)} %get-tuple-element.151), channel_id=1, source_target_pairs={{0,1},{1,0},{2,3},{3,2},{4,5},{5,4},{6,7},{7,6}} | collective-permute-start | bytes 786440 | tf_op jit(solution)/shard_map/ppermute | solution.py:402
  465.3 137.3 %collective-permute-start.68 = (bf16[4,2,1024,256]{3,2,1,0:T(8,128)(2,1)}, bf16[4,2,1024,256]{3,2,1,0:T(8,128)(2,1)}, u32[]{:S(2)}, u32[]{:S(2)}) collective-permute-start(bf16[4,2,1024,256]{3,2,1,0:T(8,128)(2,1)} %get-tuple-element.159), channel_id=1, source_target_pairs={{0,1},{1,0},{2,3},{3,2},{4,5},{5,4},{6,7},{7,6}} | collective-permute-start | bytes 12582920 | tf_op jit(solution)/shard_map/ppermute | solution.py:402
  547.5 115.5 %collective-permute-start.74 = (bf16[8,2,1024,256]{3,2,1,0:T(8,128)(2,1)}, bf16[8,2,1024,256]{3,2,1,0:T(8,128)(2,1)}, u32[]{:S(2)}, u32[]{:S(2)}) collective-permute-start(bf16[8,2,1024,256]{3,2,1,0:T(8,128)(2,1)} %get-tuple-element.169), channel_id=1, source_target_pairs={{0,1},{1,0},{2,3},{3,2},{4,5},{5,4},{6,7},{7,6}} | collective-permute-start | bytes 25165832 | tf_op jit(solution)/shard_map/ppermute | solution.py:402
  553.9 30.0 %collective-permute-start.10 = (bf16[4,5,128,128]{3,2,1,0:T(8,128)(2,1)}, bf16[4,5,128,128]{3,2,1,0:T(8,128)(2,1)S(1)}, u32[]{:S(2)}, u32[]{:S(2)}) collective-permute-start(bf16[4,5,128,128]{3,2,1,0:T(8,128)(2,1)} %get-tuple-element.99.refs_0_), channel_id=1, source_target_pairs={{0,4},{1,5},{2,6},{3,7},{4,0},{5,1},{6,2},{7,3}} | collective-permute-start | bytes 1966088 | tf_op jit(solution)/shard_map/ppermute | solution.py:402
  649.8 27.1 %collective-permute-start.71 = (bf16[4,2,1024,256]{3,2,1,0:T(8,128)(2,1)}, bf16[4,2,1024,256]{3,2,1,0:T(8,128)(2,1)}, u32[]{:S(2)}, u32[]{:S(2)}) collective-permute-start(bf16[4,2,1024,256]{3,2,1,0:T(8,128)(2,1)} %get-tuple-element.166), channel_id=1, source_target_pairs={{0,1},{1,0},{2,3},{3,2},{4,5},{5,4},{6,7},{7,6}} | collective-permute-start | bytes 12582920 | tf_op jit(solution)/shard_map/ppermute | solution.py:402
  (88 other events, 1556.4 us)
